TPU v7x, 32 devices: a whole 2x2x4 slice. The times are simulated.
32 devices in a mesh: shard: 4 (over z), context: 2 (over x), tensor: 4 (over y, core).
Axes of the slice: x: 2, y: 2, z: 4, core: 2. Of those that a mesh axis runs over, the one named last changes fastest.
Arguments:
- x_in: bfloat16 [1024, 4, 1152], P(('context', 'tensor'), 'shard'), may hold values from -6 to 6
- cond: float32 [4, 1152], replicated, may hold values from -6 to 6
- w_ada: bfloat16 [2, 1152, 6, 1152], P(None, None, None, 'shard'), may hold values from -0.1875 to 0.1875
- b_ada: bfloat16 [2, 6, 1152], P(None, None, 'shard'), may hold values from -3 to 3
- w_qkv: bfloat16 [2, 3, 1152, 1152], P(None, None, 'shard', 'tensor'), may hold values from -0.1875 to 0.1875
- b_qv: bfloat16 [2, 2, 1152], P(None, None, 'tensor'), may hold values from -3 to 3
- w_proj: bfloat16 [2, 1152, 1152], P(None, 'tensor', 'shard'), may hold values from -1.5 to 1.5
- b_proj: bfloat16 [2, 1152], replicated, may hold values from -2 to 2
- up_weight: bfloat16 [2, 1152, 4608], P(None, 'shard', 'tensor'), may hold values from -0.1875 to 0.1875
- up_bias_vector: bfloat16 [2, 4608], P(None, 'tensor'), may hold values from -3 to 3
- down_weight: bfloat16 [2, 4608, 1152], P(None, 'tensor', 'shard'), may hold values from -0.09375 to 0.09375
- down_bias_vector: bfloat16 [2, 1152], replicated, may hold values from -2 to 2
- cotangent: bfloat16 [1024, 4, 1152], P(('context', 'tensor'), 'shard'), may hold values from -6 to 6
Outputs:
- output: bfloat16 [1024, 4, 1152], P(('context', 'tensor'), 'shard')
- grad_input: float32 [1024, 4, 1152], P(('context', 'tensor'), 'shard')
- grad_cond: float32 [4, 1152], replicated
- grad_w_ada: float32 [2, 1152, 6, 1152], P(None, None, None, 'shard')
- grad_b_ada: float32 [2, 6, 1152], P(None, None, 'shard')
- grad_w_qkv: float32 [2, 3, 1152, 1152], P(None, None, 'shard', 'tensor')
- grad_b_qv: float32 [2, 2, 1152], P(None, None, 'tensor')
- grad_w_proj: float32 [2, 1152, 1152], P(None, 'tensor', 'shard')
- grad_b_proj: float32 [2, 1152], replicated
- grad_w_up: float32 [2, 1152, 4608], P(None, 'shard', 'tensor')
- grad_b_up: float32 [2, 4608], P(None, 'tensor')
- grad_w_down: float32 [2, 4608, 1152], P(None, 'tensor', 'shard')
- grad_b_down: float32 [2, 1152], replicated
All inputs are finite; a program needn't handle non-finite values.
Results may differ from a plain program's by a relative error of at most 0.024.
The roundings to bfloat16 on the way count: a program that leaves them out, or rounds other values in their place, can miss the bound.
Values may be sent and summed in bfloat16 or wider, within the bound.
A program may use at most 192 MiB of HBM per device.

v0:
```python
import jax
import jax.numpy as jnp
from jax import lax
from jax.sharding import PartitionSpec as P

D = 1152
HD = 72
FF = 4608
LAYERS = 2


epsilon = 1e-06


def normalize(values):
    center = values - jnp.mean(values, axis=-1, keepdims=True)
    inverse = lax.rsqrt(jnp.mean(center * center, axis=-1, keepdims=True) + epsilon)
    return (center * inverse, inverse)


def normalize_back(grad_normed, normed, inverse):
    mean_grad = jnp.mean(grad_normed, axis=-1, keepdims=True)
    mean_proj = jnp.mean(grad_normed * normed, axis=-1, keepdims=True)
    return inverse * (grad_normed - mean_grad - normed * mean_proj)


def gelu_tanh(values):
    return jax.nn.gelu(values, approximate=True)


def to_heads(tokens):
    return tokens.reshape(tokens.shape[0], tokens.shape[1], -1, HD).transpose(1, 2, 0, 3)


def from_heads(blocks):
    return blocks.transpose(2, 0, 1, 3).reshape(blocks.shape[2], blocks.shape[0], -1)


def over_heads(head_fn, arrays):
    return lax.map(lambda seq_items: lax.map(head_fn, seq_items), arrays)


def score_block(query_head, key_head):
    return jnp.einsum(
        "qe,ke->qk", query_head, key_head, preferred_element_type=jnp.float32
    ) * HD ** (-0.5)


def forward_head(head_parts):
    query_head, key_head, value_head = head_parts
    scores = score_block(query_head, key_head)
    maxima = jnp.max(scores, axis=-1, keepdims=True)
    exp_scores = jnp.exp(scores - maxima)
    row_total = jnp.sum(exp_scores, axis=-1, keepdims=True)
    prob_low = (exp_scores / row_total).astype(jnp.bfloat16)
    result = jnp.dot(prob_low, value_head, preferred_element_type=jnp.float32).astype(jnp.bfloat16)
    return (result, (maxima + jnp.log(row_total))[:, 0])


def full_grads(head_parts):
    query_head, key_head, value_head, grad_head, log_head = head_parts
    prob_full = jnp.exp(score_block(query_head, key_head) - log_head[:, None])
    grad_prob = jnp.einsum("qe,ke->qk", grad_head, value_head, preferred_element_type=jnp.float32)
    row_delta = jnp.sum(prob_full * grad_prob, axis=-1, keepdims=True)
    grad_score = (prob_full * (grad_prob - row_delta)).astype(jnp.bfloat16)
    grad_query = jnp.dot(grad_score, key_head, preferred_element_type=jnp.float32) * HD ** (-0.5)
    grad_key = jnp.einsum(
        "qk,qe->ke", grad_score, query_head, preferred_element_type=jnp.float32
    ) * HD ** (-0.5)
    grad_value = jnp.einsum(
        "qk,qe->ke", prob_full.astype(jnp.bfloat16), grad_head, preferred_element_type=jnp.float32
    )
    return (grad_query, grad_key, grad_value)


def fetch_weights(qkv_part, proj_part, up_part, down_part, mod_part):
    return (
        lax.all_gather(qkv_part, "shard", axis=2, tiled=True),
        lax.all_gather(proj_part, "shard", axis=2, tiled=True),
        lax.all_gather(up_part, "shard", axis=1, tiled=True),
        lax.all_gather(down_part, "shard", axis=2, tiled=True),
        lax.all_gather(mod_part, "shard", axis=3, tiled=True),
    )


def layer_forward(hidden_state, weights, modulation, biases):
    full_qkv, full_proj, full_up, full_down, mod_unused = weights
    bias_qv, bias_proj, bias_up, bias_down = biases
    normed1, inverse1 = normalize(hidden_state)
    mix_in = (normed1 * (1.0 + modulation[:, 1]) + modulation[:, 0]).astype(jnp.bfloat16)
    mixed_all = lax.all_gather(mix_in, "tensor", axis=0, tiled=True)
    projected = jnp.einsum("tbd,kde->tbke", mixed_all, full_qkv, preferred_element_type=jnp.float32)
    queries = (projected[:, :, 0] + bias_qv[0]).astype(jnp.bfloat16)
    keys_own = projected[:, :, 1].astype(jnp.bfloat16)
    values_own = (projected[:, :, 2] + bias_qv[1]).astype(jnp.bfloat16)
    keys_all, values_all = (
        lax.all_gather(keys_own, "context", axis=0, tiled=True),
        lax.all_gather(values_own, "context", axis=0, tiled=True),
    )
    head_out, log_sums = over_heads(
        forward_head, (to_heads(queries), to_heads(keys_all), to_heads(values_all))
    )
    attended = from_heads(head_out)
    row_block = attended
    branch = (
        lax.psum_scatter(
            jnp.einsum("tbe,ed->tbd", row_block, full_proj, preferred_element_type=jnp.float32),
            "tensor",
            scatter_dimension=0,
            tiled=True,
        )
        + bias_proj
    )
    after_attn = hidden_state + modulation[:, 2] * branch
    normed2, inverse2 = normalize(after_attn)
    feedforward_input = (normed2 * (1.0 + modulation[:, 4]) + modulation[:, 3]).astype(jnp.bfloat16)
    ff_all = lax.all_gather(feedforward_input, "tensor", axis=0, tiled=True)
    preactivation_value = (
        jnp.einsum("tbd,df->tbf", ff_all, full_up, preferred_element_type=jnp.float32) + bias_up
    )
    activation_value = gelu_tanh(preactivation_value).astype(jnp.bfloat16)
    row_block = activation_value
    feedforward_output = (
        lax.psum_scatter(
            jnp.einsum(
                "tbf,fd->tbd", row_block, full_down, preferred_element_type=jnp.float32
            ).astype(jnp.bfloat16),
            "tensor",
            scatter_dimension=0,
            tiled=True,
        ).astype(jnp.float32)
        + bias_down
    )
    result = after_attn + modulation[:, 5] * feedforward_output
    stash = (
        normed1,
        inverse1,
        mixed_all,
        queries,
        keys_all,
        values_all,
        attended,
        log_sums,
        branch,
        normed2,
        inverse2,
        ff_all,
        preactivation_value,
        activation_value,
        feedforward_output,
    )
    return (result, stash)


def layer_backward(grad_hidden, weights, modulation, stash):
    full_qkv, full_proj, full_up, full_down, mod_unused = weights
    (
        normed1,
        inverse1,
        mixed_all,
        queries,
        keys_all,
        values_all,
        attended,
        log_sums,
        branch,
        normed2,
        inverse2,
        ff_all,
        preactivation_value,
        activation_value,
        feedforward_output,
    ) = stash
    grad_ff = (modulation[:, 5] * grad_hidden).astype(jnp.bfloat16)
    grad_gate2 = jnp.sum(grad_hidden * feedforward_output, axis=0)
    bias_down = jnp.sum(grad_ff.astype(jnp.float32), axis=(0, 1))
    grad_ff_all = lax.all_gather(grad_ff, "tensor", axis=0, tiled=True)
    grad_w_down = jnp.einsum(
        "tbf,tbd->fd", activation_value, grad_ff_all, preferred_element_type=jnp.float32
    )
    grad_activ = jnp.einsum(
        "tbd,fd->tbf", grad_ff_all, full_down, preferred_element_type=jnp.float32
    )
    gelu_value, gelu_back = jax.vjp(gelu_tanh, preactivation_value)
    grad_pre = gelu_back(grad_activ)[0].astype(jnp.bfloat16)
    bias_up = jnp.sum(grad_pre.astype(jnp.float32), axis=(0, 1))
    grad_w_up = jnp.einsum("tbd,tbf->df", ff_all, grad_pre, preferred_element_type=jnp.float32)
    row_block = grad_pre
    grad_ffin = lax.psum_scatter(
        jnp.einsum("tbf,df->tbd", row_block, full_up, preferred_element_type=jnp.float32).astype(
            jnp.bfloat16
        ),
        "tensor",
        scatter_dimension=0,
        tiled=True,
    ).astype(jnp.float32)
    grad_shift2 = jnp.sum(grad_ffin, axis=0)
    grad_scale2 = jnp.sum(grad_ffin * normed2, axis=0)
    grad_after = grad_hidden + normalize_back(
        grad_ffin * (1.0 + modulation[:, 4]), normed2, inverse2
    )
    grad_branch = (modulation[:, 2] * grad_after).astype(jnp.bfloat16)
    grad_gate1 = jnp.sum(grad_after * branch, axis=0)
    bias_proj = jnp.sum(grad_branch.astype(jnp.float32), axis=(0, 1))
    grad_branch_all = lax.all_gather(grad_branch, "tensor", axis=0, tiled=True)
    grad_w_proj = jnp.einsum(
        "tbe,tbd->ed", attended, grad_branch_all, preferred_element_type=jnp.float32
    )
    grad_attended = jnp.einsum(
        "tbd,ed->tbe", grad_branch_all, full_proj, preferred_element_type=jnp.float32
    ).astype(jnp.bfloat16)
    head_inputs = (
        to_heads(queries),
        to_heads(keys_all),
        to_heads(values_all),
        to_heads(grad_attended),
        log_sums,
    )
    grad_q_heads, grad_k_heads, grad_v_heads = over_heads(full_grads, head_inputs)
    grad_queries = from_heads(grad_q_heads).astype(jnp.bfloat16)
    grad_keys, grad_values = (
        lax.psum_scatter(
            from_heads(grad_k_heads).astype(jnp.bfloat16),
            "context",
            scatter_dimension=0,
            tiled=True,
        ).astype(jnp.float32),
        lax.psum_scatter(
            from_heads(grad_v_heads).astype(jnp.bfloat16),
            "context",
            scatter_dimension=0,
            tiled=True,
        ).astype(jnp.float32),
    )
    grad_keys = grad_keys.astype(jnp.bfloat16)
    grad_values = grad_values.astype(jnp.bfloat16)
    grad_qkv = jnp.stack((grad_queries, grad_keys, grad_values), axis=2)
    bias_qv = jnp.stack(
        (
            jnp.sum(grad_queries.astype(jnp.float32), axis=(0, 1)),
            jnp.sum(grad_values.astype(jnp.float32), axis=(0, 1)),
        )
    )
    grad_w_qkv = jnp.einsum(
        "tbd,tbke->kde", mixed_all, grad_qkv, preferred_element_type=jnp.float32
    )
    row_block = grad_qkv
    grad_mixin = lax.psum_scatter(
        jnp.einsum("tbke,kde->tbd", row_block, full_qkv, preferred_element_type=jnp.float32).astype(
            jnp.bfloat16
        ),
        "tensor",
        scatter_dimension=0,
        tiled=True,
    ).astype(jnp.float32)
    grad_shift1 = jnp.sum(grad_mixin, axis=0)
    grad_scale1 = jnp.sum(grad_mixin * normed1, axis=0)
    grad_input = grad_after + normalize_back(
        grad_mixin * (1.0 + modulation[:, 1]), normed1, inverse1
    )
    grad_mod_own = jnp.stack(
        (grad_shift1, grad_scale1, grad_gate1, grad_shift2, grad_scale2, grad_gate2), axis=1
    )
    return (
        grad_input,
        (grad_w_qkv, grad_w_proj, grad_w_up, grad_w_down),
        (grad_mod_own, bias_qv, bias_proj, bias_up, bias_down),
    )


def body(
    x_in,
    cond,
    w_ada,
    b_ada,
    w_qkv,
    b_qv,
    w_proj,
    b_proj,
    up_weight,
    up_bias_vector,
    down_weight,
    down_bias_vector,
    cotangent,
):
    shard_index = lax.axis_index("shard")
    tensor_index = lax.axis_index("tensor")
    context_index = lax.axis_index("context")
    own_latents = x_in.shape[1]
    all_latents = cond.shape[0]
    shard_cols = w_ada.shape[3]
    head_cols = w_qkv.shape[3]
    hidden_cols = up_weight.shape[2]
    condition_reduced = jax.nn.silu(cond).astype(jnp.bfloat16)
    mod_terms = (
        jnp.einsum("sd,ldkc->lskc", condition_reduced, w_ada, preferred_element_type=jnp.float32)
        + b_ada.astype(jnp.float32)[:, None]
    ).astype(jnp.bfloat16)
    hidden_state = x_in.astype(jnp.float32)
    layer_state = []
    for layer_number_index in range(LAYERS):
        sliced = fetch_weights(
            w_qkv[layer_number_index : layer_number_index + 1],
            w_proj[layer_number_index : layer_number_index + 1],
            up_weight[layer_number_index : layer_number_index + 1],
            down_weight[layer_number_index : layer_number_index + 1],
            mod_terms[layer_number_index : layer_number_index + 1],
        )
        weights = tuple((member_entry[0] for member_entry in sliced))
        modulation = lax.dynamic_slice_in_dim(
            weights[4], shard_index * own_latents, own_latents, 0
        ).astype(jnp.float32)
        biases = (
            b_qv[layer_number_index].astype(jnp.float32),
            b_proj[layer_number_index].astype(jnp.float32),
            up_bias_vector[layer_number_index].astype(jnp.float32),
            down_bias_vector[layer_number_index].astype(jnp.float32),
        )
        hidden_state, stash = layer_forward(hidden_state, weights, modulation, biases)
        layer_state.append((weights, modulation, stash))
    output = hidden_state.astype(jnp.bfloat16)
    grad_hidden = cotangent.astype(jnp.float32)
    cond_total = jnp.zeros(cond.shape, jnp.float32)
    results = [None] * LAYERS
    context_mask = (context_index == 0).astype(jnp.float32)
    for layer_number_index in reversed(range(LAYERS)):
        weights, modulation, stash = layer_state[layer_number_index]
        grad_hidden, matrix_grads, small_terms = layer_backward(
            grad_hidden, weights, modulation, stash
        )
        grad_mod_own, bias_qv, bias_proj, bias_up, bias_down = small_terms
        grad_mod_pad = lax.dynamic_update_slice_in_dim(
            jnp.zeros((all_latents, 6, D), jnp.float32), grad_mod_own, shard_index * own_latents, 0
        )
        bias_qv_pad = lax.dynamic_update_slice_in_dim(
            jnp.zeros((2, D), jnp.float32), bias_qv, tensor_index * head_cols, 1
        )
        bias_up_pad = lax.dynamic_update_slice_in_dim(
            jnp.zeros((FF,), jnp.float32), bias_up, tensor_index * hidden_cols, 0
        )
        mod_sum, proj_sum, down_sum, qv_sum, up_sum = lax.psum(
            (grad_mod_pad, bias_proj, bias_down, bias_qv_pad, bias_up_pad),
            ("shard", "context", "tensor"),
        )
        mod_cols = lax.dynamic_slice_in_dim(
            mod_sum.astype(jnp.bfloat16), shard_index * shard_cols, shard_cols, 2
        )
        grad_w_ada = jnp.einsum(
            "sd,skc->dkc", condition_reduced, mod_cols, preferred_element_type=jnp.float32
        )
        grad_b_ada = jnp.sum(mod_cols.astype(jnp.float32), axis=0)
        cond_part = (
            jnp.einsum(
                "skc,dkc->sd",
                mod_cols,
                w_ada[layer_number_index],
                preferred_element_type=jnp.float32,
            )
            * context_mask
        )
        grad_w_qkv, grad_w_proj, grad_w_up, grad_w_down = matrix_grads
        qkv_all, proj_all, up_all, down_all, cond_sum = (
            lax.psum(grad_w_qkv.astype(jnp.bfloat16), ("shard", "context")).astype(jnp.float32),
            lax.psum(grad_w_proj.astype(jnp.bfloat16), ("shard", "context")).astype(jnp.float32),
            lax.psum(grad_w_up.astype(jnp.bfloat16), ("shard", "context")).astype(jnp.float32),
            lax.psum(grad_w_down.astype(jnp.bfloat16), ("shard", "context")).astype(jnp.float32),
            lax.psum(cond_part.astype(jnp.bfloat16), ("shard", "context")).astype(jnp.float32),
        )
        qkv_own = lax.dynamic_slice_in_dim(qkv_all, shard_index * shard_cols, shard_cols, 1)
        proj_own = lax.dynamic_slice_in_dim(proj_all, shard_index * shard_cols, shard_cols, 1)
        up_own = lax.dynamic_slice_in_dim(up_all, shard_index * shard_cols, shard_cols, 0)
        down_own = lax.dynamic_slice_in_dim(down_all, shard_index * shard_cols, shard_cols, 1)
        cond_total = cond_total + cond_sum
        results[layer_number_index] = (
            grad_w_ada,
            grad_b_ada,
            qkv_own,
            lax.dynamic_slice_in_dim(qv_sum, tensor_index * head_cols, head_cols, 1),
            proj_own,
            proj_sum,
            up_own,
            lax.dynamic_slice_in_dim(up_sum, tensor_index * hidden_cols, hidden_cols, 0),
            down_own,
            down_sum,
        )
    silu_value, silu_back = jax.vjp(jax.nn.silu, cond)
    grad_cond = silu_back(cond_total)[0]
    stacked = tuple(
        (
            jnp.stack(
                [results[layer_number_index][member_entry] for layer_number_index in range(LAYERS)]
            )
            for member_entry in range(10)
        )
    )
    return (
        output,
        grad_hidden,
        grad_cond,
        stacked[0],
        stacked[1],
        stacked[2],
        stacked[3],
        stacked[4],
        stacked[5],
        stacked[6],
        stacked[7],
        stacked[8],
        stacked[9],
    )


def solution(mesh):
    return jax.shard_map(
        body,
        mesh=mesh,
        in_specs=(
            P(("context", "tensor"), "shard", None),
            P(),
            P(None, None, None, "shard"),
            P(None, None, "shard"),
            P(None, None, "shard", "tensor"),
            P(None, None, "tensor"),
            P(None, "tensor", "shard"),
            P(),
            P(None, "shard", "tensor"),
            P(None, "tensor"),
            P(None, "tensor", "shard"),
            P(),
            P(("context", "tensor"), "shard", None),
        ),
        out_specs=(
            P(("context", "tensor"), "shard", None),
            P(("context", "tensor"), "shard", None),
            P(),
            P(None, None, None, "shard"),
            P(None, None, "shard"),
            P(None, None, "shard", "tensor"),
            P(None, None, "tensor"),
            P(None, "tensor", "shard"),
            P(),
            P(None, "shard", "tensor"),
            P(None, "tensor"),
            P(None, "tensor", "shard"),
            P(),
        ),
        check_vma=False,
    )
```

profile of v0, /device:TPU:0, one launch (start us, length us, event | category | flops | bytes accessed | tf_op | source)
XLA Modules:
  0.0 1609.9 jit_solution(5189787261982974945)
XLA Ops:
  11.0 5.8 fusion.169
  17.4 44.3 %all_gather.66 = bf16[1,4,6,1152]{2,1,0,3:T(4,128)(2,1)S(1)} all-gather(bf16[1,4,6,288]{2,1,0,3:T(4,128)(2,1)S(1)} %copy.78), channel_id=1, replica_groups=mesh['shard'=4,'context'=2,'tensor'=4] {'shard'}, dimensions={3}, use_global_device_ids=true | all-gather | bytes 69120 | tf_op jit(solution)/shard_map/all_gather | solution.py:82
  61.6 43.1 %all_gather.75 = bf16[1,4,6,1152]{2,1,0,3:T(4,128)(2,1)S(1)} all-gather(bf16[1,4,6,288]{2,1,0,3:T(4,128)(2,1)S(1)} %copy.86), channel_id=1, replica_groups=mesh['shard'=4,'context'=2,'tensor'=4] {'shard'}, dimensions={3}, use_global_device_ids=true | all-gather | bytes 69120 | tf_op jit(solution)/shard_map/all_gather | solution.py:82
  111.5 35.5 %all_gather.71 = bf16[1,288,1152]{1,0,2:T(2,128)(2,1)} all-gather(bf16[1,288,288]{1,0,2:T(2,128)(2,1)S(1)} %copy.103), channel_id=1, replica_groups=mesh['shard'=4,'context'=2,'tensor'=4] {'shard'}, dimensions={2}, use_global_device_ids=true | all-gather | bytes 829440 | tf_op jit(solution)/shard_map/all_gather | solution.py:79
  151.7 7.0 copy.80
  162.2 8.0 all_gather.70
  170.2 7.4 all-gather
  182.4 7.4 while.92
  197.0 31.3 %reduce-scatter.13.cloned.1.call-done = f32[128,1,1152]{2,0,1:T(8,128)} async-done(((f32[512,1,1152]{2,0,1:T(8,128)}), f32[128,1,1152]{2,0,1:T(8,128)}) %reduce-scatter.13.cloned.1.call-update) | async-done | bytes 589840 | tf_op jit(solution)/shard_map/reduce_scatter | solution.py:106
  232.9 52.8 %all-gather.23.cloned.1.call-done = bf16[1,1152,1152]{2,1,0:T(8,128)(2,1)} async-done(((bf16[1,288,1152]{2,1,0:T(8,128)(2,1)}), bf16[1,1152,1152]{2,1,0:T(8,128)(2,1)}) %all-gather.23.cloned.1.call-update) | async-done | bytes 2654224 | tf_op jit(solution)/shard_map/all_gather | solution.py:80
  285.6 18.2 %all-gather.21.cloned.1.call-done = bf16[512,1,1152]{2,0,1:T(8,128)(2,1)} async-done(((bf16[128,1,1152]{2,0,1:T(8,128)(2,1)}), bf16[512,1,1152]{2,0,1:T(8,128)(2,1)}) %all-gather.21.cloned.1.call-update) | async-done | bytes 1179664 | tf_op jit(solution)/shard_map/all_gather | solution.py:117
  309.2 52.0 %all-gather.25.cloned.1.call-done = bf16[1,1152,1152]{1,2,0:T(8,128)(2,1)} async-done(((bf16[1,1152,288]{1,2,0:T(8,128)(2,1)}), bf16[1,1152,1152]{1,2,0:T(8,128)(2,1)}) %all-gather.25.cloned.1.call-update) | async-done | bytes 2654224 | tf_op jit(solution)/shard_map/all_gather | solution.py:81
  361.2 5.7 fusion.90
  370.8 20.6 %reduce-scatter.15.cloned.1.call-done = bf16[128,1,1152]{2,0,1:T(8,128)(2,1)} async-done(((bf16[512,1,1152]{2,0,1:T(8,128)(2,1)}), bf16[128,1,1152]{2,0,1:T(8,128)(2,1)}) %reduce-scatter.15.cloned.1.call-update) | async-done | bytes 294928 | tf_op jit(solution)/shard_map/reduce_scatter | solution.py:124
  395.3 59.0 %all_gather.80 = bf16[1,288,1152]{1,0,2:T(2,128)(2,1)} all-gather(bf16[1,288,288]{1,0,2:T(2,128)(2,1)S(1)} %copy.106), channel_id=1, replica_groups=mesh['shard'=4,'context'=2,'tensor'=4] {'shard'}, dimensions={2}, use_global_device_ids=true | all-gather | bytes 829440 | tf_op jit(solution)/shard_map/all_gather | solution.py:79
  459.0 26.9 %all-gather.29.cloned.1.call-done = bf16[1,3,1152,288]{3,1,0,2:T(4,128)(2,1)} async-done(((bf16[1,3,288,288]{3,1,0,2:T(4,128)(2,1)}), bf16[1,3,1152,288]{3,1,0,2:T(4,128)(2,1)}) %all-gather.29.cloned.1.call-update) | async-done | bytes 1990672 | tf_op jit(solution)/shard_map/all_gather | solution.py:78
  485.9 7.0 copy.89
  493.0 10.8 all-gather.27.cloned.1.call-done
  508.0 9.9 all_gather.79
  518.0 9.0 all-gather.1
  536.0 17.2 %while.93 = (s32[]{:T(128)}, bf16[4,512,72]{1,2,0:T(8,128)(2,1)}, f32[4,512]{1,0:T(4,128)S(1)}, bf16[4,512,72]{2,1,0:T(8,128)(2,1)}, bf16[4,1024,72]{2,1,0:T(8,1...) while((s32[]{:T(128)}, bf16[4,512,72]{1,2,0:T(8,128)(2,1)}, ...), condition=%wide.region_15.16_spmd, body=%wide.region_12.15_spmd.sunk | while | flops 155749888 | bytes 7043169 | solution.py:40
  557.9 31.8 %reduce-scatter.17.cloned.1.call-done = f32[128,1,1152]{2,0,1:T(8,128)} async-done(((f32[512,1,1152]{2,0,1:T(8,128)}), f32[128,1,1152]{2,0,1:T(8,128)}) %reduce-scatter.17.cloned.1.call-update) | async-done | bytes 589840 | tf_op jit(solution)/shard_map/reduce_scatter | solution.py:106
  595.1 51.5 %all-gather.33.cloned.1.call-done = bf16[1,1152,1152]{2,1,0:T(8,128)(2,1)} async-done(((bf16[1,288,1152]{2,1,0:T(8,128)(2,1)}), bf16[1,1152,1152]{2,1,0:T(8,128)(2,1)}) %all-gather.33.cloned.1.call-update) | async-done | bytes 2654224 | tf_op jit(solution)/shard_map/all_gather | solution.py:80
  646.6 18.2 %all-gather.31.cloned.1.call-done = bf16[512,1,1152]{2,0,1:T(8,128)(2,1)} async-done(((bf16[128,1,1152]{2,0,1:T(8,128)(2,1)}), bf16[512,1,1152]{2,0,1:T(8,128)(2,1)}) %all-gather.31.cloned.1.call-update) | async-done | bytes 1179664 | tf_op jit(solution)/shard_map/all_gather | solution.py:117
  664.8 5.4 convolution_add_fusion
  670.2 14.2 all-gather.37.cloned.1.call-done
  684.4 56.7 %all-gather.35.cloned.1.call-done = bf16[1,1152,1152]{1,2,0:T(8,128)(2,1)} async-done(((bf16[1,1152,288]{1,2,0:T(8,128)(2,1)}), bf16[1,1152,1152]{1,2,0:T(8,128)(2,1)}) %all-gather.35.cloned.1.call-update) | async-done | bytes 2654224 | tf_op jit(solution)/shard_map/all_gather | solution.py:81
  741.1 6.2 convert_reduce_fusion
  751.4 5.7 fusion.91
  757.2 18.7 %reduce-scatter.21.cloned.1.call-done = bf16[128,1,1152]{2,0,1:T(8,128)(2,1)} async-done(((bf16[512,1,1152]{2,0,1:T(8,128)(2,1)}), bf16[128,1,1152]{2,0,1:T(8,128)(2,1)}) %reduce-scatter.21.cloned.1.call-update) | async-done | bytes 294928 | tf_op jit(solution)/shard_map/reduce_scatter | solution.py:189
  777.4 26.6 %reduce-scatter.19.cloned.1.call-done = bf16[128,1,1152]{2,0,1:T(8,128)(2,1)} async-done(((bf16[512,1,1152]{2,0,1:T(8,128)(2,1)}), bf16[128,1,1152]{2,0,1:T(8,128)(2,1)}) %reduce-scatter.19.cloned.1.call-update) | async-done | bytes 294928 | tf_op jit(solution)/shard_map/reduce_scatter | solution.py:124
  806.8 17.5 %all-gather.39.cloned.1.call-done = bf16[512,1,1152]{2,0,1:T(8,128)(2,1)} async-done(((bf16[128,1,1152]{2,0,1:T(8,128)(2,1)}), bf16[512,1,1152]{2,0,1:T(8,128)(2,1)}) %all-gather.39.cloned.1.call-update) | async-done | bytes 1179664 | tf_op jit(solution)/shard_map/all_gather | solution.py:205
  831.5 26.9 %while.94 = (s32[]{:T(128)}, bf16[4,512,72]{1,2,0:T(8,128)(2,1)}, bf16[4,1024,72]{1,2,0:T(8,128)(2,1)}, bf16[4,1024,72]{1,2,0:T(8,128)(2,1)}, bf16[4,512,72]{2,1...) while((s32[]{:T(128)}, bf16[4,512,72]{1,2,0:T(8,128)(2,1)}, ...), condition=%wide.region_25.26_spmd, body=%wide.region_23.25_spmd.sunk | while | flops 381791744 | bytes 30768436 | solution.py:40
  859.4 14.5 reduce-scatter.23.cloned.1.call-done
  874.0 17.6 %reduce-scatter.25.cloned.1.call-done = bf16[512,1,288]{0,2,1:T(8,128)(2,1)} async-done(((bf16[1024,1,288]{0,2,1:T(8,128)(2,1)}), bf16[512,1,288]{0,2,1:T(8,128)(2,1)}) %reduce-scatter.25.cloned.1.call-update) | async-done | bytes 294928 | tf_op jit(solution)/shard_map/reduce_scatter | solution.py:228
  896.1 25.7 %reduce-scatter.27.cloned.1.call-done = bf16[128,1,1152]{2,0,1:T(8,128)(2,1)} async-done(((bf16[512,1,1152]{2,0,1:T(8,128)(2,1)}), bf16[128,1,1152]{2,0,1:T(8,128)(2,1)}) %reduce-scatter.27.cloned.1.call-update) | async-done | bytes 294928 | tf_op jit(solution)/shard_map/reduce_scatter | solution.py:248
  925.4 17.5 %all-gather.41.cloned.1.call-done = bf16[512,1,1152]{2,0,1:T(8,128)(2,1)} async-done(((bf16[128,1,1152]{2,0,1:T(8,128)(2,1)}), bf16[512,1,1152]{2,0,1:T(8,128)(2,1)}) %all-gather.41.cloned.1.call-update) | async-done | bytes 1179664 | tf_op jit(solution)/shard_map/all_gather | solution.py:177
  942.9 5.6 convert_reduce_fusion.1
  952.5 25.7 %reduce-scatter.29.cloned.1.call-done = bf16[128,1,1152]{2,0,1:T(8,128)(2,1)} async-done(((bf16[512,1,1152]{2,0,1:T(8,128)(2,1)}), bf16[128,1,1152]{2,0,1:T(8,128)(2,1)}) %reduce-scatter.29.cloned.1.call-update) | async-done | bytes 294928 | tf_op jit(solution)/shard_map/reduce_scatter | solution.py:189
  981.8 17.5 %all-gather.43.cloned.1.call-done = bf16[512,1,1152]{2,0,1:T(8,128)(2,1)} async-done(((bf16[128,1,1152]{2,0,1:T(8,128)(2,1)}), bf16[512,1,1152]{2,0,1:T(8,128)(2,1)}) %all-gather.43.cloned.1.call-update) | async-done | bytes 1179664 | tf_op jit(solution)/shard_map/all_gather | solution.py:205
  1002.4 21.1 %while.95 = (s32[]{:T(128)}, bf16[4,512,72]{1,2,0:T(8,128)(2,1)}, bf16[4,1024,72]{1,2,0:T(8,128)(2,1)S(1)}, bf16[4,1024,72]{1,2,0:T(8,128)(2,1)S(1)}, bf16[4,512...) while((s32[]{:T(128)}, bf16[4,512,72]{1,2,0:T(8,128)(2,1)}, ...), condition=%wide.region_36.37_spmd, body=%wide.region_34.36_spmd.sunk | while | flops 381791744 | bytes 20151464 | solution.py:40
  1025.1 14.7 reduce-scatter.31.cloned.1.call-done
  1039.7 18.2 %reduce-scatter.33.cloned.1.call-done = bf16[512,1,288]{0,2,1:T(8,128)(2,1)} async-done(((bf16[1024,1,288]{0,2,1:T(8,128)(2,1)}), bf16[512,1,288]{0,2,1:T(8,128)(2,1)}) %reduce-scatter.33.cloned.1.call-update) | async-done | bytes 294928 | tf_op jit(solution)/shard_map/reduce_scatter | solution.py:228
  1062.7 5.4 convolution_convert_fusion.2
  1092.4 52.3 %all-reduce.7 = (bf16[4,6,1152]{2,0,1:T(4,128)(2,1)S(1)}, bf16[4,6,1152]{2,0,1:T(4,128)(2,1)S(1)}, f32[2,1152]{1,0:T(2,128)S(1)}, f32[2,1152]{1,0:T(2,128)S(1)},...) all-reduce(f32[4,6,1152]{2,0,1:T(4,128)S(1)} %dynamic_update_slice., ...), channel_id=1, replica_groups=mesh['shard'=4,'context'=2,'tensor'=4] {'shard','context','tensor'}, use_global_device_ids=true, to_apply=%region_56.57 | all-reduce | flops 73728 | bytes 479232 | tf_op jit(solution)/shard_map/psum | solution.py:341
  1152.9 37.0 %all-reduce.1 = (bf16[4,1152]{1,0:T(4,128)(2,1)S(1)}, bf16[4,1152]{1,0:T(4,128)(2,1)S(1)}) all-reduce(bf16[4,1152]{1,0:T(4,128)(2,1)S(1)} %fusion.134, bf16[4,1152]{1,0:T(4,128)(2,1)S(1)} %fusion.137), channel_id=1, replica_groups=mesh['shard'=4,'context'=2,'tensor'=4] {'shard','context'}, use_global_device_ids=true, to_apply=%region_57.58 | all-reduce | flops 9216 | bytes 36864 | tf_op jit(solution)/shard_map/psum | solution.py:367
  1195.6 6.0 pad_maximum_fusion
  1201.7 381.9 %all-reduce.6.cloned.1.call-done = (bf16[3,1152,288]{1,2,0:T(8,128)(2,1)}, bf16[3,1152,288]{1,2,0:T(8,128)(2,1)}, bf16[288,1152]{1,0:T(8,128)(2,1)}, bf16[288,11...) async-done(((bf16[3,1152,288]{1,2,0:T(8,128)(2,1)}, ...) | async-done | bytes 15925264 | tf_op jit(solution)/shard_map/psum | solution.py:363
  (558 shorter events, 246.7 us)
Async XLA Ops:
  7.2 144.5 %all-gather.19.cloned.1.call-start = ((), (), s32[]{:S(2)}) async-start(), calls=%async_computation.13 | async-start | bytes 4423680 | tf_op jit(solution)/shard_map/all_gather | solution.py:78
  10.9 147.8 %all-gather.17.cloned.1.call-start = ((), (), s32[]{:S(2)}) async-start(), calls=%async_computation.12 | async-start | bytes 1474560 | tf_op jit(solution)/shard_map/all_gather | solution.py:91
  16.8 88.0 %copy-start.4 = (bf16[128,1,1152]{2,0,1:T(8,128)(2,1)S(1)}, bf16[128,1,1152]{2,0,1:T(8,128)(2,1)}, u32[]{:S(2)}) copy-start(bf16[128,1,1152]{2,0,1:T(8,128)(2,1)} %param.21) | copy-start | bytes 884740
  108.7 38.2 %copy-start.41 = (f32[1152]{0:T(1024)}, f32[1152]{0:T(1024)S(1)}, u32[]{:S(2)}) copy-start(f32[1152]{0:T(1024)S(1)} %get-tuple-element.347) | copy-start | bytes 13828
  109.8 118.5 %reduce-scatter.13.cloned.1.call-start = ((), (), s32[]{:S(2)}) async-start(), calls=%async_computation.14 | async-start | bytes 2949120 | tf_op jit(solution)/shard_map/reduce_scatter | solution.py:106
  193.8 91.8 %all-gather.23.cloned.1.call-start = ((), (), s32[]{:S(2)}) async-start(), calls=%async_computation.16 | async-start | bytes 3317760 | tf_op jit(solution)/shard_map/all_gather | solution.py:80
  196.3 34.4 %copy-start.26 = (bf16[2,1152,288]{1,2,0:T(8,128)(2,1)S(1)}, bf16[2,1152,288]{1,2,0:T(8,128)(2,1)}, u32[]{:S(2)}) copy-start(bf16[2,1152,288]{1,2,0:T(8,128)(2,1)} %param.31) | copy-start | bytes 3981316
  196.4 107.5 %all-gather.21.cloned.1.call-start = ((), (), s32[]{:S(2)}) async-start(), calls=%async_computation.15 | async-start | bytes 1474560 | tf_op jit(solution)/shard_map/all_gather | solution.py:117
  197.0 34.9 %copy-start.43 = (f32[1152]{0:T(1024)}, f32[1152]{0:T(1024)S(1)}, u32[]{:S(2)}) copy-start(f32[1152]{0:T(1024)S(1)} %get-tuple-element.362) | copy-start | bytes 13828
  230.7 130.4 %all-gather.25.cloned.1.call-start = ((), (), s32[]{:S(2)}) async-start(), calls=%async_computation.17 | async-start | bytes 3317760 | tf_op jit(solution)/shard_map/all_gather | solution.py:81
  232.0 159.4 %reduce-scatter.15.cloned.1.call-start = ((), (), s32[]{:S(2)}) async-start(), calls=%async_computation.18 | async-start | bytes 1474560 | tf_op jit(solution)/shard_map/reduce_scatter | solution.py:124
  309.2 57.7 %copy-start.13 = (bf16[1,3,288,288]{3,2,1,0:T(8,128)(2,1)S(1)}, bf16[1,3,288,288]{3,2,1,0:T(8,128)(2,1)}, u32[]{:S(2)}) copy-start(bf16[1,3,288,288]{3,2,1,0:T(8,128)(2,1)} %get-tuple-element.480) | copy-start | bytes 1492996
  366.8 119.1 %all-gather.29.cloned.1.call-start = ((), (), s32[]{:S(2)}) async-start(), calls=%async_computation.20 | async-start | bytes 4423680 | tf_op jit(solution)/shard_map/all_gather | solution.py:78
  368.3 135.5 %all-gather.27.cloned.1.call-start = ((), (), s32[]{:S(2)}) async-start(), calls=%async_computation.19 | async-start | bytes 1474560 | tf_op jit(solution)/shard_map/all_gather | solution.py:91
  370.8 22.9 %copy-start.54 = (f32[1,2,288]{2,1,0:T(2,128)S(1)}, f32[1,2,288]{2,1,0:T(2,128)}, u32[]{:S(2)}) copy-start(f32[1,2,288]{2,1,0:T(2,128)} %get-tuple-element.492) | copy-start | bytes 6916
  393.7 196.0 %reduce-scatter.17.cloned.1.call-start = ((), (), s32[]{:S(2)}) async-start(), calls=%async_computation.21 | async-start | bytes 2949120 | tf_op jit(solution)/shard_map/reduce_scatter | solution.py:106
  556.7 33.0 %copy-start.45 = (f32[1152]{0:T(1024)S(1)}, f32[1152]{0:T(1024)}, u32[]{:S(2)}) copy-start(f32[1152]{0:T(1024)} %get-tuple-element.361) | copy-start | bytes 13828
  556.7 35.0 %copy-start.49 = (f32[1152]{0:T(1024)S(1)}, f32[1152]{0:T(1024)}, u32[]{:S(2)}) copy-start(f32[1152]{0:T(1024)} %get-tuple-element.338) | copy-start | bytes 13828
  556.7 89.8 %all-gather.33.cloned.1.call-start = ((), (), s32[]{:S(2)}) async-start(), calls=%async_computation.23 | async-start | bytes 3317760 | tf_op jit(solution)/shard_map/all_gather | solution.py:80
  557.5 107.3 %all-gather.31.cloned.1.call-start = ((), (), s32[]{:S(2)}) async-start(), calls=%async_computation.22 | async-start | bytes 1474560 | tf_op jit(solution)/shard_map/all_gather | solution.py:117
  590.9 73.9 %copy-start.61 = (f32[1152]{0:T(1024)S(1)}, f32[1152]{0:T(1024)}, u32[]{:S(2)}) copy-start(f32[1152]{0:T(1024)} %get-tuple-element.359) | copy-start | bytes 13828
  592.6 91.7 %all-gather.37.cloned.1.call-start = ((), (), s32[]{:S(2)}) async-start(), calls=%async_computation.26 | async-start | bytes 1474560 | tf_op jit(solution)/shard_map/all_gather | solution.py:177
  594.5 146.7 %all-gather.35.cloned.1.call-start = ((), (), s32[]{:S(2)}) async-start(), calls=%async_computation.24 | async-start | bytes 3317760 | tf_op jit(solution)/shard_map/all_gather | solution.py:81
  595.0 180.9 %reduce-scatter.21.cloned.1.call-start = ((), (), s32[]{:S(2)}) async-start(), calls=%async_computation.27 | async-start | bytes 1474560 | tf_op jit(solution)/shard_map/reduce_scatter | solution.py:189
  751.4 52.6 %reduce-scatter.19.cloned.1.call-start = ((), (), s32[]{:S(2)}) async-start(), calls=%async_computation.25 | async-start | bytes 1474560 | tf_op jit(solution)/shard_map/reduce_scatter | solution.py:124
  757.1 46.9 %copy-start.50 = (f32[1152]{0:T(1024)S(1)}, f32[1152]{0:T(1024)}, u32[]{:S(2)}) copy-start(f32[1152]{0:T(1024)} %get-tuple-element.357) | copy-start | bytes 13828
  757.1 67.2 %all-gather.39.cloned.1.call-start = ((), (), s32[]{:S(2)}) async-start(), calls=%async_computation.28 | async-start | bytes 1474560 | tf_op jit(solution)/shard_map/all_gather | solution.py:205
  806.8 67.2 %reduce-scatter.23.cloned.1.call-start = ((), (), s32[]{:S(2)}) async-start(), calls=%async_computation.29 | async-start | bytes 884736 | tf_op jit(solution)/shard_map/reduce_scatter | solution.py:222
  858.5 33.2 %reduce-scatter.25.cloned.1.call-start = ((), (), s32[]{:S(2)}) async-start(), calls=%async_computation.30 | async-start | bytes 884736 | tf_op jit(solution)/shard_map/reduce_scatter | solution.py:228
  859.2 62.6 %reduce-scatter.27.cloned.1.call-start = ((), (), s32[]{:S(2)}) async-start(), calls=%async_computation.31 | async-start | bytes 1474560 | tf_op jit(solution)/shard_map/reduce_scatter | solution.py:248
  891.6 30.2 %copy-start.59 = (f32[128]{0:T(128)S(1)}, f32[128]{0:T(128)}, u32[]{:S(2)}) copy-start(f32[128]{0:T(128)} %copy-done.58) | copy-start | bytes 1540
  891.6 30.2 %copy-start.68 = (f32[128]{0:T(128)S(1)}, f32[128]{0:T(128)}, u32[]{:S(2)}) copy-start(f32[128]{0:T(128)} %copy-done.67) | copy-start | bytes 1540
  896.0 27.1 %copy-start.15 = (f32[128,1,1152]{2,0,1:T(8,128)S(1)}, f32[128,1,1152]{2,0,1:T(8,128)}, u32[]{:S(2)}) copy-start(f32[128,1,1152]{2,0,1:T(8,128)} %reduce-scatter.17.cloned.1.call-done) | copy-start | bytes 1769476
  896.0 27.1 %copy-start.16 = (f32[128,1,1152]{2,0,1:T(8,128)S(1)}, f32[128,1,1152]{2,0,1:T(8,128)}, u32[]{:S(2)}) copy-start(f32[128,1,1152]{2,0,1:T(8,128)} %get-tuple-element.461) | copy-start | bytes 1769476
  896.0 46.9 %all-gather.41.cloned.1.call-start = ((), (), s32[]{:S(2)}) async-start(), calls=%async_computation.32 | async-start | bytes 1474560 | tf_op jit(solution)/shard_map/all_gather | solution.py:177
  925.3 52.9 %reduce-scatter.29.cloned.1.call-start = ((), (), s32[]{:S(2)}) async-start(), calls=%async_computation.33 | async-start | bytes 1474560 | tf_op jit(solution)/shard_map/reduce_scatter | solution.py:189
  949.5 28.7 %copy-start.57 = (f32[128]{0:T(128)S(1)}, f32[128]{0:T(128)}, u32[]{:S(2)}) copy-start(f32[128]{0:T(128)} %copy-done.56) | copy-start | bytes 1540
  949.5 28.7 %copy-start.66 = (f32[128]{0:T(128)S(1)}, f32[128]{0:T(128)}, u32[]{:S(2)}) copy-start(f32[128]{0:T(128)} %copy-done.65) | copy-start | bytes 1540
  952.4 27.0 %copy-start.17 = (f32[128,1,1152]{2,0,1:T(8,128)S(1)}, f32[128,1,1152]{2,0,1:T(8,128)}, u32[]{:S(2)}) copy-start(f32[128,1,1152]{2,0,1:T(8,128)} %get-tuple-element.453) | copy-start | bytes 1769476
  952.4 27.1 %copy-start.27 = (bf16[128,1,1152]{2,0,1:T(8,128)(2,1)S(1)}, bf16[128,1,1152]{2,0,1:T(8,128)(2,1)}, u32[]{:S(2)}) copy-start(bf16[128,1,1152]{2,0,1:T(8,128)(2,1)} %reduce-scatter.15.cloned.1.call-done) | copy-start | bytes 884740
  952.4 27.1 %copy-start.47 = (f32[1152]{0:T(1024)S(1)}, f32[1152]{0:T(1024)}, u32[]{:S(2)}) copy-start(f32[1152]{0:T(1024)} %copy-done.46) | copy-start | bytes 13828
  952.4 46.9 %copy-start.12 = (bf16[1,288,1152]{2,1,0:T(8,128)(2,1)S(1)}, bf16[1,288,1152]{2,1,0:T(8,128)(2,1)}, u32[]{:S(2)}) copy-start(bf16[1,288,1152]{2,1,0:T(8,128)(2,1)} %copy.85) | copy-start | bytes 1990660
  952.5 46.9 %all-gather.43.cloned.1.call-start = ((), (), s32[]{:S(2)}) async-start(), calls=%async_computation.34 | async-start | bytes 1474560 | tf_op jit(solution)/shard_map/all_gather | solution.py:205
  981.7 58.0 %reduce-scatter.31.cloned.1.call-start = ((), (), s32[]{:S(2)}) async-start(), calls=%async_computation.35 | async-start | bytes 884736 | tf_op jit(solution)/shard_map/reduce_scatter | solution.py:222
  1024.3 33.7 %reduce-scatter.33.cloned.1.call-start = ((), (), s32[]{:S(2)}) async-start(), calls=%async_computation.36 | async-start | bytes 884736 | tf_op jit(solution)/shard_map/reduce_scatter | solution.py:228
  1025.0 64.4 %reduce-scatter.35.cloned.1.call-start = ((), (), s32[]{:S(2)}) async-start(), calls=%async_computation.37 | async-start | bytes 1474560 | tf_op jit(solution)/shard_map/reduce_scatter | solution.py:248
  1062.4 521.1 %all-reduce.6.cloned.1.call-start = ((), (), s32[]{:S(2)}) async-start(), calls=%async_computation.38 | async-start | bytes 31850496 | tf_op jit(solution)/shard_map/psum | solution.py:363
  1149.9 40.8 %copy-start.38 = (f32[4,1152]{1,0:T(4,128)S(1)}, f32[4,1152]{1,0:T(4,128)}, u32[]{:S(2)}) copy-start(f32[4,1152]{1,0:T(4,128)} %param.22) | copy-start | bytes 55300
  (92 other events, 236.9 us)
Sparse Core Ops, SparseCore 0:
  11.0 111.9 all-gather.18
  125.1 15.5 all-gather.16
  193.9 34.3 reduce-scatter.12
  230.3 55.2 all-gather.22
  287.6 16.1 all-gather.20
  305.8 55.2 all-gather.24
  367.0 24.3 reduce-scatter.14
  393.5 92.3 all-gather.28
  488.1 15.6 all-gather.26
  556.8 32.8 reduce-scatter.16
  591.3 55.2 all-gather.32
  648.6 16.1 all-gather.30
  666.9 17.4 all-gather.36
  685.8 55.2 all-gather.34
  751.5 24.3 reduce-scatter.20
  778.3 25.5 reduce-scatter.18
  806.9 17.4 all-gather.38
  858.6 15.3 reduce-scatter.22
  876.2 15.3 reduce-scatter.24
  896.1 25.6 reduce-scatter.26
  925.4 17.4 all-gather.40
  952.6 25.5 reduce-scatter.28
  981.9 17.4 all-gather.42
  1024.4 15.3 reduce-scatter.30
  1042.6 15.3 reduce-scatter.32
  1062.5 25.6 reduce-scatter.34
  1094.8 488.7 all-reduce.5
where the time goes:
time: 1620 us; the launch traced here: 1610 us
  waiting for transfers between devices  984 us (61%)
  blocking collectives  305 us (19%)
  matrix products  155 us (10%)
  local copies, waits for them, and re-layouts  79.4 us (5%)
  other arithmetic  67.3 us (4%)
    psum x1, waiting for transfers between devices, body(): lax.psum(grad_w_qkv.astype(jnp.bfloat16), ('shard', 'context'))  382 us
    all_gather x2, waiting for transfers between devices, fetch_weights(): lax.all_gather(down_part, 'shard', axis=2, tiled=True)  109 us
    all_gather x2, waiting for transfers between devices, fetch_weights(): lax.all_gather(up_part, 'shard', axis=1, tiled=True)  104 us
    all_gather x2, blocking collectives, fetch_weights(): lax.all_gather(proj_part, 'shard', axis=2, tiled=True)  94.4 us
    all_gather x2, blocking collectives, fetch_weights(): lax.all_gather(mod_part, 'shard', axis=3, tiled=True)  87.4 us
    reduce_scatter x2, waiting for transfers between devices, layer_forward(): lax.psum_scatter(jnp.einsum('tbe,ed->tbd', row_block, full_proj, preferre...  63 us
    psum x1, blocking collectives, body(): lax.psum((grad_mod_pad, bias_proj, bias_down, bias_qv_pad, bias_up_pad),...  52.3 us
    reduce_scatter x2, waiting for transfers between devices, layer_forward(): lax.psum_scatter(jnp.einsum('tbf,fd->tbd', row_block, full_down, preferre...  47.2 us
  transfers between devices with their start and end apart: 27, of which 24 were waited for; matrix products, arithmetic and copies ran while one was open for 8% of the time, Pallas kernels for 0%

commit v1 on v0

--- a/solution.py
+++ b/solution.py
@@ -1,6 +1,10 @@
+import functools
+
 import jax
 import jax.numpy as jnp
 from jax import lax
+from jax.experimental import pallas as pl
+from jax.experimental.pallas import tpu as pltpu
 from jax.sharding import PartitionSpec as P
 
 D = 1152
@@ -410,9 +414,1223 @@
     )
 
 
+MESH = pl.DeviceIdType.MESH
+F32 = jnp.float32
+BF16 = jnp.bfloat16
+
+
+def nt(a, b):
+    return lax.dot_general(a, b, (((1,), (1,)), ((), ())), preferred_element_type=F32)
+
+
+def nn(a, b):
+    return jnp.dot(a, b, preferred_element_type=F32)
+
+
+def tn(a, b):
+    return lax.dot_general(a, b, (((0,), (0,)), ((), ())), preferred_element_type=F32)
+
+
+def fold(v):
+    return jnp.sum(v.reshape(v.shape[0] // 8, 8, v.shape[1]), axis=0)
+
+
+def rows_at(start, size, multiple=16):
+    return pl.ds(pl.multiple_of(start, multiple), size)
+
+
+def stage_kernel(
+    zs_n,
+    x_ref,
+    cot_ref,
+    modin_ref,
+    bias_ref,
+    s_ref,
+    out_ref,
+    gin_ref,
+    gw_ref,
+    small_ref,
+    k_mixed,
+    k_ff,
+    k_pre,
+    k_own,
+    w,
+    mixed,
+    qkv,
+    qa,
+    att,
+    ffall,
+    pre,
+    own,
+    inv,
+    lse,
+    modr,
+    modv,
+    af,
+    pool,
+    ra,
+    ysend,
+    yrecv,
+    xsend,
+    xrecv,
+    dsend,
+    drecv,
+    gff,
+    gpre,
+    gb,
+    dqkv,
+    dkv,
+    pb,
+    otw,
+    ot,
+    rx,
+    rz,
+    sm,
+    smr,
+    m_s,
+    m_r,
+    wz_s,
+    wz_r,
+    wx_s,
+    wx_r,
+    w_l,
+    ap_s,
+    ap_r,
+    at_s,
+    at_r,
+    rt_s,
+    rt_r,
+    rp_s,
+    rp_r,
+    gx_s,
+    gx_r,
+    gz_s,
+    gz_r,
+    gf_s,
+    gf_r,
+    g_l,
+    sm_s,
+    sm_r,
+    k_s,
+):
+    z = lax.axis_index("shard")
+    c = lax.axis_index("context")
+    t = lax.axis_index("tensor")
+    y = t // 2
+    k = t - 2 * y
+    tp = t + 1 - 2 * k
+    t_far = t + 2 - 4 * y
+    tp_far = tp + 2 - 4 * y
+    dev_p = (z, c, tp)
+    dev_y = (z, c, t_far)
+    dev_x = (z, 1 - c, t)
+    zo = [lax.rem(z + d, zs_n) for d in range(1, zs_n)]
+    scale = HD ** (-0.5)
+    hb = gin_ref
+
+    def rc(src, dst, ss, rs, dev):
+        return pltpu.make_async_remote_copy(
+            src_ref=src, dst_ref=dst, send_sem=ss, recv_sem=rs, device_id=dev, device_id_type=MESH
+        )
+
+    barrier = pltpu.get_barrier_semaphore()
+    for dev in [dev_p, dev_y, dev_x] + [(zz, c, t) for zz in zo]:
+        pl.semaphore_signal(barrier, inc=1, device_id=dev, device_id_type=MESH)
+    pl.semaphore_wait(barrier, 2 + zs_n)
+
+    def mod_copy(d, to, frm):
+        return rc(modin_ref.at[to], modr.at[frm], m_s.at[d], m_r.at[frm], (to, c, t))
+
+    for d, zz in enumerate(zo):
+        mod_copy(d, zz, z).start()
+
+    half = 144
+
+    def w_rows(zz, cc):
+        return rows_at(288 * zz + half * cc, half)
+
+    def w0(i):
+        pltpu.make_async_copy(s_ref.at[i], w.at[i, rows_at(288 * z, 288)], w_l.at[i]).start()
+        for d, zz in enumerate(zo):
+            rc(
+                s_ref.at[i, rows_at(half * c, half)],
+                w.at[i, w_rows(z, c)],
+                wz_s.at[i, d],
+                wz_r.at[i, z],
+                (zz, c, t),
+            ).start()
+
+    def w1(i):
+        for d, zz in enumerate(zo):
+            part = w.at[i, w_rows(zz, c)]
+            rc(part, part, wz_s.at[i, d], wz_r.at[i, zz], dev_x).wait_recv()
+            rc(part, part, wx_s.at[i, d], wx_r.at[i, d], dev_x).start()
+
+    def w2(i):
+        for d, zz in enumerate(zo):
+            part = w.at[i, w_rows(zz, 1 - c)]
+            rc(part, part, wx_s.at[i, d], wx_r.at[i, d], dev_x).wait_recv()
+        pltpu.make_async_copy(s_ref.at[i], w.at[i, rows_at(288 * z, 288)], w_l.at[i]).wait()
+
+    def w_drain(i):
+        for d, zz in enumerate(zo):
+            part = w.at[i, w_rows(zz, c)]
+            rc(part, part, wz_s.at[i, d], wz_r.at[i, zz], dev_x).wait_send()
+            rc(part, part, wx_s.at[i, d], wx_r.at[i, d], dev_x).wait_send()
+
+    for i in range(6):
+        w0(i)
+
+    modr[z] = modin_ref[z]
+    for zz in zo:
+        mod_copy(0, zz, zz).wait_recv()
+    for d in range(zs_n - 1):
+        mod_copy(d, zo[d], z).wait_send()
+    for layer in range(LAYERS):
+        for zz in range(zs_n):
+            modv[layer, 0:6, 288 * zz : 288 * (zz + 1)] = modr[zz, 8 * layer : 8 * layer + 6, 0:288]
+
+    def mrow(layer, kind):
+        return modv[layer, kind : kind + 1, :]
+
+    def ap_copy(layer, index, block, offset, size, dev):
+        part = mixed.at[rows_at(128 * block + offset, size)]
+        return rc(part, part, ap_s.at[layer, index], ap_r.at[layer, index], dev)
+
+    def ap_parts(layer):
+        b_own, b_p = 4 * c + t, 4 * c + tp
+        b_y, b_yp = 4 * c + t_far, 4 * c + tp_far
+        b_x, b_xp = 4 * (1 - c) + t, 4 * (1 - c) + tp
+        b_d, b_dp = 4 * (1 - c) + t_far, 4 * (1 - c) + tp_far
+        sends = [
+            (0, b_own, 0, 128, dev_p),
+            (1, b_own, 0, 64, dev_y),
+            (4, b_own, 64, 64, dev_x),
+            (2, b_own, 64, 64, dev_y),
+            (3, b_own, 0, 64, dev_x),
+            (5, b_y, 0, 64, dev_x),
+            (6, b_x, 64, 64, dev_y),
+            (7, b_y, 0, 64, dev_p),
+            (8, b_y, 64, 64, dev_p),
+            (9, b_x, 0, 64, dev_p),
+            (10, b_x, 64, 64, dev_p),
+            (11, b_d, 0, 64, dev_p),
+            (12, b_d, 64, 64, dev_p),
+        ]
+        recvs = {
+            0: (b_p, 0, 128),
+            1: (b_y, 0, 64),
+            2: (b_y, 64, 64),
+            3: (b_x, 0, 64),
+            4: (b_x, 64, 64),
+            5: (b_d, 0, 64),
+            6: (b_d, 64, 64),
+            7: (b_yp, 0, 64),
+            8: (b_yp, 64, 64),
+            9: (b_xp, 0, 64),
+            10: (b_xp, 64, 64),
+            11: (b_dp, 0, 64),
+            12: (b_dp, 64, 64),
+        }
+
+        def send(index):
+            for entry in sends:
+                if entry[0] == index:
+                    ap_copy(layer, *entry).start()
+
+        def wait(index):
+            ap_copy(layer, index, *recvs[index], dev_p).wait_recv()
+
+        def drain():
+            for entry in sends:
+                ap_copy(layer, *entry).wait_send()
+
+        return send, wait, drain
+
+    def gather_plane(layer, compute):
+        send, wait, drain = ap_parts(layer)
+        for index in (0, 1, 4, 2, 3):
+            send(index)
+
+        def step(i, carry):
+            b0, b1, b2 = lax.rem(i, 2), lax.rem(i // 2, 2), i // 4
+
+            @pl.when(i == 1)
+            def _():
+                wait(0)
+
+            @pl.when(i == 2)
+            def _():
+                wait(1)
+                send(5)
+                send(7)
+                wait(4)
+                send(6)
+                send(10)
+                wait(2)
+                send(8)
+                wait(3)
+                send(9)
+
+            @pl.when(i == 3)
+            def _():
+                wait(7)
+                wait(8)
+
+            @pl.when(i == 5)
+            def _():
+                wait(9)
+                wait(10)
+
+            @pl.when(i == 6)
+            def _():
+                wait(5)
+                send(11)
+                wait(6)
+                send(12)
+
+            @pl.when(i == 7)
+            def _():
+                wait(11)
+                wait(12)
+
+            block = (
+                4 * lax.rem(c + b2, 2) + 2 * lax.rem(y + b1, 2) + lax.rem(k + b0, 2)
+            )
+            compute(block)
+            return carry
+
+        lax.fori_loop(0, 8, step, 0)
+        drain()
+
+    def gather_tensor(buf, phase, layer, compute):
+        def copy(index, block, offset, size, dev):
+            part = buf.at[rows_at(128 * block + offset, size)]
+            return rc(part, part, at_s.at[phase, layer, index], at_r.at[phase, layer, index], dev)
+
+        copy(0, t, 0, 128, dev_p).start()
+        copy(1, t, 0, 64, dev_y).start()
+        copy(2, t, 64, 64, dev_y).start()
+
+        def step(i, carry):
+            b0, b1 = lax.rem(i, 2), i // 2
+
+            @pl.when(i == 1)
+            def _():
+                copy(0, tp, 0, 128, dev_p).wait_recv()
+
+            @pl.when(i == 2)
+            def _():
+                copy(1, t_far, 0, 64, dev_y).wait_recv()
+                copy(3, t_far, 0, 64, dev_p).start()
+                copy(2, t_far, 64, 64, dev_y).wait_recv()
+                copy(4, t_far, 64, 64, dev_p).start()
+
+            @pl.when(i == 3)
+            def _():
+                copy(3, tp_far, 0, 64, dev_p).wait_recv()
+                copy(4, tp_far, 64, 64, dev_p).wait_recv()
+
+            compute(2 * lax.rem(y + b1, 2) + lax.rem(k + b0, 2))
+            return carry
+
+        lax.fori_loop(0, 4, step, 0)
+        copy(0, t, 0, 128, dev_p).wait_send()
+        copy(1, t, 0, 64, dev_y).wait_send()
+        copy(2, t, 64, 64, dev_y).wait_send()
+        copy(3, t_far, 0, 64, dev_p).wait_send()
+        copy(4, t_far, 64, 64, dev_p).wait_send()
+
+    def pool_rows(i):
+        return rows_at(128 * i, 128)
+
+    def reduce_tensor(phase, layer, compute, beside):
+        def to_p(i, slot):
+            return rc(
+                pool.at[pool_rows(i)],
+                ra.at[slot],
+                rt_s.at[phase, layer, slot],
+                rt_r.at[phase, layer, slot],
+                dev_p,
+            )
+
+        to_y = rc(ysend, yrecv, rt_s.at[phase, layer, 2], rt_r.at[phase, layer, 2], dev_y)
+
+        def step(i, carry):
+            b0, b1 = 1 - lax.rem(i, 2), 1 - i // 2
+            pool[pool_rows(i), :] = compute(2 * lax.rem(y + b1, 2) + lax.rem(k + b0, 2))
+
+            @pl.when(i == 0)
+            def _():
+                to_p(0, 0).start()
+
+            @pl.when(i == 1)
+            def _():
+                to_p(0, 0).wait_recv()
+
+                def add(r, inner):
+                    rr = rows_at(16 * r, 16)
+                    ysend[rr, :] = (pool[rows_at(128 + 16 * r, 16), :] + ra[0, rr, :]).astype(BF16)
+                    return inner
+
+                lax.fori_loop(0, 8, add, 0)
+                to_y.start()
+
+            @pl.when(i == 2)
+            def _():
+                to_p(2, 1).start()
+
+            return carry
+
+        lax.fori_loop(0, 4, step, 0)
+        beside()
+        to_p(2, 1).wait_recv()
+        to_y.wait_recv()
+        to_p(0, 0).wait_send()
+        to_p(2, 1).wait_send()
+        to_y.wait_send()
+
+        def total(rr, r):
+            return pool[rows_at(384 + 16 * r, 16), :] + ra[1, rr, :] + yrecv[rr, :].astype(F32)
+
+        return total
+
+    def reduce_plane(layer, compute, beside):
+        def to_p(i, slot):
+            return rc(
+                pool.at[pool_rows(i)],
+                ra.at[slot],
+                rp_s.at[layer, slot],
+                rp_r.at[layer, slot],
+                dev_p,
+            )
+
+        d_x = rc(dsend.at[0:64], drecv.at[0:64], rp_s.at[layer, 4], rp_r.at[layer, 4], dev_x)
+        d_y = rc(dsend.at[64:128], drecv.at[64:128], rp_s.at[layer, 5], rp_r.at[layer, 5], dev_y)
+        to_x = rc(xsend, xrecv, rp_s.at[layer, 6], rp_r.at[layer, 6], dev_x)
+        to_y = rc(ysend, yrecv, rp_s.at[layer, 7], rp_r.at[layer, 7], dev_y)
+
+        def step(i, carry):
+            q = i // 2
+            b0, b1, b2 = 1 - lax.rem(i, 2), 1 - lax.rem(q, 2), 1 - q // 2
+            block = (
+                4 * lax.rem(c + b2, 2) + 2 * lax.rem(y + b1, 2) + lax.rem(k + b0, 2)
+            )
+            pool[pool_rows(i), :] = compute(block)
+
+            @pl.when(b0 == 1)
+            def _():
+                to_p(i, q).start()
+
+            @pl.when(i == 1)
+            def _():
+                to_p(0, 0).wait_recv()
+
+                def add(r, inner):
+                    rr = rows_at(16 * r, 16)
+                    dsend[rr, :] = (pool[rows_at(128 + 16 * r, 16), :] + ra[0, rr, :]).astype(BF16)
+                    return inner
+
+                lax.fori_loop(0, 8, add, 0)
+                d_x.start()
+                d_y.start()
+
+            @pl.when(i == 3)
+            def _():
+                to_p(2, 1).wait_recv()
+                d_y.wait_recv()
+
+                def add(r, inner):
+                    rr = rows_at(16 * r, 16)
+                    rh = rows_at(64 + 16 * r, 16)
+                    xsend[rr, :] = (pool[rows_at(384 + 16 * r, 16), :] + ra[1, rr, :]).astype(BF16)
+                    xsend[rh, :] = (
+                        pool[rows_at(448 + 16 * r, 16), :] + ra[1, rh, :] + drecv[rh, :].astype(F32)
+                    ).astype(BF16)
+                    return inner
+
+                lax.fori_loop(0, 4, add, 0)
+                to_x.start()
+
+            @pl.when(i == 5)
+            def _():
+                to_p(4, 2).wait_recv()
+                d_x.wait_recv()
+
+                def add(r, inner):
+                    rr = rows_at(16 * r, 16)
+                    rh = rows_at(64 + 16 * r, 16)
+                    ysend[rr, :] = (
+                        pool[rows_at(640 + 16 * r, 16), :] + ra[2, rr, :] + drecv[rr, :].astype(F32)
+                    ).astype(BF16)
+                    ysend[rh, :] = (pool[rows_at(704 + 16 * r, 16), :] + ra[2, rh, :]).astype(BF16)
+                    return inner
+
+                lax.fori_loop(0, 4, add, 0)
+                to_y.start()
+
+            return carry
+
+        lax.fori_loop(0, 8, step, 0)
+        beside()
+        to_p(6, 3).wait_recv()
+        to_x.wait_recv()
+        to_y.wait_recv()
+        for q in range(4):
+            to_p(2 * q, q).wait_send()
+        for copy in (d_x, d_y, to_x, to_y):
+            copy.wait_send()
+
+        def total(rr, r):
+            return (
+                pool[rows_at(896 + 16 * r, 16), :]
+                + ra[3, rr, :]
+                + xrecv[rr, :].astype(F32)
+                + yrecv[rr, :].astype(F32)
+            )
+
+        return total
+
+    def spread(column):
+        return jnp.broadcast_to(column, (column.shape[0], 128))
+
+    def layer_norm(v):
+        center = v - jnp.mean(v, axis=-1, keepdims=True)
+        r = lax.rsqrt(jnp.mean(center * center, axis=-1, keepdims=True) + epsilon)
+        return center * r, r
+
+    def keep(slot, src, dst):
+        return pltpu.make_async_copy(src, dst, k_s.at[slot])
+
+    def kept():
+        return [(1, ffall, k_ff), (2, pre, k_pre), (3, own, k_own)]
+
+    def head_mask(lo, rows):
+        lane = lax.broadcasted_iota(jnp.int32, (rows, 256), 1)
+        return (lane >= lo) & (lane < lo + HD)
+
+    def forward(layer, carry):
+        ia, iu, id_ = 3 * layer, 3 * layer + 1, 3 * layer + 2
+        own_block = 4 * c + t
+
+        def ln1(r, inner):
+            rr = rows_at(16 * r, 16)
+            n, iv = layer_norm(hb[rr, :])
+            own[0, rr, :] = n
+            inv[layer, 0, rr, :] = spread(iv)
+            mixed[rows_at(128 * own_block + 16 * r, 16), :] = (
+                n * (1.0 + mrow(layer, 1)) + mrow(layer, 0)
+            ).astype(BF16)
+            return inner
+
+        lax.fori_loop(0, 8, ln1, 0)
+
+        @pl.when(layer == 0)
+        def _():
+            w1(0)
+            w2(0)
+
+        @pl.when(layer == 1)
+        def _():
+            w1(4)
+            w2(3)
+
+        def project(block):
+            rr = pool_rows(block)
+            qkv[layer, rr, :] = (
+                nn(mixed[rr, :], w[ia, :, 0:896]) + bias_ref[layer, 0:1, 0:896]
+            ).astype(BF16)
+
+        gather_plane(layer, project)
+
+        @pl.when(layer == 0)
+        def _():
+            w1(1)
+
+        keep(0, mixed, k_mixed.at[layer]).start()
+
+        def take_q(b, inner):
+            v = qkv[layer, rows_at(512 * c + 128 * b, 128), 512:896].astype(F32)
+            qa[layer, rows_at(128 * b, 128), :] = pltpu.roll(v, 320, 1).astype(BF16)
+            return inner
+
+        lax.fori_loop(0, 4, take_q, 0)
+        ot[...] = jnp.zeros_like(ot)
+
+        def head(j, inner):
+            p = j // 2
+            h = j - 2 * p
+            win = pl.ds(pl.multiple_of(128 * p, 128), 256)
+            vwin = pl.ds(pl.multiple_of(256 + 128 * p, 128), 256)
+            lo = 16 * p + 72 * h
+            qm = jnp.where(head_mask(lo, 512), qa[layer, :, win].astype(F32), 0.0).astype(BF16)
+            pb[0:512, 0:256] = qm
+
+            def scores(kb, m8):
+                rr = rows_at(256 * kb, 256)
+                s = nt(qkv[layer, rr, win], pb[0:512, 0:256]) * scale
+                pool[rr, 0:512] = s
+                return jnp.maximum(m8, jnp.max(s.reshape(32, 8, 512), axis=0))
+
+            m8 = lax.fori_loop(0, 4, scores, jnp.full((8, 512), -jnp.inf, F32))
+            mx = jnp.max(m8, axis=0, keepdims=True)
+
+            def exps(kb, l8):
+                rr = rows_at(128 * kb, 128)
+                e = jnp.exp(pool[rr, 0:512] - mx)
+                pool[rr, 0:512] = e
+                return l8 + fold(e)
+
+            l8 = lax.fori_loop(0, 8, exps, jnp.zeros((8, 512), F32))
+            row_sum = jnp.sum(l8, axis=0, keepdims=True)
+            lse[layer, j, 0:1, :] = mx + jnp.log(row_sum)
+            inverse = 1.0 / row_sum
+
+            def probs(kb, inner2):
+                rr = rows_at(128 * kb, 128)
+                pb[rows_at(512 + 128 * kb, 128), :] = (pool[rr, 0:512] * inverse).astype(BF16)
+                return inner2
+
+            lax.fori_loop(0, 8, probs, 0)
+            otw[...] = tn(qkv[layer, :, vwin], pb[512:1536, :])
+            ot[pl.ds(pl.multiple_of(96 + 72 * j, 8), 72), :] = otw[
+                pl.ds(pl.multiple_of(32 + lo, 8), 72), :
+            ]
+            return inner
+
+        lax.fori_loop(0, 4, head, 0)
+
+        def put_att(b, inner):
+            cols = ot[:, pl.ds(pl.multiple_of(128 * b, 128), 128)]
+            att[layer, rows_at(128 * b, 128), :] = cols.T.astype(BF16)
+            return inner
+
+        lax.fori_loop(0, 4, put_att, 0)
+
+        @pl.when(layer == 0)
+        def _():
+            w1(2)
+
+        @pl.when(layer == 1)
+        def _():
+            w1(5)
+
+        def branch(b):
+            return nt(att[layer, rows_at(128 * b, 128), :], w[ia, :, 768:1152])
+
+        total1 = reduce_tensor(0, layer, branch, lambda: None)
+
+        def ln2(r, inner):
+            rr = rows_at(16 * r, 16)
+            br = total1(rr, r) + bias_ref[layer, 1:2, :]
+            own[2, rr, :] = br
+            v = hb[rr, :] + mrow(layer, 2) * br
+            af[rr, :] = v
+            n, iv = layer_norm(v)
+            own[1, rr, :] = n
+            inv[layer, 1, rr, :] = spread(iv)
+            ffall[rows_at(128 * t + 16 * r, 16), :] = (
+                n * (1.0 + mrow(layer, 4)) + mrow(layer, 3)
+            ).astype(BF16)
+            return inner
+
+        lax.fori_loop(0, 8, ln2, 0)
+        w2(iu)
+
+        def up(b):
+            rr = rows_at(128 * b, 128)
+            pre[rr, :] = nn(ffall[rr, :], w[iu]) + bias_ref[layer, 2:3, :]
+
+            def gelu(r, inner):
+                r2 = rows_at(128 * b + 16 * r, 16)
+                gpre[r2, :] = jax.nn.gelu(pre[r2, :], approximate=True).astype(BF16)
+                return inner
+
+            lax.fori_loop(0, 8, gelu, 0)
+
+        gather_tensor(ffall, 0, layer, up)
+        w2(id_)
+
+        @pl.when(layer == 0)
+        def _():
+            keep(1, ffall, k_ff).start()
+            keep(2, pre, k_pre).start()
+
+        def down(b):
+            return nt(gpre[rows_at(128 * b, 128), :], w[id_])
+
+        def beside():
+            @pl.when(layer == 0)
+            def _():
+                w1(3)
+
+        keep(0, mixed, k_mixed.at[layer]).wait()
+        total2 = reduce_tensor(1, layer, down, beside)
+
+        def finish(r, inner):
+            rr = rows_at(16 * r, 16)
+            fo = total2(rr, r) + bias_ref[layer, 3:4, :]
+            own[3, rr, :] = fo
+            hb[rr, :] = af[rr, :] + mrow(layer, 5) * fo
+            return inner
+
+        lax.fori_loop(0, 8, finish, 0)
+
+        @pl.when(layer == 0)
+        def _():
+            keep(3, own, k_own).start()
+            for slot, src, dst in kept():
+                keep(slot, src, dst).wait()
+
+        return carry
+
+    hb[...] = x_ref[...].astype(F32)
+    lax.fori_loop(0, LAYERS, forward, 0)
+    out_ref[...] = hb[...].astype(BF16)
+    for i in range(6):
+        w_drain(i)
+    hb[...] = cot_ref[...].astype(F32)
+
+    def g_copy0(i, m, d, zz):
+        return rc(w.at[i, w_rows(zz, 1 - c)], rx.at[m, zz], gx_s.at[i, d], gx_r.at[i, zz], dev_x)
+
+    def g0(i, m):
+        for d, zz in enumerate(zo + [z]):
+            g_copy0(i, m, d, zz).start()
+
+    def g_copy1(i, d, zz):
+        return rc(w.at[i, w_rows(zz, c)], rz.at[i, d], gz_s.at[i, d], gz_r.at[i, d], (zz, c, t))
+
+    def g1(i, m):
+        for d, zz in enumerate(zo + [z]):
+            g_copy0(i, m, d, zz).wait_recv()
+
+            def add(r, inner):
+                rr = rows_at(288 * zz + half * c + 16 * r, 16)
+                w[i, rr, :] = (
+                    w[i, rr, :].astype(F32) + rx[m, zz, rows_at(16 * r, 16), :].astype(F32)
+                ).astype(BF16)
+                return inner
+
+            lax.fori_loop(0, 9, add, 0)
+            if d < zs_n - 1:
+                g_copy1(i, d, zz).start()
+
+    def g_copy2(i):
+        here = gw_ref.at[i, rows_at(half * c, half)]
+        return rc(w.at[i, w_rows(z, c)], here, gf_s.at[i], gf_r.at[i], dev_x)
+
+    def g_out(i):
+        here = gw_ref.at[i, rows_at(half * c, half)]
+        return pltpu.make_async_copy(w.at[i, w_rows(z, c)], here, g_l.at[i])
+
+    def g2(i, m):
+        for d in range(zs_n - 1):
+            rc(rz.at[i, d], rz.at[i, d], gz_s.at[i, d], gz_r.at[i, d], dev_x).wait_recv()
+        for d, zz in enumerate(zo + [z]):
+            g_copy0(i, m, d, zz).wait_send()
+
+        def add(r, inner):
+            rr = rows_at(288 * z + half * c + 16 * r, 16)
+            total = w[i, rr, :].astype(F32)
+            for d in range(zs_n - 1):
+                total = total + rz[i, d, rows_at(16 * r, 16), :].astype(F32)
+            w[i, rr, :] = total.astype(BF16)
+            return inner
+
+        lax.fori_loop(0, 9, add, 0)
+        g_copy2(i).start()
+        g_out(i).start()
+
+    def g3(i):
+        other = gw_ref.at[i, rows_at(half * (1 - c), half)]
+        rc(other, other, gf_s.at[i], gf_r.at[i], dev_x).wait_recv()
+        g_copy2(i).wait_send()
+        g_out(i).wait()
+        for d, zz in enumerate(zo):
+            g_copy1(i, d, zz).wait_send()
+
+    def sm_copy(layer, index, size, dev):
+        return rc(
+            sm.at[layer, 0:size],
+            smr.at[layer, index, 0:size],
+            sm_s.at[layer, index],
+            sm_r.at[layer, index],
+            dev,
+        )
+
+    def small(layer):
+        for index, size, dev in ((0, 8, dev_p), (1, 8, dev_y), (2, 16, dev_x)):
+            step = sm_copy(layer, index, size, dev)
+            step.start()
+            step.wait_send()
+            step.wait_recv()
+            sm[layer, 0:size, :] = sm[layer, 0:size, :] + smr[layer, index, 0:size, :]
+        small_ref[layer, z] = sm[layer]
+        for d, zz in enumerate(zo):
+            rc(
+                sm.at[layer],
+                small_ref.at[layer, z],
+                sm_s.at[layer, 3 + d],
+                sm_r.at[layer, 3 + z],
+                (zz, c, t),
+            ).start()
+
+    def small_end(layer):
+        for d, zz in enumerate(zo):
+            end = rc(
+                sm.at[layer],
+                small_ref.at[layer, zz],
+                sm_s.at[layer, 3 + d],
+                sm_r.at[layer, 3 + zz],
+                (zz, c, t),
+            )
+            end.wait_recv()
+            end.wait_send()
+
+    zero8 = jnp.zeros((8, D), F32)
+
+    def put_sum(layer, row, v8):
+        sm[layer, row : row + 1, 0 : v8.shape[1]] = jnp.sum(v8, axis=0, keepdims=True)
+
+    def backward(step_index, carry):
+        layer = LAYERS - 1 - step_index
+        ia, iu, id_ = 3 * layer, 3 * layer + 1, 3 * layer + 2
+
+        @pl.when(layer == 0)
+        def _():
+            keep(3, k_own, own).wait()
+
+        def start(r, sums):
+            rr = rows_at(16 * r, 16)
+            g = hb[rr, :]
+            gf = (mrow(layer, 5) * g).astype(BF16)
+            gff[rows_at(128 * t + 16 * r, 16), :] = gf
+            return (sums[0] + fold(g * own[3, rr, :]), sums[1] + fold(gf.astype(F32)))
+
+        s_gate2, s_bdown = lax.fori_loop(0, 8, start, (zero8, zero8))
+        put_sum(layer, 5, s_gate2)
+        put_sum(layer, 7, s_bdown)
+
+        @pl.when(layer == 0)
+        def _():
+            keep(2, k_pre, pre).wait()
+
+        sm[layer, 9:10, :] = jnp.zeros((1, D), F32)
+
+        def act_back(b):
+            rr = rows_at(128 * b, 128)
+            pool[rows_at(512, 128), :] = nn(gff[rr, :], w[id_])
+
+            def one(r, total):
+                r2 = rows_at(128 * b + 16 * r, 16)
+                v = pre[r2, :]
+                inner = 0.7978845608028654 * (v + 0.044715 * (v * v * v))
+                th = jnp.tanh(inner)
+                mixed[r2, :] = (0.5 * v * (1.0 + th)).astype(BF16)
+                slope = 0.5 * (1.0 + th) + 0.5 * v * (1.0 - th * th) * (
+                    0.7978845608028654 * (1.0 + 0.134145 * (v * v))
+                )
+                gp = (pool[rows_at(512 + 16 * r, 16), :] * slope).astype(BF16)
+                gpre[r2, :] = gp
+                return total + fold(gp.astype(F32))
+
+            total = lax.fori_loop(0, 8, one, zero8)
+            sm[layer, 9:10, :] = sm[layer, 9:10, :] + jnp.sum(total, axis=0, keepdims=True)
+
+        gather_tensor(gff, 1, layer, act_back)
+
+        @pl.when(layer == 1)
+        def _():
+            keep(2, k_pre, pre).start()
+
+        @pl.when(layer == 0)
+        def _():
+            g2(5, 2)
+            keep(1, k_ff, ffall).wait()
+
+        def ffin_back(b):
+            return nt(gpre[rows_at(128 * b, 128), :], w[iu])
+
+        def beside1():
+            def one_d(i, inner):
+                cols = pl.ds(pl.multiple_of(128 * i, 128), 128)
+                w[id_, rows_at(128 * i, 128), :] = tn(gff[:, cols], mixed[0:512, :]).astype(BF16)
+                return inner
+
+            lax.fori_loop(0, 9, one_d, 0)
+            g0(id_, 2)
+            keep(0, k_mixed.at[layer], mixed).start()
+
+            def one_u(i, inner):
+                cols = pl.ds(pl.multiple_of(128 * i, 128), 128)
+                w[iu, rows_at(128 * i, 128), :] = tn(ffall[:, cols], gpre[...]).astype(BF16)
+                return inner
+
+            lax.fori_loop(0, 9, one_u, 0)
+            g0(iu, 1 + 2 * layer)
+
+            @pl.when(layer == 1)
+            def _():
+                keep(1, k_ff, ffall).start()
+
+        total1 = reduce_tensor(2, layer, ffin_back, beside1)
+
+        @pl.when(layer == 0)
+        def _():
+            g1(3, 0)
+
+        def mid(r, sums):
+            rr = rows_at(16 * r, 16)
+            gf = total1(rr, r)
+            n = own[1, rr, :]
+            e = gf * (1.0 + mrow(layer, 4))
+            iv = inv[layer, 1, rr, 0:1]
+            ga = hb[rr, :] + iv * (
+                e
+                - jnp.mean(e, axis=-1, keepdims=True)
+                - n * jnp.mean(e * n, axis=-1, keepdims=True)
+            )
+            hb[rr, :] = ga
+            gbv = (mrow(layer, 2) * ga).astype(BF16)
+            gb[rows_at(128 * t + 16 * r, 16), :] = gbv
+            return (
+                sums[0] + fold(gf),
+                sums[1] + fold(gf * n),
+                sums[2] + fold(ga * own[2, rr, :]),
+                sums[3] + fold(gbv.astype(F32)),
+            )
+
+        s_shift2, s_scale2, s_gate1, s_bproj = lax.fori_loop(
+            0, 8, mid, (zero8, zero8, zero8, zero8)
+        )
+        put_sum(layer, 3, s_shift2)
+        put_sum(layer, 4, s_scale2)
+        put_sum(layer, 2, s_gate1)
+        put_sum(layer, 6, s_bproj)
+
+        def att_back(b):
+            rr = rows_at(128 * b, 128)
+            v = nn(gb[rr, :], w[ia, :, 768:1152])
+            dqkv[rr, 0:384] = pltpu.roll(v, 320, 1).astype(BF16)
+
+        gather_tensor(gb, 2, layer, att_back)
+
+        @pl.when(layer == 0)
+        def _():
+            g2(4, 3)
+
+        dkv[...] = jnp.zeros_like(dkv)
+        ot[...] = jnp.zeros_like(ot)
+
+        def head(j, inner):
+            p = j // 2
+            h = j - 2 * p
+            win = pl.ds(pl.multiple_of(128 * p, 128), 256)
+            vwin = pl.ds(pl.multiple_of(256 + 128 * p, 128), 256)
+            lo = 16 * p + 72 * h
+            qm = jnp.where(head_mask(lo, 512), qa[layer, :, win].astype(F32), 0.0).astype(BF16)
+            dm = jnp.where(head_mask(32 + lo, 512), dqkv[0:512, win].astype(F32), 0.0).astype(BF16)
+            pb[0:512, 0:256] = qm
+            pb[0:512, 256:512] = dm
+            log_row = lse[layer, j, 0:1, :]
+
+            def first(kb, d8):
+                rr = rows_at(256 * kb, 256)
+                s = nt(qkv[layer, rr, win], pb[0:512, 0:256]) * scale
+                pr = jnp.exp(s - log_row)
+                dp = nt(qkv[layer, rr, vwin], pb[0:512, 256:512])
+                pool[rr, 0:512] = pr
+                pool[rr, 512:1024] = dp
+                dkv[rr, vwin] = dkv[rr, vwin] + nn(pr.astype(BF16), pb[0:512, 256:512])
+                return d8 + fold(pr * dp)
+
+            d8 = lax.fori_loop(0, 4, first, jnp.zeros((8, 512), F32))
+            delta = jnp.sum(d8, axis=0, keepdims=True)
+
+            def second(kb, inner2):
+                rr = rows_at(256 * kb, 256)
+                ds = (pool[rr, 0:512] * (pool[rr, 512:1024] - delta)).astype(BF16)
+                pb[rows_at(512 + 256 * kb, 256), :] = ds
+                dkv[rr, win] = dkv[rr, win] + nn(ds, pb[0:512, 0:256]) * scale
+                return inner2
+
+            lax.fori_loop(0, 4, second, 0)
+            otw[...] = tn(qkv[layer, :, win], pb[512:1536, :]) * scale
+            ot[pl.ds(pl.multiple_of(64 + 72 * j, 8), 72), :] = otw[
+                pl.ds(pl.multiple_of(lo, 8), 72), :
+            ]
+            return inner
+
+        lax.fori_loop(0, 4, head, 0)
+
+        def put_kv(b, total):
+            rr = rows_at(128 * b, 128)
+            kv = dkv[rr, :].astype(BF16)
+            dqkv[rr, 0:640] = kv
+            dqkv[rr, 640:896] = jnp.zeros((128, 256), BF16)
+            return total + fold(kv.astype(F32))
+
+        s_kv = lax.fori_loop(0, 8, put_kv, jnp.zeros((8, 640), F32))
+
+        def put_q(b, total):
+            rr = rows_at(512 * c + 128 * b, 128)
+            dq = ot[:, pl.ds(pl.multiple_of(128 * b, 128), 128)].T.astype(BF16).astype(F32)
+            dqkv[rr, 512:640] = (dkv[rr, 512:640] + dq[:, 0:128]).astype(BF16)
+            dqkv[rr, 640:896] = dq[:, 128:384].astype(BF16)
+            return total + fold(dq)
+
+        s_q = lax.fori_loop(0, 4, put_q, jnp.zeros((8, 384), F32))
+        sm[layer, 8:9, :] = jnp.zeros((1, D), F32)
+        sm[layer, 8:9, 0:640] = jnp.sum(s_kv, axis=0, keepdims=True)
+        sm[layer, 8:9, 512:896] = sm[layer, 8:9, 512:896] + jnp.sum(s_q, axis=0, keepdims=True)
+        g1(id_, 2)
+
+        @pl.when(layer == 0)
+        def _():
+            g2(3, 0)
+
+        def mix_back(block):
+            return nt(dqkv[pool_rows(block), :], w[ia, :, 0:896])
+
+        def beside2():
+            keep(0, k_mixed.at[layer], mixed).wait()
+
+            def one(i, inner):
+                cols = pl.ds(pl.multiple_of(128 * i, 128), 128)
+                rr = rows_at(128 * i, 128)
+                w[ia, rr, 0:640] = tn(mixed[:, cols], dqkv[:, 0:640]).astype(BF16)
+                here = rows_at(512 * c, 512)
+                r2 = tn(mixed[here, cols], dqkv[here, 640:896])
+                r3 = tn(gb[:, cols], att[layer])
+                w[ia, rr, 640:768] = r2[:, 0:128].astype(BF16)
+                w[ia, rr, 768:896] = (r2[:, 128:256] + r3[:, 0:128]).astype(BF16)
+                w[ia, rr, 896:1152] = r3[:, 128:384].astype(BF16)
+                return inner
+
+            lax.fori_loop(0, 9, one, 0)
+            g0(ia, 0)
+            g1(iu, 1 + 2 * layer)
+
+
+        total2 = reduce_plane(layer, mix_back, beside2)
+
+        def last(r, sums):
+            rr = rows_at(16 * r, 16)
+            gm = total2(rr, r)
+            n = own[0, rr, :]
+            e = gm * (1.0 + mrow(layer, 1))
+            iv = inv[layer, 0, rr, 0:1]
+            hb[rr, :] = hb[rr, :] + iv * (
+                e
+                - jnp.mean(e, axis=-1, keepdims=True)
+                - n * jnp.mean(e * n, axis=-1, keepdims=True)
+            )
+            return (sums[0] + fold(gm), sums[1] + fold(gm * n))
+
+        s_shift1, s_scale1 = lax.fori_loop(0, 8, last, (zero8, zero8))
+        put_sum(layer, 0, s_shift1)
+        put_sum(layer, 1, s_scale1)
+
+        @pl.when(layer == 1)
+        def _():
+            keep(3, k_own, own).start()
+
+        return carry
+
+    sm[...] = jnp.zeros_like(sm)
+    lax.fori_loop(0, LAYERS, backward, 0)
+    small(1)
+    small(0)
+    g2(2, 2)
+    g1(0, 0)
+    g2(1, 1)
+    small_end(1)
+    small_end(0)
+    g2(0, 0)
+    for i in range(6):
+        g3(i)
+
+
+def run_stage(zs_n, x_in, cot, modin, bias, blocks):
+    vm = pl.BlockSpec(memory_space=pltpu.VMEM)
+    anyspace = pl.BlockSpec(memory_space=pl.ANY)
+    dma = pltpu.SemaphoreType.DMA
+    sds = jax.ShapeDtypeStruct
+    scratch = [
+        pltpu.VMEM((6, D, D), BF16),
+        pltpu.VMEM((1024, D), BF16),
+        pltpu.VMEM((2, 1024, 896), BF16),
+        pltpu.VMEM((2, 512, 384), BF16),
+        pltpu.VMEM((2, 512, 384), BF16),
+        pltpu.VMEM((512, D), BF16),
+        pltpu.VMEM((512, D), F32),
+        pltpu.VMEM((4, 128, D), F32),
+        pltpu.VMEM((2, 2, 128, 128), F32),
+        pltpu.VMEM((2, 4, 8, 512), F32),
+        pltpu.VMEM((zs_n, 16, 384), F32),
+        pltpu.VMEM((2, 8, D), F32),
+        pltpu.VMEM((128, D), F32),
+        pltpu.VMEM((1024, D), F32),
+        pltpu.VMEM((4, 128, D), F32),
+        pltpu.VMEM((128, D), BF16),
+        pltpu.VMEM((128, D), BF16),
+        pltpu.VMEM((128, D), BF16),
+        pltpu.VMEM((128, D), BF16),
+        pltpu.VMEM((128, D), BF16),
+        pltpu.VMEM((128, D), BF16),
+        pltpu.VMEM((512, D), BF16),
+        pltpu.VMEM((512, D), BF16),
+        pltpu.VMEM((512, D), BF16),
+        pltpu.VMEM((1024, 896), BF16),
+        pltpu.VMEM((1024, 640), F32),
+        pltpu.VMEM((1536, 512), BF16),
+        pltpu.VMEM((256, 512), F32),
+        pltpu.VMEM((384, 512), F32),
+        pltpu.VMEM((4, zs_n, 144, D), BF16),
+        pltpu.VMEM((6, zs_n - 1, 144, D), BF16),
+        pltpu.VMEM((2, 16, D), F32),
+        pltpu.VMEM((2, 3, 16, D), F32),
+        dma((zs_n - 1,)),
+        dma((zs_n,)),
+        dma((6, zs_n)),
+        dma((6, zs_n)),
+        dma((6, zs_n)),
+        dma((6, zs_n)),
+        dma((6,)),
+        dma((2, 13)),
+        dma((2, 13)),
+        dma((3, 2, 5)),
+        dma((3, 2, 5)),
+        dma((3, 2, 3)),
+        dma((3, 2, 3)),
+        dma((2, 8)),
+        dma((2, 8)),
+        dma((6, zs_n)),
+        dma((6, zs_n)),
+        dma((6, zs_n)),
+        dma((6, zs_n)),
+        dma((6,)),
+        dma((6,)),
+        dma((6,)),
+        dma((2, 3 + zs_n)),
+        dma((2, 3 + zs_n)),
+        dma((4,)),
+    ]
+    return pl.pallas_call(
+        functools.partial(stage_kernel, zs_n),
+        name="two_blocks",
+        out_shape=(
+            sds((128, D), BF16),
+            sds((128, D), F32),
+            sds((6, 288, D), BF16),
+            sds((2, zs_n, 16, D), F32),
+            sds((2, 1024, D), BF16),
+            sds((512, D), BF16),
+            sds((512, D), F32),
+            sds((4, 128, D), F32),
+        ),
+        in_specs=[vm, vm, vm, vm, anyspace],
+        out_specs=(vm, vm, anyspace, vm, anyspace, anyspace, anyspace, anyspace),
+        scratch_shapes=scratch,
+        compiler_params=pltpu.CompilerParams(
+            collective_id=0, has_side_effects=True, vmem_limit_bytes=67043328
+        ),
+    )(x_in, cot, modin, bias, blocks)
+
+
+def fast_body(
+    zs_n,
+    x_in,
+    cond,
+    w_ada,
+    b_ada,
+    w_qkv,
+    b_qv,
+    w_proj,
+    b_proj,
+    up_weight,
+    up_bias_vector,
+    down_weight,
+    down_bias_vector,
+    cotangent,
+):
+    z = lax.axis_index("shard")
+    cols = w_ada.shape[3]
+    heads = w_qkv.shape[3]
+    cond_low = jax.nn.silu(cond).astype(BF16)
+    mod_terms = (
+        jnp.einsum("sd,ldkc->lskc", cond_low, w_ada, preferred_element_type=F32)
+        + b_ada.astype(F32)[:, None]
+    ).astype(BF16)
+    modin = jnp.pad(
+        mod_terms.astype(F32).transpose(1, 0, 2, 3), ((0, 0), (0, 0), (0, 2), (0, 384 - cols))
+    ).reshape(zs_n, 16, 384)
+    parts = []
+    for layer in range(LAYERS):
+        parts.append(
+            jnp.concatenate(
+                (
+                    w_qkv[layer, 1],
+                    w_qkv[layer, 2],
+                    w_qkv[layer, 0],
+                    w_proj[layer].T,
+                ),
+                axis=1,
+            )
+        )
+        parts.append(up_weight[layer])
+        parts.append(down_weight[layer].T)
+    blocks = jnp.stack(parts)
+    zero = jnp.zeros((LAYERS, heads), F32)
+    b_qkv = jnp.concatenate(
+        (zero, b_qv[:, 1].astype(F32), b_qv[:, 0].astype(F32), zero), axis=1
+    )
+    bias = jnp.stack(
+        (b_qkv, b_proj.astype(F32), up_bias_vector.astype(F32), down_bias_vector.astype(F32)),
+        axis=1,
+    )
+    out, grad_in, gw, small = run_stage(
+        zs_n, x_in[:, 0], cotangent[:, 0], modin, bias, blocks
+    )[:4]
+    grad_mod = small[:, :, 0:6, :].astype(BF16)
+    mod_cols = lax.dynamic_slice_in_dim(grad_mod, z * cols, cols, 3)
+    grad_w_ada = jnp.einsum("sd,lskc->ldkc", cond_low, mod_cols, preferred_element_type=F32)
+    grad_b_ada = jnp.sum(mod_cols.astype(F32), axis=1)
+    cond_part = jnp.einsum("lskc,ldkc->sd", mod_cols, w_ada, preferred_element_type=F32)
+    cond_total = lax.psum(cond_part, "shard")
+    silu_value, silu_back = jax.vjp(jax.nn.silu, cond)
+    grad_cond = silu_back(cond_total)[0]
+    sums = jnp.sum(small[:, :, 6:10, :], axis=1)
+    gw = gw.reshape(LAYERS, 3, cols, D).astype(F32)
+    ga = gw[:, 0]
+    return (
+        out[:, None],
+        grad_in[:, None],
+        grad_cond,
+        grad_w_ada,
+        grad_b_ada,
+        jnp.stack(
+            (ga[:, :, 2 * heads : 3 * heads], ga[:, :, 0:heads], ga[:, :, heads : 2 * heads]),
+            axis=1,
+        ),
+        jnp.stack((sums[:, 2, 2 * heads : 3 * heads], sums[:, 2, heads : 2 * heads]), axis=1),
+        ga[:, :, 3 * heads :].transpose(0, 2, 1),
+        sums[:, 0],
+        gw[:, 1],
+        sums[:, 3],
+        gw[:, 2].transpose(0, 2, 1),
+        sums[:, 1],
+    )
+
+
 def solution(mesh):
+    shape = mesh.shape
+    program = body
+    if shape["context"] == 2 and shape["tensor"] == 4 and shape["shard"] == 4:
+        program = functools.partial(fast_body, shape["shard"])
     return jax.shard_map(
-        body,
+        program,
         mesh=mesh,
         in_specs=(
             P(("context", "tensor"), "shard", None),

time: 1620 us -> 631 us (0.39)
  waiting for transfers between devices: 984 us -> 0 us
  Pallas kernels: 0 us -> 539 us
  blocking collectives: 305 us -> 32.2 us
  matrix products: 155 us -> 18.5 us
  other arithmetic: 67.3 us -> 6.6 us
  local copies, waits for them, and re-layouts: 79.4 us -> 32.7 us
    pallas_call x0 -> x1, Pallas kernels: none -> 539 us  [run_stage(): pl.pallas_call(functools.partial(stage_kernel, zs_n), name='two_blocks',...]
    psum x1 -> x0, waiting for transfers between devices: 382 us -> none  [body(): lax.psum(grad_w_qkv.astype(jnp.bfloat16), ('shard', 'context'))]
    all_gather x14 -> x0, waiting for transfers between devices: 354 us -> none  [the longest x2 109 us: fetch_weights(): lax.all_gather(down_part, 'shard', axis=2, tiled=True)]
    reduce_scatter x12 -> x0, waiting for transfers between devices: 245 us -> none  [the longest x2 63 us: layer_forward(): lax.psum_scatter(jnp.einsum('tbe,ed->tbd', row_block, full_proj, preferre...]
    all_gather x8 -> x0, blocking collectives: 216 us -> none  [the longest x2 94.4 us: fetch_weights(): lax.all_gather(proj_part, 'shard', axis=2, tiled=True)]
    dot_general x85 -> x3, matrix products: 155 us -> 18.5 us  [the longest x1 8.16 us: fast_body(): jnp.einsum('sd,lskc->ldkc', cond_low, mod_cols, preferred_element_type=F32)]
    psum x2 -> x1, blocking collectives: 89.3 us -> 32.2 us  [fast_body(): cond_total = lax.psum(cond_part, 'shard')]
    reduce_sum x31 -> x2, other arithmetic: 25.1 us -> 1.21 us  [the longest x1 1.12 us: fast_body(): sums = jnp.sum(small[:, :, 6:10, :], axis=1)]
  transfers between devices with their start and end apart: 27 -> 0, of which waited for: 24 -> 0; matrix products, arithmetic and copies ran while one was open for 8% -> 0% of each run, Pallas kernels for 0% -> 0%
where the time goes in v1:
time: 631 us; the launch traced here: 630 us
  Pallas kernels  539 us (85%)
  local copies, waits for them, and re-layouts  32.7 us (5%)
  blocking collectives  32.2 us (5%)
  matrix products  18.5 us (3%)
  other arithmetic  6.6 us (1%)
    pallas_call x1, Pallas kernels, run_stage(): pl.pallas_call(functools.partial(stage_kernel, zs_n), name='two_blocks',...  539 us
    psum x1, blocking collectives, fast_body(): cond_total = lax.psum(cond_part, 'shard')  32.2 us
    unnamed x33, local copies, waits for them, and re-layouts  16.3 us

profile of v1, /device:TPU:0, one launch (start us, length us, event | category | flops | bytes accessed | tf_op | source)
XLA Modules:
  0.0 630.2 jit_solution(7412083617984460162)
XLA Ops:
  0.6 0.8 fusion.21
  1.4 0.1 concatenate.9
  1.6 0.7 reshape.45
  2.3 0.7 reshape.46
  2.9 0.7 reshape.47
  3.6 0.7 pad_maximum_fusion.1.bias_ref
  4.3 0.7 copy.56
  5.0 6.0 fusion.14
  11.0 0.7 bitcast_convert_fusion.modin_ref
  11.7 0.0 copy-start.1
  11.7 0.2 copy.79
  11.9 0.2 copy.78
  12.1 1.0 slice_bitcast_fusion.6
  13.1 1.5 concatenate.11
  14.6 1.4 concatenate.10
  16.0 0.0 copy-start.2
  16.0 0.9 bitcast_dynamic-update-slice_fusion.3
  16.9 0.9 slice_dynamic-update-slice_fusion.1
  17.8 2.0 bitcast_dynamic-update-slice_fusion.1
  19.7 0.9 bitcast_dynamic-update-slice_fusion.2
  20.6 0.9 slice_dynamic-update-slice_fusion
  21.5 0.9 bitcast_dynamic-update-slice_fusion.s_ref
  22.4 539.4 %two_blocks.1 = (bf16[128,1152]{1,0:T(8,128)(2,1)}, f32[128,1152]{1,0:T(8,128)}, bf16[6,288,1152]{2,1,0:T(8,128)(2,1)}, f32[2,4,16,1152]{3,2,1,0:T(8,128)}, bf16...) custom-call(bf16[128,1152]{1,0:T(8,128)(2,1)} %bitcast.101, ...), custom_call_target="tpu_custom_call" | custom-call | tf_op jit(solution)/shard_map/two_blocks/pallas_call | solution.py:1520
  561.8 2.5 copy.68
  564.3 1.1 slice_reduce_fusion
  565.4 1.0 slice.113
  566.4 0.1 convert_reduce_fusion
  566.5 0.0 copy-start.4
  566.5 0.6 copy.69
  567.1 0.1 fusion.20
  567.2 0.6 copy.103
  567.8 0.6 pad_maximum_fusion.2
  568.4 0.6 copy.104
  569.1 0.6 copy.105
  569.7 4.4 fusion.2
  574.1 32.2 %psum.7 = f32[4,1152]{1,0:T(4,128)S(1)} all-reduce(f32[4,1152]{1,0:T(4,128)S(1)} %fusion.2), channel_id=1, replica_groups=mesh['shard'=4,'context'=2,'tensor'=4] {'shard'}, use_global_device_ids=true, to_apply=%region_0.1 | all-reduce | flops 4608 | bytes 36864 | tf_op jit(solution)/shard_map/psum | solution.py:1601
  606.2 0.6 fusion.9
  606.9 3.0 slice.114
  609.9 2.4 copy.80
  612.3 1.1 slice_bitcast_fusion.2
  613.4 0.2 pad_maximum_fusion
  613.6 2.3 copy.70
  615.9 2.6 convert.13
  618.6 0.0 copy-start.5
  618.6 0.0 copy-start.8
  618.6 2.7 slice_bitcast_fusion
  621.3 8.2 %convolution_bitcast_fusion = f32[2,1152,6,288]{1,3,2,0:T(8,128)} fusion(bf16[2,4,6,288]{3,2,1,0:T(8,128)(2,1)S(1)} %copy-done.5, f32[4,1152]{1,0:T(4,128)S(1)} %copy-done.8), kind=kOutput, calls=%fused_computation | convolution fusion | flops 31873536 | bytes 15971328 | tf_op jit(solution)/shard_map/sd,lskc->ldkc/dot_general | solution.py:1598
  629.5 0.7 copy.112
  (19 shorter events, 0.1 us)
Async XLA Ops:
  5.0 6.6 %copy-start.3 = (bf16[2,288,288]{2,1,0:T(8,128)(2,1)S(1)}, bf16[2,288,288]{2,1,0:T(8,128)(2,1)}, u32[]{:S(2)}) copy-start(bf16[2,288,288]{2,1,0:T(8,128)(2,1)} %param.19) | copy-start | bytes 995332
  5.0 7.1 %copy-start = (bf16[2,3,288,288]{3,2,1,0:T(8,128)(2,1)S(1)}, bf16[2,3,288,288]{3,2,1,0:T(8,128)(2,1)}, u32[]{:S(2)}) copy-start(bf16[2,3,288,288]{3,2,1,0:T(8,128)(2,1)} %param.17) | copy-start | bytes 2985988
  11.7 5.2 copy-start.1
  16.0 5.6 copy-start.2
  566.5 3.2 copy-start.4
  569.7 36.6 %copy-start.7 = (f32[4,1152]{1,0:T(4,128)S(1)}, f32[4,1152]{1,0:T(4,128)}, u32[]{:S(2)}) copy-start(f32[4,1152]{1,0:T(4,128)} %param.14) | copy-start | bytes 55300
  618.6 2.7 copy-start.5
  618.6 2.7 copy-start.8
  621.3 8.2 %copy-start.6 = (bf16[128,1152]{1,0:T(8,128)(2,1)S(1)}, bf16[128,1152]{1,0:T(8,128)(2,1)}, u32[]{:S(2)}) copy-start(bf16[128,1152]{1,0:T(8,128)(2,1)} %get-tuple-element.17) | copy-start | bytes 884740

commit v2 on v1

--- a/solution.py
+++ b/solution.py
@@ -445,15 +445,13 @@
     cot_ref,
     modin_ref,
     bias_ref,
-    s_ref,
+    sa_ref,
+    su_ref,
+    sd_ref,
     out_ref,
     gin_ref,
     gw_ref,
     small_ref,
-    k_mixed,
-    k_ff,
-    k_pre,
-    k_own,
     w,
     mixed,
     qkv,
@@ -461,6 +459,7 @@
     att,
     ffall,
     pre,
+    act,
     own,
     inv,
     lse,
@@ -478,12 +477,12 @@
     gff,
     gpre,
     gb,
+    doa,
     dqkv,
     dkv,
     pb,
     otw,
     ot,
-    rx,
     rz,
     sm,
     smr,
@@ -491,19 +490,11 @@
     m_r,
     wz_s,
     wz_r,
-    wx_s,
-    wx_r,
     w_l,
     ap_s,
     ap_r,
-    at_s,
-    at_r,
-    rt_s,
-    rt_r,
     rp_s,
     rp_r,
-    gx_s,
-    gx_r,
     gz_s,
     gz_r,
     gf_s,
@@ -511,7 +502,6 @@
     g_l,
     sm_s,
     sm_r,
-    k_s,
 ):
     z = lax.axis_index("shard")
     c = lax.axis_index("context")
@@ -544,42 +534,74 @@
     for d, zz in enumerate(zo):
         mod_copy(d, zz, z).start()
 
-    half = 144
-
-    def w_rows(zz, cc):
-        return rows_at(288 * zz + half * cc, half)
-
-    def w0(i):
-        pltpu.make_async_copy(s_ref.at[i], w.at[i, rows_at(288 * z, 288)], w_l.at[i]).start()
-        for d, zz in enumerate(zo):
-            rc(
-                s_ref.at[i, rows_at(half * c, half)],
-                w.at[i, w_rows(z, c)],
-                wz_s.at[i, d],
-                wz_r.at[i, z],
-                (zz, c, t),
-            ).start()
-
-    def w1(i):
-        for d, zz in enumerate(zo):
-            part = w.at[i, w_rows(zz, c)]
-            rc(part, part, wz_s.at[i, d], wz_r.at[i, zz], dev_x).wait_recv()
-            rc(part, part, wx_s.at[i, d], wx_r.at[i, d], dev_x).start()
+    shards = (sa_ref, su_ref, sd_ref)
+    z_far = z + 2 - 4 * (z // 2)
+    z_end = 3 * (z // 2)
+    is_mid = (z == 1) | (z == 2)
+
+    def w_rows(zz):
+        return rows_at(288 * zz, 288)
+
+    def w_send(layer, m, slot, zz):
+        i = 3 * layer + m
+        return rc(
+            shards[m].at[layer], w.at[i, w_rows(z)], wz_s.at[i, slot], wz_r.at[i, z], (zz, c, t)
+        )
+
+    def w_local(layer, m):
+        i = 3 * layer + m
+        return pltpu.make_async_copy(shards[m].at[layer], w.at[i, w_rows(z)], w_l.at[i])
+
+    def w0(layer, m):
+        w_local(layer, m).start()
+        w_send(layer, m, 0, z_far).start()
+
+        @pl.when(z < zs_n - 1)
+        def _():
+            w_send(layer, m, 1, z + 1).start()
+
+        @pl.when(z > 0)
+        def _():
+            w_send(layer, m, 2, z - 1).start()
+
+    def w_take(i, zz):
+        part = w.at[i, w_rows(zz)]
+        return rc(part, part, wz_s.at[i, 3], wz_r.at[i, zz], (z_end, c, t))
+
+    def relay(i):
+        @pl.when(is_mid)
+        def _():
+            w_take(i, z_far).wait_recv()
+            w_take(i, z_far).start()
 
     def w2(i):
-        for d, zz in enumerate(zo):
-            part = w.at[i, w_rows(zz, 1 - c)]
-            rc(part, part, wx_s.at[i, d], wx_r.at[i, d], dev_x).wait_recv()
-        pltpu.make_async_copy(s_ref.at[i], w.at[i, rows_at(288 * z, 288)], w_l.at[i]).wait()
-
-    def w_drain(i):
-        for d, zz in enumerate(zo):
-            part = w.at[i, w_rows(zz, c)]
-            rc(part, part, wz_s.at[i, d], wz_r.at[i, zz], dev_x).wait_send()
-            rc(part, part, wx_s.at[i, d], wx_r.at[i, d], dev_x).wait_send()
-
-    for i in range(6):
-        w0(i)
+        for zz in zo:
+
+            @pl.when(jnp.logical_not(is_mid & (zz == z_far)))
+            def _():
+                w_take(i, zz).wait_recv()
+
+        part = w.at[i, w_rows(z)]
+        pltpu.make_async_copy(part, part, w_l.at[i]).wait()
+
+    def w_drain(layer, m):
+        w_send(layer, m, 0, z_far).wait_send()
+
+        @pl.when(z < zs_n - 1)
+        def _():
+            w_send(layer, m, 1, z + 1).wait_send()
+
+        @pl.when(z > 0)
+        def _():
+            w_send(layer, m, 2, z - 1).wait_send()
+
+        @pl.when(is_mid)
+        def _():
+            w_take(3 * layer + m, z_far).wait_send()
+
+    for layer in range(LAYERS):
+        for m in range(3):
+            w0(layer, m)
 
     modr[z] = modin_ref[z]
     for zz in zo:
@@ -593,11 +615,11 @@
     def mrow(layer, kind):
         return modv[layer, kind : kind + 1, :]
 
-    def ap_copy(layer, index, block, offset, size, dev):
-        part = mixed.at[rows_at(128 * block + offset, size)]
-        return rc(part, part, ap_s.at[layer, index], ap_r.at[layer, index], dev)
-
-    def ap_parts(layer):
+    def ap_copy(buf, phase, layer, index, block, offset, size, dev):
+        part = buf.at[rows_at(128 * block + offset, size)]
+        return rc(part, part, ap_s.at[phase, layer, index], ap_r.at[phase, layer, index], dev)
+
+    def ap_parts(buf, phase, layer):
         b_own, b_p = 4 * c + t, 4 * c + tp
         b_y, b_yp = 4 * c + t_far, 4 * c + tp_far
         b_x, b_xp = 4 * (1 - c) + t, 4 * (1 - c) + tp
@@ -636,19 +658,19 @@
         def send(index):
             for entry in sends:
                 if entry[0] == index:
-                    ap_copy(layer, *entry).start()
+                    ap_copy(buf, phase, layer, *entry).start()
 
         def wait(index):
-            ap_copy(layer, index, *recvs[index], dev_p).wait_recv()
+            ap_copy(buf, phase, layer, index, *recvs[index], dev_p).wait_recv()
 
         def drain():
             for entry in sends:
-                ap_copy(layer, *entry).wait_send()
+                ap_copy(buf, phase, layer, *entry).wait_send()
 
         return send, wait, drain
 
-    def gather_plane(layer, compute):
-        send, wait, drain = ap_parts(layer)
+    def gather_plane(buf, phase, layer, compute):
+        send, wait, drain = ap_parts(buf, phase, layer)
         for index in (0, 1, 4, 2, 3):
             send(index)
 
@@ -703,112 +725,23 @@
         lax.fori_loop(0, 8, step, 0)
         drain()
 
-    def gather_tensor(buf, phase, layer, compute):
-        def copy(index, block, offset, size, dev):
-            part = buf.at[rows_at(128 * block + offset, size)]
-            return rc(part, part, at_s.at[phase, layer, index], at_r.at[phase, layer, index], dev)
-
-        copy(0, t, 0, 128, dev_p).start()
-        copy(1, t, 0, 64, dev_y).start()
-        copy(2, t, 64, 64, dev_y).start()
-
-        def step(i, carry):
-            b0, b1 = lax.rem(i, 2), i // 2
-
-            @pl.when(i == 1)
-            def _():
-                copy(0, tp, 0, 128, dev_p).wait_recv()
-
-            @pl.when(i == 2)
-            def _():
-                copy(1, t_far, 0, 64, dev_y).wait_recv()
-                copy(3, t_far, 0, 64, dev_p).start()
-                copy(2, t_far, 64, 64, dev_y).wait_recv()
-                copy(4, t_far, 64, 64, dev_p).start()
-
-            @pl.when(i == 3)
-            def _():
-                copy(3, tp_far, 0, 64, dev_p).wait_recv()
-                copy(4, tp_far, 64, 64, dev_p).wait_recv()
-
-            compute(2 * lax.rem(y + b1, 2) + lax.rem(k + b0, 2))
-            return carry
-
-        lax.fori_loop(0, 4, step, 0)
-        copy(0, t, 0, 128, dev_p).wait_send()
-        copy(1, t, 0, 64, dev_y).wait_send()
-        copy(2, t, 64, 64, dev_y).wait_send()
-        copy(3, t_far, 0, 64, dev_p).wait_send()
-        copy(4, t_far, 64, 64, dev_p).wait_send()
-
     def pool_rows(i):
         return rows_at(128 * i, 128)
 
-    def reduce_tensor(phase, layer, compute, beside):
+    def reduce_plane(phase, layer, compute, beside):
         def to_p(i, slot):
             return rc(
                 pool.at[pool_rows(i)],
                 ra.at[slot],
-                rt_s.at[phase, layer, slot],
-                rt_r.at[phase, layer, slot],
+                rp_s.at[phase, layer, slot],
+                rp_r.at[phase, layer, slot],
                 dev_p,
             )
 
-        to_y = rc(ysend, yrecv, rt_s.at[phase, layer, 2], rt_r.at[phase, layer, 2], dev_y)
-
-        def step(i, carry):
-            b0, b1 = 1 - lax.rem(i, 2), 1 - i // 2
-            pool[pool_rows(i), :] = compute(2 * lax.rem(y + b1, 2) + lax.rem(k + b0, 2))
-
-            @pl.when(i == 0)
-            def _():
-                to_p(0, 0).start()
-
-            @pl.when(i == 1)
-            def _():
-                to_p(0, 0).wait_recv()
-
-                def add(r, inner):
-                    rr = rows_at(16 * r, 16)
-                    ysend[rr, :] = (pool[rows_at(128 + 16 * r, 16), :] + ra[0, rr, :]).astype(BF16)
-                    return inner
-
-                lax.fori_loop(0, 8, add, 0)
-                to_y.start()
-
-            @pl.when(i == 2)
-            def _():
-                to_p(2, 1).start()
-
-            return carry
-
-        lax.fori_loop(0, 4, step, 0)
-        beside()
-        to_p(2, 1).wait_recv()
-        to_y.wait_recv()
-        to_p(0, 0).wait_send()
-        to_p(2, 1).wait_send()
-        to_y.wait_send()
-
-        def total(rr, r):
-            return pool[rows_at(384 + 16 * r, 16), :] + ra[1, rr, :] + yrecv[rr, :].astype(F32)
-
-        return total
-
-    def reduce_plane(layer, compute, beside):
-        def to_p(i, slot):
-            return rc(
-                pool.at[pool_rows(i)],
-                ra.at[slot],
-                rp_s.at[layer, slot],
-                rp_r.at[layer, slot],
-                dev_p,
-            )
-
-        d_x = rc(dsend.at[0:64], drecv.at[0:64], rp_s.at[layer, 4], rp_r.at[layer, 4], dev_x)
-        d_y = rc(dsend.at[64:128], drecv.at[64:128], rp_s.at[layer, 5], rp_r.at[layer, 5], dev_y)
-        to_x = rc(xsend, xrecv, rp_s.at[layer, 6], rp_r.at[layer, 6], dev_x)
-        to_y = rc(ysend, yrecv, rp_s.at[layer, 7], rp_r.at[layer, 7], dev_y)
+        d_x = rc(dsend.at[0:64], drecv.at[0:64], rp_s.at[phase, layer, 4], rp_r.at[phase, layer, 4], dev_x)
+        d_y = rc(dsend.at[64:128], drecv.at[64:128], rp_s.at[phase, layer, 5], rp_r.at[phase, layer, 5], dev_y)
+        to_x = rc(xsend, xrecv, rp_s.at[phase, layer, 6], rp_r.at[phase, layer, 6], dev_x)
+        to_y = rc(ysend, yrecv, rp_s.at[phase, layer, 7], rp_r.at[phase, layer, 7], dev_y)
 
         def step(i, carry):
             q = i // 2
@@ -899,76 +832,76 @@
         r = lax.rsqrt(jnp.mean(center * center, axis=-1, keepdims=True) + epsilon)
         return center * r, r
 
-    def keep(slot, src, dst):
-        return pltpu.make_async_copy(src, dst, k_s.at[slot])
-
-    def kept():
-        return [(1, ffall, k_ff), (2, pre, k_pre), (3, own, k_own)]
-
-    def head_mask(lo, rows):
-        lane = lax.broadcasted_iota(jnp.int32, (rows, 256), 1)
+    def head_mask(lo):
+        lane = lax.broadcasted_iota(jnp.int32, (512, 256), 1)
         return (lane >= lo) & (lane < lo + HD)
+
+    own_block = 4 * c + t
+
+    def own_rows(r):
+        return rows_at(128 * own_block + 16 * r, 16)
+
+    def cols128(b):
+        return pl.ds(pl.multiple_of(128 * b, 128), 128)
 
     def forward(layer, carry):
         ia, iu, id_ = 3 * layer, 3 * layer + 1, 3 * layer + 2
-        own_block = 4 * c + t
 
         def ln1(r, inner):
             rr = rows_at(16 * r, 16)
             n, iv = layer_norm(hb[rr, :])
-            own[0, rr, :] = n
+            own[layer, 0, rr, :] = n
             inv[layer, 0, rr, :] = spread(iv)
-            mixed[rows_at(128 * own_block + 16 * r, 16), :] = (
-                n * (1.0 + mrow(layer, 1)) + mrow(layer, 0)
-            ).astype(BF16)
+            mixed[layer, own_rows(r), :] = (n * (1.0 + mrow(layer, 1)) + mrow(layer, 0)).astype(
+                BF16
+            )
             return inner
 
         lax.fori_loop(0, 8, ln1, 0)
-
-        @pl.when(layer == 0)
-        def _():
-            w1(0)
-            w2(0)
-
-        @pl.when(layer == 1)
-        def _():
-            w1(4)
-            w2(3)
 
         def project(block):
             rr = pool_rows(block)
             qkv[layer, rr, :] = (
-                nn(mixed[rr, :], w[ia, :, 0:896]) + bias_ref[layer, 0:1, 0:896]
+                nn(mixed[layer, rr, :], w[ia, :, 0:512]) + bias_ref[layer, 0:1, 0:512]
             ).astype(BF16)
-
-        gather_plane(layer, project)
 
         @pl.when(layer == 0)
         def _():
-            w1(1)
-
-        keep(0, mixed, k_mixed.at[layer]).start()
+            relay(0)
+            gather_plane(mixed.at[layer], 0, layer, lambda block: None)
+            w2(0)
+
+            def one(block, inner):
+                project(block)
+                return inner
+
+            lax.fori_loop(0, 8, one, 0)
+
+        @pl.when(layer > 0)
+        def _():
+            w2(ia)
+            gather_plane(mixed.at[layer], 0, layer, project)
 
         def take_q(b, inner):
-            v = qkv[layer, rows_at(512 * c + 128 * b, 128), 512:896].astype(F32)
-            qa[layer, rows_at(128 * b, 128), :] = pltpu.roll(v, 320, 1).astype(BF16)
+            rr = pool_rows(b)
+            v = qkv[layer, rr, 256:512].astype(F32)
+            qa[layer, rr, :] = pltpu.roll(v, 224, 1).astype(BF16)
             return inner
 
-        lax.fori_loop(0, 4, take_q, 0)
+        lax.fori_loop(0, 8, take_q, 0)
         ot[...] = jnp.zeros_like(ot)
 
         def head(j, inner):
-            p = j // 2
-            h = j - 2 * p
-            win = pl.ds(pl.multiple_of(128 * p, 128), 256)
-            vwin = pl.ds(pl.multiple_of(256 + 128 * p, 128), 256)
-            lo = 16 * p + 72 * h
-            qm = jnp.where(head_mask(lo, 512), qa[layer, :, win].astype(F32), 0.0).astype(BF16)
-            pb[0:512, 0:256] = qm
+            h = j // 2
+            qh = j - 2 * h
+            q_rows = rows_at(512 * qh, 512)
+            q_cols = pl.ds(pl.multiple_of(512 * qh, 512), 512)
+            qm = jnp.where(head_mask(72 * h), qa[layer, q_rows, :].astype(F32), 0.0)
+            pb[0:512, 0:256] = qm.astype(BF16)
 
             def scores(kb, m8):
                 rr = rows_at(256 * kb, 256)
-                s = nt(qkv[layer, rr, win], pb[0:512, 0:256]) * scale
+                s = nt(qkv[layer, rr, 0:256], pb[0:512, 0:256]) * scale
                 pool[rr, 0:512] = s
                 return jnp.maximum(m8, jnp.max(s.reshape(32, 8, 512), axis=0))
 
@@ -992,199 +925,142 @@
                 return inner2
 
             lax.fori_loop(0, 8, probs, 0)
-            otw[...] = tn(qkv[layer, :, vwin], pb[512:1536, :])
-            ot[pl.ds(pl.multiple_of(96 + 72 * j, 8), 72), :] = otw[
-                pl.ds(pl.multiple_of(32 + lo, 8), 72), :
+            otw[...] = tn(qkv[layer, :, 128:384], pb[512:1536, :])
+            ot[pl.ds(pl.multiple_of(48 + 72 * h, 8), 72), q_cols] = otw[
+                pl.ds(pl.multiple_of(16 + 72 * h, 8), 72), :
             ]
             return inner
 
         lax.fori_loop(0, 4, head, 0)
 
         def put_att(b, inner):
-            cols = ot[:, pl.ds(pl.multiple_of(128 * b, 128), 128)]
-            att[layer, rows_at(128 * b, 128), :] = cols.T.astype(BF16)
+            att[layer, pool_rows(b), :] = ot[:, cols128(b)].T.astype(BF16)
             return inner
 
-        lax.fori_loop(0, 4, put_att, 0)
-
-        @pl.when(layer == 0)
-        def _():
-            w1(2)
-
-        @pl.when(layer == 1)
-        def _():
-            w1(5)
+        lax.fori_loop(0, 8, put_att, 0)
+        relay(iu)
 
         def branch(b):
-            return nt(att[layer, rows_at(128 * b, 128), :], w[ia, :, 768:1152])
-
-        total1 = reduce_tensor(0, layer, branch, lambda: None)
+            return nt(att[layer, pool_rows(b), :], w[ia, :, 384:640])
+
+        total1 = reduce_plane(0, layer, branch, lambda: relay(id_))
 
         def ln2(r, inner):
             rr = rows_at(16 * r, 16)
             br = total1(rr, r) + bias_ref[layer, 1:2, :]
-            own[2, rr, :] = br
+            own[layer, 2, rr, :] = br
             v = hb[rr, :] + mrow(layer, 2) * br
             af[rr, :] = v
             n, iv = layer_norm(v)
-            own[1, rr, :] = n
+            own[layer, 1, rr, :] = n
             inv[layer, 1, rr, :] = spread(iv)
-            ffall[rows_at(128 * t + 16 * r, 16), :] = (
-                n * (1.0 + mrow(layer, 4)) + mrow(layer, 3)
-            ).astype(BF16)
+            ffall[layer, own_rows(r), :] = (n * (1.0 + mrow(layer, 4)) + mrow(layer, 3)).astype(
+                BF16
+            )
             return inner
 
         lax.fori_loop(0, 8, ln2, 0)
         w2(iu)
 
         def up(b):
-            rr = rows_at(128 * b, 128)
-            pre[rr, :] = nn(ffall[rr, :], w[iu]) + bias_ref[layer, 2:3, :]
+            rr = pool_rows(b)
+            pre[layer, rr, :] = nn(ffall[layer, rr, :], w[iu]) + bias_ref[layer, 2:3, 0:640]
 
             def gelu(r, inner):
                 r2 = rows_at(128 * b + 16 * r, 16)
-                gpre[r2, :] = jax.nn.gelu(pre[r2, :], approximate=True).astype(BF16)
+                act[r2, :] = jax.nn.gelu(pre[layer, r2, :], approximate=True).astype(BF16)
                 return inner
 
             lax.fori_loop(0, 8, gelu, 0)
 
-        gather_tensor(ffall, 0, layer, up)
+        gather_plane(ffall.at[layer], 1, layer, up)
         w2(id_)
 
-        @pl.when(layer == 0)
-        def _():
-            keep(1, ffall, k_ff).start()
-            keep(2, pre, k_pre).start()
-
         def down(b):
-            return nt(gpre[rows_at(128 * b, 128), :], w[id_])
+            return nt(act[pool_rows(b), :], w[id_])
 
         def beside():
-            @pl.when(layer == 0)
+            @pl.when(layer < LAYERS - 1)
             def _():
-                w1(3)
-
-        keep(0, mixed, k_mixed.at[layer]).wait()
-        total2 = reduce_tensor(1, layer, down, beside)
+                relay(id_ + 1)
+
+        total2 = reduce_plane(1, layer, down, beside)
 
         def finish(r, inner):
             rr = rows_at(16 * r, 16)
             fo = total2(rr, r) + bias_ref[layer, 3:4, :]
-            own[3, rr, :] = fo
+            own[layer, 3, rr, :] = fo
             hb[rr, :] = af[rr, :] + mrow(layer, 5) * fo
             return inner
 
         lax.fori_loop(0, 8, finish, 0)
-
-        @pl.when(layer == 0)
-        def _():
-            keep(3, own, k_own).start()
-            for slot, src, dst in kept():
-                keep(slot, src, dst).wait()
-
         return carry
 
     hb[...] = x_ref[...].astype(F32)
     lax.fori_loop(0, LAYERS, forward, 0)
     out_ref[...] = hb[...].astype(BF16)
-    for i in range(6):
-        w_drain(i)
+    for layer in range(LAYERS):
+        for m in range(3):
+            w_drain(layer, m)
     hb[...] = cot_ref[...].astype(F32)
 
-    def g_copy0(i, m, d, zz):
-        return rc(w.at[i, w_rows(zz, 1 - c)], rx.at[m, zz], gx_s.at[i, d], gx_r.at[i, zz], dev_x)
-
-    def g0(i, m):
-        for d, zz in enumerate(zo + [z]):
-            g_copy0(i, m, d, zz).start()
-
-    def g_copy1(i, d, zz):
-        return rc(w.at[i, w_rows(zz, c)], rz.at[i, d], gz_s.at[i, d], gz_r.at[i, d], (zz, c, t))
-
-    def g1(i, m):
-        for d, zz in enumerate(zo + [z]):
-            g_copy0(i, m, d, zz).wait_recv()
-
-            def add(r, inner):
-                rr = rows_at(288 * zz + half * c + 16 * r, 16)
-                w[i, rr, :] = (
-                    w[i, rr, :].astype(F32) + rx[m, zz, rows_at(16 * r, 16), :].astype(F32)
-                ).astype(BF16)
-                return inner
-
-            lax.fori_loop(0, 9, add, 0)
-            if d < zs_n - 1:
-                g_copy1(i, d, zz).start()
-
-    def g_copy2(i):
-        here = gw_ref.at[i, rows_at(half * c, half)]
-        return rc(w.at[i, w_rows(z, c)], here, gf_s.at[i], gf_r.at[i], dev_x)
-
-    def g_out(i):
-        here = gw_ref.at[i, rows_at(half * c, half)]
-        return pltpu.make_async_copy(w.at[i, w_rows(z, c)], here, g_l.at[i])
-
-    def g2(i, m):
-        for d in range(zs_n - 1):
+    def g_copy(i, d, zz):
+        return rc(w.at[i, w_rows(zz)], rz.at[i, d], gz_s.at[i, d], gz_r.at[i, d], (zz, c, t))
+
+    def g0(i):
+        for d, zz in enumerate(zo):
+            g_copy(i, d, zz).start()
+
+    def g_send(i):
+        return rc(w.at[i, w_rows(z)], gw_ref.at[i, c], gf_s.at[i], gf_r.at[i], dev_x)
+
+    def g_keep(i):
+        return pltpu.make_async_copy(w.at[i, w_rows(z)], gw_ref.at[i, c], g_l.at[i])
+
+    def g2(i):
+        for d, zz in enumerate(zo):
             rc(rz.at[i, d], rz.at[i, d], gz_s.at[i, d], gz_r.at[i, d], dev_x).wait_recv()
-        for d, zz in enumerate(zo + [z]):
-            g_copy0(i, m, d, zz).wait_send()
 
         def add(r, inner):
-            rr = rows_at(288 * z + half * c + 16 * r, 16)
+            rr = rows_at(288 * z + 16 * r, 16)
             total = w[i, rr, :].astype(F32)
             for d in range(zs_n - 1):
                 total = total + rz[i, d, rows_at(16 * r, 16), :].astype(F32)
             w[i, rr, :] = total.astype(BF16)
             return inner
 
-        lax.fori_loop(0, 9, add, 0)
-        g_copy2(i).start()
-        g_out(i).start()
+        lax.fori_loop(0, 18, add, 0)
+        g_send(i).start()
+        g_keep(i).start()
 
     def g3(i):
-        other = gw_ref.at[i, rows_at(half * (1 - c), half)]
+        other = gw_ref.at[i, 1 - c]
         rc(other, other, gf_s.at[i], gf_r.at[i], dev_x).wait_recv()
-        g_copy2(i).wait_send()
-        g_out(i).wait()
+        g_send(i).wait_send()
+        g_keep(i).wait()
         for d, zz in enumerate(zo):
-            g_copy1(i, d, zz).wait_send()
-
-    def sm_copy(layer, index, size, dev):
-        return rc(
-            sm.at[layer, 0:size],
-            smr.at[layer, index, 0:size],
-            sm_s.at[layer, index],
-            sm_r.at[layer, index],
-            dev,
-        )
-
-    def small(layer):
+            g_copy(i, d, zz).wait_send()
+
+    def small():
         for index, size, dev in ((0, 8, dev_p), (1, 8, dev_y), (2, 16, dev_x)):
-            step = sm_copy(layer, index, size, dev)
+            step = rc(
+                sm.at[:, 0:size],
+                smr.at[index, :, 0:size],
+                sm_s.at[index],
+                sm_r.at[index],
+                dev,
+            )
             step.start()
             step.wait_send()
             step.wait_recv()
-            sm[layer, 0:size, :] = sm[layer, 0:size, :] + smr[layer, index, 0:size, :]
-        small_ref[layer, z] = sm[layer]
+            sm[:, 0:size, :] = sm[:, 0:size, :] + smr[index, :, 0:size, :]
+        small_ref[z] = sm[...]
         for d, zz in enumerate(zo):
-            rc(
-                sm.at[layer],
-                small_ref.at[layer, z],
-                sm_s.at[layer, 3 + d],
-                sm_r.at[layer, 3 + z],
-                (zz, c, t),
-            ).start()
-
-    def small_end(layer):
+            rc(sm, small_ref.at[z], sm_s.at[3 + d], sm_r.at[3 + z], (zz, c, t)).start()
+
+    def small_end():
         for d, zz in enumerate(zo):
-            end = rc(
-                sm.at[layer],
-                small_ref.at[layer, zz],
-                sm_s.at[layer, 3 + d],
-                sm_r.at[layer, 3 + zz],
-                (zz, c, t),
-            )
+            end = rc(sm, small_ref.at[zz], sm_s.at[3 + d], sm_r.at[3 + zz], (zz, c, t))
             end.wait_recv()
             end.wait_send()
 
@@ -1192,98 +1068,72 @@
 
     def put_sum(layer, row, v8):
         sm[layer, row : row + 1, 0 : v8.shape[1]] = jnp.sum(v8, axis=0, keepdims=True)
+
+    def add_sum(layer, row, v8):
+        here = (layer, pl.ds(row, 1), slice(0, v8.shape[1]))
+        sm[here] = sm[here] + jnp.sum(v8, axis=0, keepdims=True)
 
     def backward(step_index, carry):
         layer = LAYERS - 1 - step_index
         ia, iu, id_ = 3 * layer, 3 * layer + 1, 3 * layer + 2
-
-        @pl.when(layer == 0)
-        def _():
-            keep(3, k_own, own).wait()
 
         def start(r, sums):
             rr = rows_at(16 * r, 16)
             g = hb[rr, :]
             gf = (mrow(layer, 5) * g).astype(BF16)
-            gff[rows_at(128 * t + 16 * r, 16), :] = gf
-            return (sums[0] + fold(g * own[3, rr, :]), sums[1] + fold(gf.astype(F32)))
+            gff[own_rows(r), :] = gf
+            return (sums[0] + fold(g * own[layer, 3, rr, :]), sums[1] + fold(gf.astype(F32)))
 
         s_gate2, s_bdown = lax.fori_loop(0, 8, start, (zero8, zero8))
         put_sum(layer, 5, s_gate2)
         put_sum(layer, 7, s_bdown)
 
-        @pl.when(layer == 0)
-        def _():
-            keep(2, k_pre, pre).wait()
-
-        sm[layer, 9:10, :] = jnp.zeros((1, D), F32)
-
         def act_back(b):
-            rr = rows_at(128 * b, 128)
-            pool[rows_at(512, 128), :] = nn(gff[rr, :], w[id_])
+            rr = pool_rows(b)
+            pool[rows_at(512, 128), 0:640] = nn(gff[rr, :], w[id_])
 
             def one(r, total):
                 r2 = rows_at(128 * b + 16 * r, 16)
-                v = pre[r2, :]
-                inner = 0.7978845608028654 * (v + 0.044715 * (v * v * v))
-                th = jnp.tanh(inner)
-                mixed[r2, :] = (0.5 * v * (1.0 + th)).astype(BF16)
+                v = pre[layer, r2, :]
+                th = jnp.tanh(0.7978845608028654 * (v + 0.044715 * (v * v * v)))
+                act[r2, :] = (0.5 * v * (1.0 + th)).astype(BF16)
                 slope = 0.5 * (1.0 + th) + 0.5 * v * (1.0 - th * th) * (
                     0.7978845608028654 * (1.0 + 0.134145 * (v * v))
                 )
-                gp = (pool[rows_at(512 + 16 * r, 16), :] * slope).astype(BF16)
+                gp = (pool[rows_at(512 + 16 * r, 16), 0:640] * slope).astype(BF16)
                 gpre[r2, :] = gp
                 return total + fold(gp.astype(F32))
 
-            total = lax.fori_loop(0, 8, one, zero8)
-            sm[layer, 9:10, :] = sm[layer, 9:10, :] + jnp.sum(total, axis=0, keepdims=True)
-
-        gather_tensor(gff, 1, layer, act_back)
-
-        @pl.when(layer == 1)
-        def _():
-            keep(2, k_pre, pre).start()
-
-        @pl.when(layer == 0)
-        def _():
-            g2(5, 2)
-            keep(1, k_ff, ffall).wait()
+            add_sum(layer, 10 + c, lax.fori_loop(0, 8, one, jnp.zeros((8, 640), F32)))
+
+        gather_plane(gff, 2, layer, act_back)
 
         def ffin_back(b):
-            return nt(gpre[rows_at(128 * b, 128), :], w[iu])
+            return nt(gpre[pool_rows(b), :], w[iu])
 
         def beside1():
             def one_d(i, inner):
-                cols = pl.ds(pl.multiple_of(128 * i, 128), 128)
-                w[id_, rows_at(128 * i, 128), :] = tn(gff[:, cols], mixed[0:512, :]).astype(BF16)
+                w[id_, rows_at(128 * i, 128), :] = tn(gff[:, cols128(i)], act[...]).astype(BF16)
                 return inner
 
             lax.fori_loop(0, 9, one_d, 0)
-            g0(id_, 2)
-            keep(0, k_mixed.at[layer], mixed).start()
+            g0(id_)
 
             def one_u(i, inner):
-                cols = pl.ds(pl.multiple_of(128 * i, 128), 128)
-                w[iu, rows_at(128 * i, 128), :] = tn(ffall[:, cols], gpre[...]).astype(BF16)
+                w[iu, rows_at(128 * i, 128), :] = tn(ffall[layer, :, cols128(i)], gpre[...]).astype(
+                    BF16
+                )
                 return inner
 
             lax.fori_loop(0, 9, one_u, 0)
-            g0(iu, 1 + 2 * layer)
-
-            @pl.when(layer == 1)
-            def _():
-                keep(1, k_ff, ffall).start()
-
-        total1 = reduce_tensor(2, layer, ffin_back, beside1)
-
-        @pl.when(layer == 0)
-        def _():
-            g1(3, 0)
+            g0(iu)
+
+        total1 = reduce_plane(2, layer, ffin_back, beside1)
 
         def mid(r, sums):
             rr = rows_at(16 * r, 16)
             gf = total1(rr, r)
-            n = own[1, rr, :]
+            n = own[layer, 1, rr, :]
             e = gf * (1.0 + mrow(layer, 4))
             iv = inv[layer, 1, rr, 0:1]
             ga = hb[rr, :] + iv * (
@@ -1293,11 +1143,11 @@
             )
             hb[rr, :] = ga
             gbv = (mrow(layer, 2) * ga).astype(BF16)
-            gb[rows_at(128 * t + 16 * r, 16), :] = gbv
+            gb[own_rows(r), :] = gbv
             return (
                 sums[0] + fold(gf),
                 sums[1] + fold(gf * n),
-                sums[2] + fold(ga * own[2, rr, :]),
+                sums[2] + fold(ga * own[layer, 2, rr, :]),
                 sums[3] + fold(gbv.astype(F32)),
             )
 
@@ -1310,39 +1160,32 @@
         put_sum(layer, 6, s_bproj)
 
         def att_back(b):
-            rr = rows_at(128 * b, 128)
-            v = nn(gb[rr, :], w[ia, :, 768:1152])
-            dqkv[rr, 0:384] = pltpu.roll(v, 320, 1).astype(BF16)
-
-        gather_tensor(gb, 2, layer, att_back)
-
-        @pl.when(layer == 0)
-        def _():
-            g2(4, 3)
-
+            rr = pool_rows(b)
+            doa[rr, :] = pltpu.roll(nn(gb[rr, :], w[ia, :, 384:640]), 224, 1).astype(BF16)
+
+        gather_plane(gb, 3, layer, att_back)
         dkv[...] = jnp.zeros_like(dkv)
         ot[...] = jnp.zeros_like(ot)
 
         def head(j, inner):
-            p = j // 2
-            h = j - 2 * p
-            win = pl.ds(pl.multiple_of(128 * p, 128), 256)
-            vwin = pl.ds(pl.multiple_of(256 + 128 * p, 128), 256)
-            lo = 16 * p + 72 * h
-            qm = jnp.where(head_mask(lo, 512), qa[layer, :, win].astype(F32), 0.0).astype(BF16)
-            dm = jnp.where(head_mask(32 + lo, 512), dqkv[0:512, win].astype(F32), 0.0).astype(BF16)
-            pb[0:512, 0:256] = qm
-            pb[0:512, 256:512] = dm
+            h = j // 2
+            qh = j - 2 * h
+            q_rows = rows_at(512 * qh, 512)
+            q_cols = pl.ds(pl.multiple_of(512 * qh, 512), 512)
+            qm = jnp.where(head_mask(72 * h), qa[layer, q_rows, :].astype(F32), 0.0)
+            dm = jnp.where(head_mask(16 + 72 * h), doa[q_rows, :].astype(F32), 0.0)
+            pb[0:512, 0:256] = qm.astype(BF16)
+            pb[0:512, 256:512] = dm.astype(BF16)
             log_row = lse[layer, j, 0:1, :]
 
             def first(kb, d8):
                 rr = rows_at(256 * kb, 256)
-                s = nt(qkv[layer, rr, win], pb[0:512, 0:256]) * scale
+                s = nt(qkv[layer, rr, 0:256], pb[0:512, 0:256]) * scale
                 pr = jnp.exp(s - log_row)
-                dp = nt(qkv[layer, rr, vwin], pb[0:512, 256:512])
+                dp = nt(qkv[layer, rr, 128:384], pb[0:512, 256:512])
                 pool[rr, 0:512] = pr
                 pool[rr, 512:1024] = dp
-                dkv[rr, vwin] = dkv[rr, vwin] + nn(pr.astype(BF16), pb[0:512, 256:512])
+                dkv[rr, 128:384] = dkv[rr, 128:384] + nn(pr.astype(BF16), pb[0:512, 256:512])
                 return d8 + fold(pr * dp)
 
             d8 = lax.fori_loop(0, 4, first, jnp.zeros((8, 512), F32))
@@ -1352,73 +1195,57 @@
                 rr = rows_at(256 * kb, 256)
                 ds = (pool[rr, 0:512] * (pool[rr, 512:1024] - delta)).astype(BF16)
                 pb[rows_at(512 + 256 * kb, 256), :] = ds
-                dkv[rr, win] = dkv[rr, win] + nn(ds, pb[0:512, 0:256]) * scale
+                dkv[rr, 0:256] = dkv[rr, 0:256] + nn(ds, pb[0:512, 0:256]) * scale
                 return inner2
 
             lax.fori_loop(0, 4, second, 0)
-            otw[...] = tn(qkv[layer, :, win], pb[512:1536, :]) * scale
-            ot[pl.ds(pl.multiple_of(64 + 72 * j, 8), 72), :] = otw[
-                pl.ds(pl.multiple_of(lo, 8), 72), :
+            otw[...] = tn(qkv[layer, :, 0:256], pb[512:1536, :]) * scale
+            ot[pl.ds(pl.multiple_of(32 + 72 * h, 8), 72), q_cols] = otw[
+                pl.ds(pl.multiple_of(72 * h, 8), 72), :
             ]
             return inner
 
         lax.fori_loop(0, 4, head, 0)
 
-        def put_kv(b, total):
-            rr = rows_at(128 * b, 128)
-            kv = dkv[rr, :].astype(BF16)
-            dqkv[rr, 0:640] = kv
-            dqkv[rr, 640:896] = jnp.zeros((128, 256), BF16)
-            return total + fold(kv.astype(F32))
-
-        s_kv = lax.fori_loop(0, 8, put_kv, jnp.zeros((8, 640), F32))
-
-        def put_q(b, total):
-            rr = rows_at(512 * c + 128 * b, 128)
-            dq = ot[:, pl.ds(pl.multiple_of(128 * b, 128), 128)].T.astype(BF16).astype(F32)
-            dqkv[rr, 512:640] = (dkv[rr, 512:640] + dq[:, 0:128]).astype(BF16)
-            dqkv[rr, 640:896] = dq[:, 128:384].astype(BF16)
-            return total + fold(dq)
-
-        s_q = lax.fori_loop(0, 4, put_q, jnp.zeros((8, 384), F32))
-        sm[layer, 8:9, :] = jnp.zeros((1, D), F32)
-        sm[layer, 8:9, 0:640] = jnp.sum(s_kv, axis=0, keepdims=True)
-        sm[layer, 8:9, 512:896] = sm[layer, 8:9, 512:896] + jnp.sum(s_q, axis=0, keepdims=True)
-        g1(id_, 2)
+        def put(b, total):
+            rr = pool_rows(b)
+            dq = ot[:, cols128(b)].T
+            kv = dkv[rr, :]
+            both = jnp.concatenate(
+                (kv[:, 0:256], kv[:, 256:384] + dq[:, 0:128], dq[:, 128:256]), axis=1
+            ).astype(BF16)
+            dqkv[rr, :] = both
+            return total + fold(both.astype(F32))
+
+        add_sum(layer, 8 + c, lax.fori_loop(0, 8, put, jnp.zeros((8, 512), F32)))
 
         @pl.when(layer == 0)
         def _():
-            g2(3, 0)
+            g2(5)
+            g2(4)
 
         def mix_back(block):
-            return nt(dqkv[pool_rows(block), :], w[ia, :, 0:896])
+            return nt(dqkv[pool_rows(block), :], w[ia, :, 0:512])
 
         def beside2():
-            keep(0, k_mixed.at[layer], mixed).wait()
-
             def one(i, inner):
-                cols = pl.ds(pl.multiple_of(128 * i, 128), 128)
                 rr = rows_at(128 * i, 128)
-                w[ia, rr, 0:640] = tn(mixed[:, cols], dqkv[:, 0:640]).astype(BF16)
-                here = rows_at(512 * c, 512)
-                r2 = tn(mixed[here, cols], dqkv[here, 640:896])
-                r3 = tn(gb[:, cols], att[layer])
-                w[ia, rr, 640:768] = r2[:, 0:128].astype(BF16)
-                w[ia, rr, 768:896] = (r2[:, 128:256] + r3[:, 0:128]).astype(BF16)
-                w[ia, rr, 896:1152] = r3[:, 128:384].astype(BF16)
+                r1 = tn(mixed[layer, :, cols128(i)], dqkv[...])
+                r3 = tn(gb[:, cols128(i)], att[layer])
+                w[ia, rr, 0:384] = r1[:, 0:384].astype(BF16)
+                w[ia, rr, 384:512] = (r1[:, 384:512] + r3[:, 0:128]).astype(BF16)
+                w[ia, rr, 512:640] = r3[:, 128:256].astype(BF16)
                 return inner
 
             lax.fori_loop(0, 9, one, 0)
-            g0(ia, 0)
-            g1(iu, 1 + 2 * layer)
-
-
-        total2 = reduce_plane(layer, mix_back, beside2)
+            g0(ia)
+
+        total2 = reduce_plane(3, layer, mix_back, beside2)
 
         def last(r, sums):
             rr = rows_at(16 * r, 16)
             gm = total2(rr, r)
-            n = own[0, rr, :]
+            n = own[layer, 0, rr, :]
             e = gm * (1.0 + mrow(layer, 1))
             iv = inv[layer, 0, rr, 0:1]
             hb[rr, :] = hb[rr, :] + iv * (
@@ -1431,41 +1258,85 @@
         s_shift1, s_scale1 = lax.fori_loop(0, 8, last, (zero8, zero8))
         put_sum(layer, 0, s_shift1)
         put_sum(layer, 1, s_scale1)
-
-        @pl.when(layer == 1)
-        def _():
-            keep(3, k_own, own).start()
-
         return carry
 
     sm[...] = jnp.zeros_like(sm)
     lax.fori_loop(0, LAYERS, backward, 0)
-    small(1)
-    small(0)
-    g2(2, 2)
-    g1(0, 0)
-    g2(1, 1)
-    small_end(1)
-    small_end(0)
-    g2(0, 0)
+    small()
+    g2(3)
+    g2(2)
+    g2(1)
+    small_end()
+    g2(0)
     for i in range(6):
         g3(i)
 
 
-def run_stage(zs_n, x_in, cot, modin, bias, blocks):
+def sum_kernel(zs_n, part_ref, out_ref, got, send_sem, recv_sem):
+    z = lax.axis_index("shard")
+    c = lax.axis_index("context")
+    t = lax.axis_index("tensor")
+    others = [lax.rem(z + d, zs_n) for d in range(1, zs_n)]
+    barrier = pltpu.get_barrier_semaphore()
+    for zz in others:
+        pl.semaphore_signal(barrier, inc=1, device_id=(zz, c, t), device_id_type=MESH)
+    pl.semaphore_wait(barrier, zs_n - 1)
+
+    def copy(d, slot, zz):
+        return pltpu.make_async_remote_copy(
+            src_ref=part_ref,
+            dst_ref=got.at[slot],
+            send_sem=send_sem.at[d],
+            recv_sem=recv_sem.at[slot],
+            device_id=(zz, c, t),
+            device_id_type=MESH,
+        )
+
+    for d, zz in enumerate(others):
+        copy(d, z, zz).start()
+    got[z] = part_ref[...]
+    for d, zz in enumerate(others):
+        copy(d, zz, zz).wait_recv()
+        copy(d, z, zz).wait_send()
+    total = got[0]
+    for zz in range(1, zs_n):
+        total = total + got[zz]
+    out_ref[...] = total
+
+
+def sum_shards(zs_n, part):
+    vm = pl.BlockSpec(memory_space=pltpu.VMEM)
+    dma = pltpu.SemaphoreType.DMA
+    return pl.pallas_call(
+        functools.partial(sum_kernel, zs_n),
+        name="sum_shards",
+        out_shape=jax.ShapeDtypeStruct(part.shape, F32),
+        in_specs=[vm],
+        out_specs=vm,
+        scratch_shapes=[
+            pltpu.VMEM((zs_n,) + part.shape, F32),
+            dma((zs_n - 1,)),
+            dma((zs_n,)),
+        ],
+        compiler_params=pltpu.CompilerParams(collective_id=1, has_side_effects=True),
+    )(part)
+
+
+def run_stage(zs_n, x_in, cot, modin, bias, block_a, block_u, block_d):
     vm = pl.BlockSpec(memory_space=pltpu.VMEM)
     anyspace = pl.BlockSpec(memory_space=pl.ANY)
     dma = pltpu.SemaphoreType.DMA
     sds = jax.ShapeDtypeStruct
     scratch = [
-        pltpu.VMEM((6, D, D), BF16),
-        pltpu.VMEM((1024, D), BF16),
-        pltpu.VMEM((2, 1024, 896), BF16),
-        pltpu.VMEM((2, 512, 384), BF16),
-        pltpu.VMEM((2, 512, 384), BF16),
-        pltpu.VMEM((512, D), BF16),
-        pltpu.VMEM((512, D), F32),
-        pltpu.VMEM((4, 128, D), F32),
+        pltpu.VMEM((6, D, 640), BF16),
+        pltpu.VMEM((2, 1024, D), BF16),
+        pltpu.VMEM((2, 1024, 512), BF16),
+        pltpu.VMEM((2, 1024, 256), BF16),
+        pltpu.VMEM((2, 1024, 256), BF16),
+        pltpu.VMEM((2, 1024, D), BF16),
+        pltpu.VMEM((2, 1024, 640), F32),
+        pltpu.VMEM((1024, 640), BF16),
+        pltpu.VMEM((2, 4, 128, D), F32),
         pltpu.VMEM((2, 2, 128, 128), F32),
         pltpu.VMEM((2, 4, 8, 512), F32),
         pltpu.VMEM((zs_n, 16, 384), F32),
@@ -1479,43 +1350,34 @@
         pltpu.VMEM((128, D), BF16),
         pltpu.VMEM((128, D), BF16),
         pltpu.VMEM((128, D), BF16),
-        pltpu.VMEM((512, D), BF16),
-        pltpu.VMEM((512, D), BF16),
-        pltpu.VMEM((512, D), BF16),
-        pltpu.VMEM((1024, 896), BF16),
-        pltpu.VMEM((1024, 640), F32),
+        pltpu.VMEM((1024, D), BF16),
+        pltpu.VMEM((1024, 640), BF16),
+        pltpu.VMEM((1024, D), BF16),
+        pltpu.VMEM((1024, 256), BF16),
+        pltpu.VMEM((1024, 512), BF16),
+        pltpu.VMEM((1024, 384), F32),
         pltpu.VMEM((1536, 512), BF16),
         pltpu.VMEM((256, 512), F32),
-        pltpu.VMEM((384, 512), F32),
-        pltpu.VMEM((4, zs_n, 144, D), BF16),
-        pltpu.VMEM((6, zs_n - 1, 144, D), BF16),
+        pltpu.VMEM((256, 1024), F32),
+        pltpu.VMEM((6, zs_n - 1, 288, 640), BF16),
         pltpu.VMEM((2, 16, D), F32),
-        pltpu.VMEM((2, 3, 16, D), F32),
+        pltpu.VMEM((3, 2, 16, D), F32),
         dma((zs_n - 1,)),
         dma((zs_n,)),
-        dma((6, zs_n)),
-        dma((6, zs_n)),
-        dma((6, zs_n)),
+        dma((6, 4)),
         dma((6, zs_n)),
         dma((6,)),
-        dma((2, 13)),
-        dma((2, 13)),
-        dma((3, 2, 5)),
-        dma((3, 2, 5)),
-        dma((3, 2, 3)),
-        dma((3, 2, 3)),
-        dma((2, 8)),
-        dma((2, 8)),
-        dma((6, zs_n)),
-        dma((6, zs_n)),
+        dma((4, 2, 13)),
+        dma((4, 2, 13)),
+        dma((4, 2, 8)),
+        dma((4, 2, 8)),
         dma((6, zs_n)),
         dma((6, zs_n)),
         dma((6,)),
         dma((6,)),
         dma((6,)),
-        dma((2, 3 + zs_n)),
-        dma((2, 3 + zs_n)),
-        dma((4,)),
+        dma((3 + zs_n,)),
+        dma((3 + zs_n,)),
     ]
     return pl.pallas_call(
         functools.partial(stage_kernel, zs_n),
@@ -1523,20 +1385,16 @@
         out_shape=(
             sds((128, D), BF16),
             sds((128, D), F32),
-            sds((6, 288, D), BF16),
-            sds((2, zs_n, 16, D), F32),
-            sds((2, 1024, D), BF16),
-            sds((512, D), BF16),
-            sds((512, D), F32),
-            sds((4, 128, D), F32),
+            sds((6, 2, 288, 640), BF16),
+            sds((zs_n, 2, 16, D), F32),
         ),
-        in_specs=[vm, vm, vm, vm, anyspace],
-        out_specs=(vm, vm, anyspace, vm, anyspace, anyspace, anyspace, anyspace),
+        in_specs=[vm, vm, vm, vm, anyspace, anyspace, anyspace],
+        out_specs=(vm, vm, anyspace, vm),
         scratch_shapes=scratch,
         compiler_params=pltpu.CompilerParams(
             collective_id=0, has_side_effects=True, vmem_limit_bytes=67043328
         ),
-    )(x_in, cot, modin, bias, blocks)
+    )(x_in, cot, modin, bias, block_a, block_u, block_d)
 
 
 def fast_body(
@@ -1556,8 +1414,10 @@
     cotangent,
 ):
     z = lax.axis_index("shard")
+    c = lax.axis_index("context")
     cols = w_ada.shape[3]
-    heads = w_qkv.shape[3]
+    part = w_qkv.shape[3] // 2
+    units = up_weight.shape[2] // 2
     cond_low = jax.nn.silu(cond).astype(BF16)
     mod_terms = (
         jnp.einsum("sd,ldkc->lskc", cond_low, w_ada, preferred_element_type=F32)
@@ -1566,60 +1426,77 @@
     modin = jnp.pad(
         mod_terms.astype(F32).transpose(1, 0, 2, 3), ((0, 0), (0, 0), (0, 2), (0, 384 - cols))
     ).reshape(zs_n, 16, 384)
-    parts = []
-    for layer in range(LAYERS):
-        parts.append(
-            jnp.concatenate(
-                (
-                    w_qkv[layer, 1],
-                    w_qkv[layer, 2],
-                    w_qkv[layer, 0],
-                    w_proj[layer].T,
-                ),
-                axis=1,
-            )
-        )
-        parts.append(up_weight[layer])
-        parts.append(down_weight[layer].T)
-    blocks = jnp.stack(parts)
-    zero = jnp.zeros((LAYERS, heads), F32)
-    b_qkv = jnp.concatenate(
-        (zero, b_qv[:, 1].astype(F32), b_qv[:, 0].astype(F32), zero), axis=1
-    )
+
+    def mine(array, size, axis):
+        return lax.dynamic_slice_in_dim(array, c * size, size, axis)
+
+    def wide(array, size):
+        return jnp.pad(array, ((0, 0),) * (array.ndim - 1) + ((0, size - array.shape[-1]),))
+
+    heads = mine(w_qkv, part, 3)
+    block_a = wide(
+        jnp.concatenate(
+            (
+                heads[:, 1],
+                heads[:, 2],
+                heads[:, 0],
+                mine(w_proj, part, 1).transpose(0, 2, 1),
+            ),
+            axis=2,
+        ),
+        640,
+    )
+    block_u = wide(mine(up_weight, units, 2), 640)
+    block_d = wide(mine(down_weight, units, 1).transpose(0, 2, 1), 640)
+    b_heads = mine(b_qv, part, 2).astype(F32)
+    b_qkv = jnp.concatenate((jnp.zeros((LAYERS, part), F32), b_heads[:, 1], b_heads[:, 0]), axis=1)
     bias = jnp.stack(
-        (b_qkv, b_proj.astype(F32), up_bias_vector.astype(F32), down_bias_vector.astype(F32)),
+        (
+            wide(b_qkv, D),
+            b_proj.astype(F32),
+            wide(mine(up_bias_vector, units, 1).astype(F32), D),
+            down_bias_vector.astype(F32),
+        ),
         axis=1,
     )
     out, grad_in, gw, small = run_stage(
-        zs_n, x_in[:, 0], cotangent[:, 0], modin, bias, blocks
-    )[:4]
+        zs_n, x_in[:, 0], cotangent[:, 0], modin, bias, block_a, block_u, block_d
+    )
     grad_mod = small[:, :, 0:6, :].astype(BF16)
     mod_cols = lax.dynamic_slice_in_dim(grad_mod, z * cols, cols, 3)
-    grad_w_ada = jnp.einsum("sd,lskc->ldkc", cond_low, mod_cols, preferred_element_type=F32)
-    grad_b_ada = jnp.sum(mod_cols.astype(F32), axis=1)
-    cond_part = jnp.einsum("lskc,ldkc->sd", mod_cols, w_ada, preferred_element_type=F32)
-    cond_total = lax.psum(cond_part, "shard")
+    grad_w_ada = jnp.einsum("sd,slkc->ldkc", cond_low, mod_cols, preferred_element_type=F32)
+    grad_b_ada = jnp.sum(mod_cols.astype(F32), axis=0)
+    cond_part = jnp.einsum("slkc,ldkc->sd", mod_cols, w_ada, preferred_element_type=F32)
+    cond_total = sum_shards(zs_n, cond_part)
     silu_value, silu_back = jax.vjp(jax.nn.silu, cond)
     grad_cond = silu_back(cond_total)[0]
-    sums = jnp.sum(small[:, :, 6:10, :], axis=1)
-    gw = gw.reshape(LAYERS, 3, cols, D).astype(F32)
-    ga = gw[:, 0]
+    sums = jnp.sum(small[:, :, 6:12, :], axis=0)
+
+    def halves(row, start, size):
+        return jnp.concatenate(
+            (sums[:, row, start : start + size], sums[:, row + 1, start : start + size]), axis=1
+        )
+
+    gw = gw.reshape(LAYERS, 3, 2, cols, 640)
+
+    def both(m, start, size):
+        return jnp.concatenate(
+            (gw[:, m, 0, :, start : start + size], gw[:, m, 1, :, start : start + size]), axis=2
+        ).astype(F32)
+
     return (
         out[:, None],
         grad_in[:, None],
         grad_cond,
         grad_w_ada,
         grad_b_ada,
-        jnp.stack(
-            (ga[:, :, 2 * heads : 3 * heads], ga[:, :, 0:heads], ga[:, :, heads : 2 * heads]),
-            axis=1,
-        ),
-        jnp.stack((sums[:, 2, 2 * heads : 3 * heads], sums[:, 2, heads : 2 * heads]), axis=1),
-        ga[:, :, 3 * heads :].transpose(0, 2, 1),
+        jnp.stack((both(0, 2 * part, part), both(0, 0, part), both(0, part, part)), axis=1),
+        jnp.stack((halves(2, 2 * part, part), halves(2, part, part)), axis=1),
+        both(0, 3 * part, part).transpose(0, 2, 1),
         sums[:, 0],
-        gw[:, 1],
-        sums[:, 3],
-        gw[:, 2].transpose(0, 2, 1),
+        both(1, 0, units),
+        halves(4, 0, units),
+        both(2, 0, units).transpose(0, 2, 1),
         sums[:, 1],
     )
 

time: 631 us -> 515 us (0.82)
  Pallas kernels: 539 us -> 459 us
  blocking collectives: 32.2 us -> 0 us
  local copies, waits for them, and re-layouts: 32.7 us -> 22.5 us
  other arithmetic: 6.6 us -> 13.3 us
    pallas_call x1, Pallas kernels: 539 us -> 451 us  [run_stage(): pl.pallas_call(functools.partial(stage_kernel, zs_n), name='two_blocks',...]
    psum x1 -> x0, blocking collectives: 32.2 us -> none  [fast_body(): cond_total = lax.psum(cond_part, 'shard')]
    pallas_call x0 -> x1, Pallas kernels: none -> 8.05 us  [sum_shards(): pl.pallas_call(functools.partial(sum_kernel, zs_n), name='sum_shards', ou...]
    unnamed x33 -> x34, local copies, waits for them, and re-layouts: 16.3 us -> 8.89 us
where the time goes in v2:
time: 515 us
  Pallas kernels  459 us (89%)
  local copies, waits for them, and re-layouts  22.5 us (4%)
  matrix products  19.2 us (4%)
  other arithmetic  13.3 us (3%)
    pallas_call x1, Pallas kernels, run_stage(): pl.pallas_call(functools.partial(stage_kernel, zs_n), name='two_blocks',...  451 us

profile of v2, /device:TPU:0, one launch (start us, length us, event | category | flops | bytes accessed | tf_op | source)
XLA Modules:
  0.0 514.6 jit_solution(4689093532355409384)
XLA Ops:
  0.7 0.8 constant_dynamic-slice_fusion.3
  1.5 0.1 pad_maximum_fusion.3
  1.5 0.8 constant_dynamic-slice_fusion.2
  2.4 0.7 reshape.133
  3.1 0.7 reshape.135
  3.7 0.7 pad_maximum_fusion.bias_ref
  4.4 0.7 copy.75
  5.1 6.0 %fusion.19 = f32[4,2,6,288]{3,0,2,1:T(4,128)S(1)} fusion(bf16[2,1152,6,288]{1,3,2,0:T(8,128)(2,1)} %param.15, f32[4,1152]{1,0:T(4,128)} %param.14), kind=kOutput, calls=%fused_computation.66 | convolution fusion | flops 31873536 | bytes 8036352 | tf_op jit(solution)/shard_map/sd,ldkc->lskc/dot_general | solution.py:1423
  11.1 0.7 bitcast_convert_fusion.modin_ref
  11.8 0.0 copy-done.12
  11.8 0.2 copy.113
  12.0 0.0 copy-done.7
  12.0 0.0 copy-start.4
  12.0 0.4 constant_dynamic-slice_fusion
  12.3 0.9 pad.28.su_ref
  13.3 0.0 copy-done.8
  13.3 0.3 dynamic-slice_bitcast_fusion
  13.6 0.9 pad.29.sd_ref
  14.6 0.0 copy-done.4
  14.6 0.4 dynamic-slice_bitcast_fusion.3
  14.9 1.3 fusion.11.sa_ref
  16.3 450.6 %two_blocks.1 = (bf16[128,1152]{1,0:T(8,128)(2,1)}, f32[128,1152]{1,0:T(8,128)}, bf16[6,2,288,640]{3,2,1,0:T(8,128)(2,1)}, f32[4,2,16,1152]{3,2,1,0:T(8,128)}) custom-call(bf16[128,1152]{1,0:T(8,128)(2,1)} %bitcast.113, bf16[128,1152]{1,0:T(8,128)(2,1)} %bitcast.114, f32[4,16,384]{2,1,0:T(8,128)} %bitcast_convert_fusion.modin_ref, ...), custom_call_target="tpu_custom_call" | custom-call | tf_op jit(solution)/shard_map/two_blocks/pallas_call | solution.py:1382
  466.9 2.5 copy.99
  469.4 1.1 slice_reduce_fusion
  470.5 1.0 slice.111
  471.5 0.1 convert_reduce_fusion
  471.6 0.6 copy.100
  472.3 0.1 fusion.26
  472.4 0.1 maximum_bitcast_fusion.1
  472.4 0.1 maximum_bitcast_fusion
  472.5 0.6 copy.101
  473.2 0.7 pad_maximum_fusion.1
  473.9 0.6 copy_bitcast_fusion
  474.5 5.0 fusion.2.part_ref
  479.5 8.1 %sum_shards.1 = f32[4,1152]{1,0:T(4,128)} custom-call(f32[4,1152]{1,0:T(4,128)} %fusion.2.part_ref), custom_call_target="tpu_custom_call" | custom-call | tf_op jit(solution)/shard_map/sum_shards/pallas_call | solution.py:1310
  487.6 0.0 copy-done.10
  487.6 1.4 fusion.16
  488.9 3.9 fusion.23
  492.8 2.0 slice_bitcast_fusion.1
  494.9 1.8 copy.123
  496.7 1.8 copy.124
  498.5 2.0 convert_bitcast_fusion.1
  500.5 3.2 convert_bitcast_fusion
  503.7 0.0 copy-done.2
  503.7 0.0 copy-done.3
  503.7 2.0 maximum_convert_fusion
  505.7 8.2 %convolution_bitcast_fusion = f32[2,1152,6,288]{1,3,2,0:T(8,128)} fusion(bf16[4,2,6,288]{3,2,1,0:T(8,128)(2,1)S(1)} %copy-done.6, f32[4,1152]{1,0:T(4,128)S(1)} %copy-done.11), kind=kOutput, calls=%fused_computation | convolution fusion | flops 31873536 | bytes 15971328 | tf_op jit(solution)/shard_map/sd,slkc->ldkc/dot_general | solution.py:1467
  513.9 0.7 copy.151
  (34 shorter events, 0.2 us)
Async XLA Ops:
  5.1 6.7 %copy-start.12 = (bf16[2,288,288]{2,1,0:T(8,128)(2,1)S(1)}, bf16[2,288,288]{2,1,0:T(8,128)(2,1)}, u32[]{:S(2)}) copy-start(bf16[2,288,288]{2,1,0:T(8,128)(2,1)} %param.19) | copy-start | bytes 995332
  5.1 6.9 %copy-start.7 = (bf16[2,288,1152]{2,1,0:T(8,128)(2,1)S(1)}, bf16[2,288,1152]{2,1,0:T(8,128)(2,1)}, u32[]{:S(2)}) copy-start(bf16[2,288,1152]{2,1,0:T(8,128)(2,1)} %param.21) | copy-start | bytes 3981316
  11.1 2.2 copy-start.8
  12.0 2.6 copy-start.4
  471.6 2.8 copy-start.5
  474.5 13.1 %copy-start.10 = (f32[4,1152]{1,0:T(4,128)S(1)}, f32[4,1152]{1,0:T(4,128)}, u32[]{:S(2)}) copy-start(f32[4,1152]{1,0:T(4,128)} %param.14) | copy-start | bytes 55300
  500.5 3.2 copy-start
  500.5 3.2 copy-start.1
  500.5 3.2 copy-start.2
  500.5 3.2 copy-start.3
  503.7 2.0 copy-start.6
  503.7 2.0 copy-start.11
  505.7 8.2 %copy-start.9 = (bf16[128,1152]{1,0:T(8,128)(2,1)S(1)}, bf16[128,1152]{1,0:T(8,128)(2,1)}, u32[]{:S(2)}) copy-start(bf16[128,1152]{1,0:T(8,128)(2,1)} %get-tuple-element.17) | copy-start | bytes 884740

commit v3 on v2

--- a/solution.py
+++ b/solution.py
@@ -484,6 +484,7 @@
     otw,
     ot,
     rz,
+    rzr,
     sm,
     smr,
     m_s,
@@ -500,6 +501,8 @@
     gf_s,
     gf_r,
     g_l,
+    g_c,
+    r_c,
     sm_s,
     sm_r,
 ):
@@ -599,9 +602,9 @@
         def _():
             w_take(3 * layer + m, z_far).wait_send()
 
-    for layer in range(LAYERS):
-        for m in range(3):
-            w0(layer, m)
+    w0(0, 0)
+    w0(0, 1)
+
 
     modr[z] = modin_ref[z]
     for zz in zo:
@@ -615,214 +618,234 @@
     def mrow(layer, kind):
         return modv[layer, kind : kind + 1, :]
 
-    def ap_copy(buf, phase, layer, index, block, offset, size, dev):
-        part = buf.at[rows_at(128 * block + offset, size)]
-        return rc(part, part, ap_s.at[phase, layer, index], ap_r.at[phase, layer, index], dev)
-
-    def ap_parts(buf, phase, layer):
-        b_own, b_p = 4 * c + t, 4 * c + tp
-        b_y, b_yp = 4 * c + t_far, 4 * c + tp_far
-        b_x, b_xp = 4 * (1 - c) + t, 4 * (1 - c) + tp
-        b_d, b_dp = 4 * (1 - c) + t_far, 4 * (1 - c) + tp_far
-        sends = [
-            (0, b_own, 0, 128, dev_p),
-            (1, b_own, 0, 64, dev_y),
-            (4, b_own, 64, 64, dev_x),
-            (2, b_own, 64, 64, dev_y),
-            (3, b_own, 0, 64, dev_x),
-            (5, b_y, 0, 64, dev_x),
-            (6, b_x, 64, 64, dev_y),
-            (7, b_y, 0, 64, dev_p),
-            (8, b_y, 64, 64, dev_p),
-            (9, b_x, 0, 64, dev_p),
-            (10, b_x, 64, 64, dev_p),
-            (11, b_d, 0, 64, dev_p),
-            (12, b_d, 64, 64, dev_p),
-        ]
-        recvs = {
-            0: (b_p, 0, 128),
-            1: (b_y, 0, 64),
-            2: (b_y, 64, 64),
-            3: (b_x, 0, 64),
-            4: (b_x, 64, 64),
-            5: (b_d, 0, 64),
-            6: (b_d, 64, 64),
-            7: (b_yp, 0, 64),
-            8: (b_yp, 64, 64),
-            9: (b_xp, 0, 64),
-            10: (b_xp, 64, 64),
-            11: (b_dp, 0, 64),
-            12: (b_dp, 64, 64),
-        }
-
-        def send(index):
-            for entry in sends:
-                if entry[0] == index:
-                    ap_copy(buf, phase, layer, *entry).start()
-
-        def wait(index):
-            ap_copy(buf, phase, layer, index, *recvs[index], dev_p).wait_recv()
-
-        def drain():
-            for entry in sends:
-                ap_copy(buf, phase, layer, *entry).wait_send()
-
-        return send, wait, drain
-
-    def gather_plane(buf, phase, layer, compute):
-        send, wait, drain = ap_parts(buf, phase, layer)
-        for index in (0, 1, 4, 2, 3):
-            send(index)
-
-        def step(i, carry):
-            b0, b1, b2 = lax.rem(i, 2), lax.rem(i // 2, 2), i // 4
-
-            @pl.when(i == 1)
-            def _():
-                wait(0)
-
-            @pl.when(i == 2)
-            def _():
-                wait(1)
-                send(5)
-                send(7)
-                wait(4)
-                send(6)
-                send(10)
-                wait(2)
-                send(8)
-                wait(3)
-                send(9)
-
-            @pl.when(i == 3)
-            def _():
-                wait(7)
-                wait(8)
-
-            @pl.when(i == 5)
-            def _():
-                wait(9)
-                wait(10)
-
-            @pl.when(i == 6)
-            def _():
-                wait(5)
-                send(11)
-                wait(6)
-                send(12)
-
-            @pl.when(i == 7)
-            def _():
-                wait(11)
-                wait(12)
-
-            block = (
-                4 * lax.rem(c + b2, 2) + 2 * lax.rem(y + b1, 2) + lax.rem(k + b0, 2)
-            )
-            compute(block)
-            return carry
-
-        lax.fori_loop(0, 8, step, 0)
-        drain()
+    def when(condition, action):
+        @pl.when(condition)
+        def _():
+            action()
+
+    def rows_of(s, block, offset=0, size=64):
+        return rows_at(512 * s + 64 * block + offset, size)
+
+    b_own, b_p = 4 * c + t, 4 * c + tp
+    b_y, b_yp = 4 * c + t_far, 4 * c + tp_far
+    b_x, b_xp = 4 * (1 - c) + t, 4 * (1 - c) + tp
+    b_d, b_dp = 4 * (1 - c) + t_far, 4 * (1 - c) + tp_far
+    sends = {
+        0: (b_own, 0, 64, dev_p),
+        1: (b_own, 0, 64, dev_y),
+        2: (b_own, 0, 64, dev_x),
+        3: (b_y, 0, 32, dev_x),
+        4: (b_x, 32, 32, dev_y),
+        5: (b_y, 0, 64, dev_p),
+        6: (b_x, 0, 64, dev_p),
+        7: (b_d, 0, 32, dev_p),
+        8: (b_d, 32, 32, dev_p),
+    }
+    recvs = {
+        0: (b_p, 0, 64),
+        1: (b_y, 0, 64),
+        2: (b_x, 0, 64),
+        3: (b_d, 0, 32),
+        4: (b_d, 32, 32),
+        5: (b_yp, 0, 64),
+        6: (b_xp, 0, 64),
+        7: (b_dp, 0, 32),
+        8: (b_dp, 32, 32),
+    }
+
+    class Gather:
+        def __init__(self, buf, phase, layer):
+            self.buf, self.phase, self.layer = buf, phase, layer
+
+        def copy(self, s, index, block, offset, size, dev):
+            part = self.buf.at[rows_of(s, block, offset, size)]
+            at = (self.phase, self.layer, s, index)
+            return rc(part, part, ap_s.at[at], ap_r.at[at], dev)
+
+        def send(self, s, *indices):
+            for index in indices:
+                self.copy(s, index, *sends[index]).start()
+
+        def wait(self, s, *indices):
+            for index in indices:
+                self.copy(s, index, *recvs[index], dev_p).wait_recv()
+
+        def begin(self, s):
+            self.send(s, 1, 2, 0)
+
+        def hand_on(self, s):
+            self.wait(s, 1)
+            self.send(s, 3, 5)
+            self.wait(s, 2)
+            self.send(s, 4, 6)
+
+        def hand_last(self, s):
+            self.wait(s, 3)
+            self.send(s, 7)
+            self.wait(s, 4)
+            self.send(s, 8)
+
+        def drain(self):
+            for s in range(2):
+                for index, entry in sends.items():
+                    self.copy(s, index, *entry).wait_send()
+
+        def alone(self):
+            for s in range(2):
+                self.hand_on(s)
+            for s in range(2):
+                self.hand_last(s)
+            for s in range(2):
+                self.wait(s, 0, 5, 6, 7, 8)
+
+        def run(self, compute, live=True):
+            def step(n, carry):
+                s, f = lax.rem(n, 2), n // 2
+
+                def comm(*a):
+                    first = a[0]
+                    when((n == first) & live, lambda: a[1]())
+
+                comm(0, lambda: self.wait(0, 0))
+                comm(1, lambda: self.wait(1, 0))
+                comm(2, lambda: (self.hand_on(0), self.wait(0, 5)))
+                comm(3, lambda: (self.hand_on(1), self.wait(1, 5)))
+                comm(4, lambda: self.wait(0, 6))
+                comm(5, lambda: (self.wait(1, 6), self.hand_last(0)))
+                comm(6, lambda: (self.wait(0, 7, 8), self.hand_last(1)))
+                comm(7, lambda: self.wait(1, 7, 8))
+                chip = 2 * lax.rem(c + f // 2, 2) + lax.rem(y + lax.rem(f, 2), 2)
+                compute(s, 512 * s + 128 * chip)
+                return carry
+
+            lax.fori_loop(0, 8, step, 0)
+            when(jnp.logical_and(live, True), self.drain)
 
     def pool_rows(i):
         return rows_at(128 * i, 128)
 
-    def reduce_plane(phase, layer, compute, beside):
-        def to_p(i, slot):
+    def add_rows(count, fn):
+        def one(r, inner):
+            fn(16 * r)
+            return inner
+
+        lax.fori_loop(0, count // 16, one, 0)
+
+    class Reduce:
+        def __init__(self, phase, layer, compute):
+            self.phase, self.layer, self.compute = phase, layer, compute
+
+        def sem(self, s, index):
+            at = (self.phase, self.layer, s, index)
+            return rp_s.at[at], rp_r.at[at]
+
+        def to_p(self, s, q):
+            there = pool.at[rows_at(512 * s + 128 * q + 64 * (1 - k), 64)]
+            return rc(there, ra.at[s, q], *self.sem(s, q), dev_p)
+
+        def part(self, s, index, src, dst, offset, dev):
             return rc(
-                pool.at[pool_rows(i)],
-                ra.at[slot],
-                rp_s.at[phase, layer, slot],
-                rp_r.at[phase, layer, slot],
-                dev_p,
+                src.at[s, pl.ds(offset, 32)],
+                dst.at[s, pl.ds(offset, 32)],
+                *self.sem(s, index),
+                dev,
             )
 
-        d_x = rc(dsend.at[0:64], drecv.at[0:64], rp_s.at[phase, layer, 4], rp_r.at[phase, layer, 4], dev_x)
-        d_y = rc(dsend.at[64:128], drecv.at[64:128], rp_s.at[phase, layer, 5], rp_r.at[phase, layer, 5], dev_y)
-        to_x = rc(xsend, xrecv, rp_s.at[phase, layer, 6], rp_r.at[phase, layer, 6], dev_x)
-        to_y = rc(ysend, yrecv, rp_s.at[phase, layer, 7], rp_r.at[phase, layer, 7], dev_y)
-
-        def step(i, carry):
-            q = i // 2
-            b0, b1, b2 = 1 - lax.rem(i, 2), 1 - lax.rem(q, 2), 1 - q // 2
-            block = (
-                4 * lax.rem(c + b2, 2) + 2 * lax.rem(y + b1, 2) + lax.rem(k + b0, 2)
+        def leg(self, s, index):
+            src, dst, offset, dev = {
+                4: (dsend, drecv, 0, dev_x),
+                5: (dsend, drecv, 32, dev_y),
+                6: (xsend, xrecv, 0, dev_x),
+                7: (ysend, yrecv, 32, dev_y),
+                8: (xsend, xrecv, 32, dev_x),
+                9: (ysend, yrecv, 0, dev_y),
+            }[index]
+            return self.part(s, index, src, dst, offset, dev)
+
+        def pair(self, s, q, row):
+            mine = pool[rows_at(512 * s + 128 * q + 64 * k + row, 16), :]
+            return mine + ra[s, q, rows_at(row, 16), :]
+
+        def step(self, s, q):
+            chip = 2 * lax.rem(c + 1 - q // 2, 2) + lax.rem(y + 1 - lax.rem(q, 2), 2)
+            pool[rows_at(512 * s + 128 * q, 128), :] = self.compute(512 * s + 128 * chip)
+            self.to_p(s, q).start()
+            def diagonal():
+                self.to_p(s, 0).wait_recv()
+
+                def fn(row):
+                    dsend[s, rows_at(row, 16), :] = self.pair(s, 0, row).astype(BF16)
+
+                add_rows(64, fn)
+                self.leg(s, 4).start()
+                self.leg(s, 5).start()
+
+            def across_x():
+                self.to_p(s, 1).wait_recv()
+
+                def fn(row):
+                    xsend[s, rows_at(row, 16), :] = self.pair(s, 1, row).astype(BF16)
+
+                add_rows(32, fn)
+                self.leg(s, 6).start()
+
+            def across_y():
+                self.to_p(s, 2).wait_recv()
+
+                def fn(row):
+                    ysend[s, rows_at(32 + row, 16), :] = self.pair(s, 2, 32 + row).astype(BF16)
+
+                add_rows(32, fn)
+                self.leg(s, 7).start()
+
+            when(q == 1, diagonal)
+            when(q == 2, across_x)
+            when(q == 3, across_y)
+
+        def hand_on(self, s):
+            self.leg(s, 5).wait_recv()
+
+            def fx(row):
+                rr = rows_at(32 + row, 16)
+                xsend[s, rr, :] = (
+                    self.pair(s, 1, 32 + row) + drecv[s, rr, :].astype(F32)
+                ).astype(BF16)
+
+            add_rows(32, fx)
+            self.leg(s, 8).start()
+            self.leg(s, 4).wait_recv()
+
+            def fy(row):
+                rr = rows_at(row, 16)
+                ysend[s, rr, :] = (self.pair(s, 2, row) + drecv[s, rr, :].astype(F32)).astype(BF16)
+
+            add_rows(32, fy)
+            self.leg(s, 9).start()
+
+        def run(self):
+            def one(n, carry):
+                s, q = n // 4, lax.rem(n, 4)
+                self.step(s, q)
+                when(n == 5, lambda: self.hand_on(0))
+                return carry
+
+            lax.fori_loop(0, 8, one, 0)
+            self.hand_on(1)
+
+        def finish(self, s):
+            self.to_p(s, 3).wait_recv()
+            for index in (6, 7, 8, 9):
+                self.leg(s, index).wait_recv()
+            for q in range(4):
+                self.to_p(s, q).wait_send()
+            for index in range(4, 10):
+                self.leg(s, index).wait_send()
+
+        def total(self, s, row):
+            rr = rows_at(row, 16)
+            return (
+                self.pair(s, 3, row) + xrecv[s, rr, :].astype(F32) + yrecv[s, rr, :].astype(F32)
             )
-            pool[pool_rows(i), :] = compute(block)
-
-            @pl.when(b0 == 1)
-            def _():
-                to_p(i, q).start()
-
-            @pl.when(i == 1)
-            def _():
-                to_p(0, 0).wait_recv()
-
-                def add(r, inner):
-                    rr = rows_at(16 * r, 16)
-                    dsend[rr, :] = (pool[rows_at(128 + 16 * r, 16), :] + ra[0, rr, :]).astype(BF16)
-                    return inner
-
-                lax.fori_loop(0, 8, add, 0)
-                d_x.start()
-                d_y.start()
-
-            @pl.when(i == 3)
-            def _():
-                to_p(2, 1).wait_recv()
-                d_y.wait_recv()
-
-                def add(r, inner):
-                    rr = rows_at(16 * r, 16)
-                    rh = rows_at(64 + 16 * r, 16)
-                    xsend[rr, :] = (pool[rows_at(384 + 16 * r, 16), :] + ra[1, rr, :]).astype(BF16)
-                    xsend[rh, :] = (
-                        pool[rows_at(448 + 16 * r, 16), :] + ra[1, rh, :] + drecv[rh, :].astype(F32)
-                    ).astype(BF16)
-                    return inner
-
-                lax.fori_loop(0, 4, add, 0)
-                to_x.start()
-
-            @pl.when(i == 5)
-            def _():
-                to_p(4, 2).wait_recv()
-                d_x.wait_recv()
-
-                def add(r, inner):
-                    rr = rows_at(16 * r, 16)
-                    rh = rows_at(64 + 16 * r, 16)
-                    ysend[rr, :] = (
-                        pool[rows_at(640 + 16 * r, 16), :] + ra[2, rr, :] + drecv[rr, :].astype(F32)
-                    ).astype(BF16)
-                    ysend[rh, :] = (pool[rows_at(704 + 16 * r, 16), :] + ra[2, rh, :]).astype(BF16)
-                    return inner
-
-                lax.fori_loop(0, 4, add, 0)
-                to_y.start()
-
-            return carry
-
-        lax.fori_loop(0, 8, step, 0)
-        beside()
-        to_p(6, 3).wait_recv()
-        to_x.wait_recv()
-        to_y.wait_recv()
-        for q in range(4):
-            to_p(2 * q, q).wait_send()
-        for copy in (d_x, d_y, to_x, to_y):
-            copy.wait_send()
-
-        def total(rr, r):
-            return (
-                pool[rows_at(896 + 16 * r, 16), :]
-                + ra[3, rr, :]
-                + xrecv[rr, :].astype(F32)
-                + yrecv[rr, :].astype(F32)
-            )
-
-        return total
 
     def spread(column):
         return jnp.broadcast_to(column, (column.shape[0], 128))
@@ -836,180 +859,250 @@
         lane = lax.broadcasted_iota(jnp.int32, (512, 256), 1)
         return (lane >= lo) & (lane < lo + HD)
 
-    own_block = 4 * c + t
-
-    def own_rows(r):
-        return rows_at(128 * own_block + 16 * r, 16)
+    def own_rows(s, row):
+        return rows_at(512 * s + 64 * b_own + row, 16)
 
     def cols128(b):
         return pl.ds(pl.multiple_of(128 * b, 128), 128)
 
-    def forward(layer, carry):
-        ia, iu, id_ = 3 * layer, 3 * layer + 1, 3 * layer + 2
-
+    def piece(start):
+        return rows_at(start, 128)
+
+    def norm_in(layer, s):
         def ln1(r, inner):
-            rr = rows_at(16 * r, 16)
+            rr = rows_at(64 * s + 16 * r, 16)
             n, iv = layer_norm(hb[rr, :])
             own[layer, 0, rr, :] = n
             inv[layer, 0, rr, :] = spread(iv)
-            mixed[layer, own_rows(r), :] = (n * (1.0 + mrow(layer, 1)) + mrow(layer, 0)).astype(
-                BF16
-            )
+            mixed[layer, own_rows(s, 16 * r), :] = (
+                n * (1.0 + mrow(layer, 1)) + mrow(layer, 0)
+            ).astype(BF16)
             return inner
 
-        lax.fori_loop(0, 8, ln1, 0)
-
-        def project(block):
-            rr = pool_rows(block)
+        lax.fori_loop(0, 4, ln1, 0)
+        Gather(mixed.at[layer], 0, layer).begin(s)
+
+    def forward(layer, carry):
+        ia, iu, id_ = 3 * layer, 3 * layer + 1, 3 * layer + 2
+        more = layer < LAYERS - 1
+
+        def project(start):
+            rr = piece(start)
             qkv[layer, rr, :] = (
                 nn(mixed[layer, rr, :], w[ia, :, 0:512]) + bias_ref[layer, 0:1, 0:512]
             ).astype(BF16)
-
-        @pl.when(layer == 0)
-        def _():
-            relay(0)
-            gather_plane(mixed.at[layer], 0, layer, lambda block: None)
-            w2(0)
-
-            def one(block, inner):
-                project(block)
-                return inner
-
-            lax.fori_loop(0, 8, one, 0)
-
-        @pl.when(layer > 0)
-        def _():
-            w2(ia)
-            gather_plane(mixed.at[layer], 0, layer, project)
-
-        def take_q(b, inner):
-            rr = pool_rows(b)
             v = qkv[layer, rr, 256:512].astype(F32)
             qa[layer, rr, :] = pltpu.roll(v, 224, 1).astype(BF16)
-            return inner
-
-        lax.fori_loop(0, 8, take_q, 0)
+
+        w2(ia)
+        Gather(mixed.at[layer], 0, layer).run(lambda s, start: project(start), layer > 0)
+        relay(iu)
+        when(more, lambda: w0(layer + 1, 0))
         ot[...] = jnp.zeros_like(ot)
-
-        def head(j, inner):
-            h = j // 2
-            qh = j - 2 * h
+        sum1 = Reduce(
+            0, layer, lambda start: nt(att[layer, piece(start), :], w[ia, :, 384:640])
+        )
+
+        def half(qh, carry1):
             q_rows = rows_at(512 * qh, 512)
             q_cols = pl.ds(pl.multiple_of(512 * qh, 512), 512)
-            qm = jnp.where(head_mask(72 * h), qa[layer, q_rows, :].astype(F32), 0.0)
-            pb[0:512, 0:256] = qm.astype(BF16)
-
-            def scores(kb, m8):
-                rr = rows_at(256 * kb, 256)
-                s = nt(qkv[layer, rr, 0:256], pb[0:512, 0:256]) * scale
-                pool[rr, 0:512] = s
-                return jnp.maximum(m8, jnp.max(s.reshape(32, 8, 512), axis=0))
-
-            m8 = lax.fori_loop(0, 4, scores, jnp.full((8, 512), -jnp.inf, F32))
-            mx = jnp.max(m8, axis=0, keepdims=True)
-
-            def exps(kb, l8):
-                rr = rows_at(128 * kb, 128)
-                e = jnp.exp(pool[rr, 0:512] - mx)
-                pool[rr, 0:512] = e
-                return l8 + fold(e)
-
-            l8 = lax.fori_loop(0, 8, exps, jnp.zeros((8, 512), F32))
-            row_sum = jnp.sum(l8, axis=0, keepdims=True)
-            lse[layer, j, 0:1, :] = mx + jnp.log(row_sum)
-            inverse = 1.0 / row_sum
-
-            def probs(kb, inner2):
-                rr = rows_at(128 * kb, 128)
-                pb[rows_at(512 + 128 * kb, 128), :] = (pool[rr, 0:512] * inverse).astype(BF16)
-                return inner2
-
-            lax.fori_loop(0, 8, probs, 0)
-            otw[...] = tn(qkv[layer, :, 128:384], pb[512:1536, :])
-            ot[pl.ds(pl.multiple_of(48 + 72 * h, 8), 72), q_cols] = otw[
-                pl.ds(pl.multiple_of(16 + 72 * h, 8), 72), :
-            ]
-            return inner
-
-        lax.fori_loop(0, 4, head, 0)
-
-        def put_att(b, inner):
-            att[layer, pool_rows(b), :] = ot[:, cols128(b)].T.astype(BF16)
-            return inner
-
-        lax.fori_loop(0, 8, put_att, 0)
-        relay(iu)
-
-        def branch(b):
-            return nt(att[layer, pool_rows(b), :], w[ia, :, 384:640])
-
-        total1 = reduce_plane(0, layer, branch, lambda: relay(id_))
-
-        def ln2(r, inner):
-            rr = rows_at(16 * r, 16)
-            br = total1(rr, r) + bias_ref[layer, 1:2, :]
-            own[layer, 2, rr, :] = br
-            v = hb[rr, :] + mrow(layer, 2) * br
-            af[rr, :] = v
-            n, iv = layer_norm(v)
-            own[layer, 1, rr, :] = n
-            inv[layer, 1, rr, :] = spread(iv)
-            ffall[layer, own_rows(r), :] = (n * (1.0 + mrow(layer, 4)) + mrow(layer, 3)).astype(
-                BF16
-            )
-            return inner
-
-        lax.fori_loop(0, 8, ln2, 0)
+
+            def head(h, inner):
+                when((qh == 1) & (h == 1), lambda: sum1.hand_on(0))
+                qm = jnp.where(head_mask(72 * h), qa[layer, q_rows, :].astype(F32), 0.0)
+                pb[0:512, 0:256] = qm.astype(BF16)
+
+                def scores(kb, m8):
+                    rr = rows_at(256 * kb, 256)
+                    v = nt(qkv[layer, rr, 0:256], pb[0:512, 0:256]) * scale
+                    pre[layer, rr, 0:512] = v
+                    return jnp.maximum(m8, jnp.max(v.reshape(32, 8, 512), axis=0))
+
+                m8 = lax.fori_loop(0, 4, scores, jnp.full((8, 512), -jnp.inf, F32))
+                mx = jnp.max(m8, axis=0, keepdims=True)
+
+                def exps(kb, l8):
+                    rr = rows_at(128 * kb, 128)
+                    e = jnp.exp(pre[layer, rr, 0:512] - mx)
+                    pre[layer, rr, 0:512] = e
+                    return l8 + fold(e)
+
+                l8 = lax.fori_loop(0, 8, exps, jnp.zeros((8, 512), F32))
+                row_sum = jnp.sum(l8, axis=0, keepdims=True)
+                lse[layer, 2 * qh + h, 0:1, :] = mx + jnp.log(row_sum)
+                inverse = 1.0 / row_sum
+
+                def probs(kb, inner2):
+                    rr = rows_at(128 * kb, 128)
+                    pb[rows_at(512 + 128 * kb, 128), :] = (pre[layer, rr, 0:512] * inverse).astype(BF16)
+                    return inner2
+
+                lax.fori_loop(0, 8, probs, 0)
+                otw[...] = tn(qkv[layer, :, 128:384], pb[512:1536, :])
+                ot[pl.ds(pl.multiple_of(48 + 72 * h, 8), 72), q_cols] = otw[
+                    pl.ds(pl.multiple_of(16 + 72 * h, 8), 72), :
+                ]
+                return inner
+
+            lax.fori_loop(0, 2, head, 0)
+
+            def put_att(b, inner):
+                here = 4 * qh + b
+                att[layer, pool_rows(here), :] = ot[:, cols128(here)].T.astype(BF16)
+                return inner
+
+            lax.fori_loop(0, 4, put_att, 0)
+
+            def reduce_step(q, inner):
+                sum1.step(qh, q)
+                return inner
+
+            lax.fori_loop(0, 4, reduce_step, 0)
+            return carry1
+
+        lax.fori_loop(0, 2, half, 0)
+        sum1.hand_on(1)
+        gather2 = Gather(ffall.at[layer], 1, layer)
+
+        def norm_mid(s, carry1):
+            sum1.finish(s)
+
+            def ln2(r, inner):
+                rr = rows_at(64 * s + 16 * r, 16)
+                br = sum1.total(s, 16 * r) + bias_ref[layer, 1:2, :]
+                own[layer, 2, rr, :] = br
+                v = hb[rr, :] + mrow(layer, 2) * br
+                af[rr, :] = v
+                n, iv = layer_norm(v)
+                own[layer, 1, rr, :] = n
+                inv[layer, 1, rr, :] = spread(iv)
+                ffall[layer, own_rows(s, 16 * r), :] = (
+                    n * (1.0 + mrow(layer, 4)) + mrow(layer, 3)
+                ).astype(BF16)
+                return inner
+
+            lax.fori_loop(0, 4, ln2, 0)
+            gather2.begin(s)
+            return carry1
+
+        lax.fori_loop(0, 2, norm_mid, 0)
+        relay(id_)
+        when(more, lambda: w0(layer + 1, 1))
         w2(iu)
 
-        def up(b):
-            rr = pool_rows(b)
+        def up(s, start):
+            rr = piece(start)
             pre[layer, rr, :] = nn(ffall[layer, rr, :], w[iu]) + bias_ref[layer, 2:3, 0:640]
 
             def gelu(r, inner):
-                r2 = rows_at(128 * b + 16 * r, 16)
+                r2 = rows_at(start + 16 * r, 16)
                 act[r2, :] = jax.nn.gelu(pre[layer, r2, :], approximate=True).astype(BF16)
                 return inner
 
             lax.fori_loop(0, 8, gelu, 0)
 
-        gather_plane(ffall.at[layer], 1, layer, up)
+        gather2.run(up)
         w2(id_)
-
-        def down(b):
-            return nt(act[pool_rows(b), :], w[id_])
-
-        def beside():
-            @pl.when(layer < LAYERS - 1)
-            def _():
-                relay(id_ + 1)
-
-        total2 = reduce_plane(1, layer, down, beside)
-
-        def finish(r, inner):
-            rr = rows_at(16 * r, 16)
-            fo = total2(rr, r) + bias_ref[layer, 3:4, :]
-            own[layer, 3, rr, :] = fo
-            hb[rr, :] = af[rr, :] + mrow(layer, 5) * fo
-            return inner
-
-        lax.fori_loop(0, 8, finish, 0)
+        sum2 = Reduce(1, layer, lambda start: nt(act[piece(start), :], w[id_]))
+        sum2.run()
+
+        def hand():
+            relay(id_ + 1)
+            w0(layer + 1, 2)
+
+        when(more, hand)
+
+        def finish(s, carry1):
+            sum2.finish(s)
+
+            def one(r, inner):
+                rr = rows_at(64 * s + 16 * r, 16)
+                fo = sum2.total(s, 16 * r) + bias_ref[layer, 3:4, :]
+                own[layer, 3, rr, :] = fo
+                hb[rr, :] = af[rr, :] + mrow(layer, 5) * fo
+                return inner
+
+            lax.fori_loop(0, 4, one, 0)
+            when(more, lambda: norm_in(layer + 1, s))
+            return carry1
+
+        lax.fori_loop(0, 2, finish, 0)
         return carry
 
     hb[...] = x_ref[...].astype(F32)
+    for s in range(2):
+        norm_in(0, s)
+    first_gather = Gather(mixed.at[0], 0, 0)
+    last_gather = Gather(gff, 2, LAYERS - 1)
+    for s in range(2):
+        for r in range(4):
+            g_in = cot_ref[64 * s + 16 * r : 64 * s + 16 * r + 16, :].astype(F32)
+            gff[own_rows(s, 16 * r), :] = (mrow(LAYERS - 1, 5) * g_in).astype(BF16)
+        last_gather.begin(s)
+    first_gather.alone()
+    relay(0)
+    w0(0, 2)
+    last_gather.alone()
+    first_gather.drain()
+    last_gather.drain()
     lax.fori_loop(0, LAYERS, forward, 0)
+
+    for dev in (dev_p, dev_y, dev_x):
+        pl.semaphore_signal(r_c, inc=1, device_id=dev, device_id_type=MESH)
     out_ref[...] = hb[...].astype(BF16)
     for layer in range(LAYERS):
         for m in range(3):
             w_drain(layer, m)
     hb[...] = cot_ref[...].astype(F32)
 
+    def clear(d):
+        rz[:, d] = jnp.zeros((6, 288, 640), BF16)
+
+    when(z == 0, lambda: clear(0))
+    when(z == 3, lambda: clear(2))
+
     def g_copy(i, d, zz):
         return rc(w.at[i, w_rows(zz)], rz.at[i, d], gz_s.at[i, d], gz_r.at[i, d], (zz, c, t))
 
-    def g0(i):
-        for d, zz in enumerate(zo):
-            g_copy(i, d, zz).start()
+    def g_relay(i):
+        return rc(w.at[i, w_rows(3 - z)], rzr, gz_s.at[i, 3], gz_r.at[i, 3], (1 + z // 2, c, t))
+
+    def g_end_copies(i):
+        return (
+            (z == 0, lambda: g_copy(i, 0, 1)),
+            (z == 3, lambda: g_copy(i, 2, 2)),
+            (jnp.logical_not(is_mid), lambda: g_copy(i, 1, z_far)),
+        )
+
+    def g0(i, credit):
+        def from_mid():
+            g_copy(i, 0, z + 1).start()
+            g_copy(i, 2, z - 1).start()
+
+        def from_end():
+            when(jnp.logical_and(credit, True), lambda: pl.semaphore_wait(g_c, 1))
+            g_relay(i).start()
+
+        when(is_mid, from_mid)
+        when(jnp.logical_not(is_mid), from_end)
+        for condition, copy in g_end_copies(i):
+            when(condition, lambda copy=copy: copy().start())
+
+    def g1(i):
+        def at_mid():
+            g_relay(i).wait_recv()
+
+            def add(row):
+                rr = rows_at(288 * z_far + row, 16)
+                w[i, rr, :] = (
+                    w[i, rr, :].astype(F32) + rzr[rows_at(row, 16), :].astype(F32)
+                ).astype(BF16)
+
+            add_rows(288, add)
+            g_copy(i, 1, z_far).start()
+            pl.semaphore_signal(g_c, inc=1, device_id=(z_end, c, t), device_id_type=MESH)
+
+        when(is_mid, at_mid)
 
     def g_send(i):
         return rc(w.at[i, w_rows(z)], gw_ref.at[i, c], gf_s.at[i], gf_r.at[i], dev_x)
@@ -1018,18 +1111,21 @@
         return pltpu.make_async_copy(w.at[i, w_rows(z)], gw_ref.at[i, c], g_l.at[i])
 
     def g2(i):
-        for d, zz in enumerate(zo):
-            rc(rz.at[i, d], rz.at[i, d], gz_s.at[i, d], gz_r.at[i, d], dev_x).wait_recv()
-
-        def add(r, inner):
-            rr = rows_at(288 * z + 16 * r, 16)
+        def got(d):
+            return rc(rz.at[i, d], rz.at[i, d], gz_s.at[i, d], gz_r.at[i, d], dev_x)
+
+        when(z != 0, lambda: got(0).wait_recv())
+        when(z != 3, lambda: got(2).wait_recv())
+        got(1).wait_recv()
+
+        def add(row):
+            rr = rows_at(288 * z + row, 16)
             total = w[i, rr, :].astype(F32)
-            for d in range(zs_n - 1):
-                total = total + rz[i, d, rows_at(16 * r, 16), :].astype(F32)
+            for d in range(3):
+                total = total + rz[i, d, rows_at(row, 16), :].astype(F32)
             w[i, rr, :] = total.astype(BF16)
-            return inner
-
-        lax.fori_loop(0, 18, add, 0)
+
+        add_rows(288, add)
         g_send(i).start()
         g_keep(i).start()
 
@@ -1038,8 +1134,15 @@
         rc(other, other, gf_s.at[i], gf_r.at[i], dev_x).wait_recv()
         g_send(i).wait_send()
         g_keep(i).wait()
-        for d, zz in enumerate(zo):
-            g_copy(i, d, zz).wait_send()
+
+        def from_mid():
+            for d, zz in ((0, z + 1), (1, z_far), (2, z - 1)):
+                g_copy(i, d, zz).wait_send()
+
+        when(is_mid, from_mid)
+        when(jnp.logical_not(is_mid), lambda: g_relay(i).wait_send())
+        for condition, copy in g_end_copies(i):
+            when(condition, lambda copy=copy: copy().wait_send())
 
     def small():
         for index, size, dev in ((0, 8, dev_p), (1, 8, dev_y), (2, 16, dev_x)):
@@ -1066,110 +1169,115 @@
 
     zero8 = jnp.zeros((8, D), F32)
 
-    def put_sum(layer, row, v8):
-        sm[layer, row : row + 1, 0 : v8.shape[1]] = jnp.sum(v8, axis=0, keepdims=True)
-
     def add_sum(layer, row, v8):
         here = (layer, pl.ds(row, 1), slice(0, v8.shape[1]))
         sm[here] = sm[here] + jnp.sum(v8, axis=0, keepdims=True)
 
+    def grad_in_ff(layer, s, live):
+        def start(r, sums):
+            rr = rows_at(64 * s + 16 * r, 16)
+            g = hb[rr, :]
+            gf = (mrow(layer, 5) * g).astype(BF16)
+            gff[own_rows(s, 16 * r), :] = gf
+            return (sums[0] + fold(g * own[layer, 3, rr, :]), sums[1] + fold(gf.astype(F32)))
+
+        s_gate2, s_bdown = lax.fori_loop(0, 4, start, (zero8, zero8))
+        add_sum(layer, 5, s_gate2)
+        add_sum(layer, 7, s_bdown)
+        if live:
+            Gather(gff, 2, layer).begin(s)
+
     def backward(step_index, carry):
         layer = LAYERS - 1 - step_index
         ia, iu, id_ = 3 * layer, 3 * layer + 1, 3 * layer + 2
-
-        def start(r, sums):
-            rr = rows_at(16 * r, 16)
-            g = hb[rr, :]
-            gf = (mrow(layer, 5) * g).astype(BF16)
-            gff[own_rows(r), :] = gf
-            return (sums[0] + fold(g * own[layer, 3, rr, :]), sums[1] + fold(gf.astype(F32)))
-
-        s_gate2, s_bdown = lax.fori_loop(0, 8, start, (zero8, zero8))
-        put_sum(layer, 5, s_gate2)
-        put_sum(layer, 7, s_bdown)
-
-        def act_back(b):
-            rr = pool_rows(b)
-            pool[rows_at(512, 128), 0:640] = nn(gff[rr, :], w[id_])
+        more = layer > 0
+
+        def act_back(s, start):
+            rr = piece(start)
+            temp = rows_at(512 * s, 128)
+            pool[temp, 0:640] = nn(gff[rr, :], w[id_])
 
             def one(r, total):
-                r2 = rows_at(128 * b + 16 * r, 16)
+                r2 = rows_at(start + 16 * r, 16)
                 v = pre[layer, r2, :]
                 th = jnp.tanh(0.7978845608028654 * (v + 0.044715 * (v * v * v)))
                 act[r2, :] = (0.5 * v * (1.0 + th)).astype(BF16)
                 slope = 0.5 * (1.0 + th) + 0.5 * v * (1.0 - th * th) * (
                     0.7978845608028654 * (1.0 + 0.134145 * (v * v))
                 )
-                gp = (pool[rows_at(512 + 16 * r, 16), 0:640] * slope).astype(BF16)
+                gp = (pool[rows_at(512 * s + 16 * r, 16), 0:640] * slope).astype(BF16)
                 gpre[r2, :] = gp
                 return total + fold(gp.astype(F32))
 
             add_sum(layer, 10 + c, lax.fori_loop(0, 8, one, jnp.zeros((8, 640), F32)))
 
-        gather_plane(gff, 2, layer, act_back)
-
-        def ffin_back(b):
-            return nt(gpre[pool_rows(b), :], w[iu])
-
-        def beside1():
-            def one_d(i, inner):
-                w[id_, rows_at(128 * i, 128), :] = tn(gff[:, cols128(i)], act[...]).astype(BF16)
-                return inner
-
-            lax.fori_loop(0, 9, one_d, 0)
-            g0(id_)
-
-            def one_u(i, inner):
-                w[iu, rows_at(128 * i, 128), :] = tn(ffall[layer, :, cols128(i)], gpre[...]).astype(
-                    BF16
+        Gather(gff, 2, layer).run(act_back, layer < LAYERS - 1)
+        when(layer == LAYERS - 1, lambda: pl.semaphore_wait(r_c, 3))
+        sum1 = Reduce(2, layer, lambda start: nt(gpre[piece(start), :], w[iu]))
+        sum1.run()
+
+        def one_d(i, inner):
+            w[id_, rows_at(128 * i, 128), :] = tn(gff[:, cols128(i)], act[...]).astype(BF16)
+            return inner
+
+        lax.fori_loop(0, 9, one_d, 0)
+        when(layer == 0, lambda: g1(3))
+        g0(id_, layer < LAYERS - 1)
+        gather2 = Gather(gb, 3, layer)
+
+        def middle(s, carry1):
+            sum1.finish(s)
+
+            def mid(r, sums):
+                rr = rows_at(64 * s + 16 * r, 16)
+                gf = sum1.total(s, 16 * r)
+                n = own[layer, 1, rr, :]
+                e = gf * (1.0 + mrow(layer, 4))
+                iv = inv[layer, 1, rr, 0:1]
+                ga = hb[rr, :] + iv * (
+                    e
+                    - jnp.mean(e, axis=-1, keepdims=True)
+                    - n * jnp.mean(e * n, axis=-1, keepdims=True)
                 )
-                return inner
-
-            lax.fori_loop(0, 9, one_u, 0)
-            g0(iu)
-
-        total1 = reduce_plane(2, layer, ffin_back, beside1)
-
-        def mid(r, sums):
-            rr = rows_at(16 * r, 16)
-            gf = total1(rr, r)
-            n = own[layer, 1, rr, :]
-            e = gf * (1.0 + mrow(layer, 4))
-            iv = inv[layer, 1, rr, 0:1]
-            ga = hb[rr, :] + iv * (
-                e
-                - jnp.mean(e, axis=-1, keepdims=True)
-                - n * jnp.mean(e * n, axis=-1, keepdims=True)
+                hb[rr, :] = ga
+                gbv = (mrow(layer, 2) * ga).astype(BF16)
+                gb[own_rows(s, 16 * r), :] = gbv
+                return (
+                    sums[0] + fold(gf),
+                    sums[1] + fold(gf * n),
+                    sums[2] + fold(ga * own[layer, 2, rr, :]),
+                    sums[3] + fold(gbv.astype(F32)),
+                )
+
+            all_sums = lax.fori_loop(0, 4, mid, (zero8, zero8, zero8, zero8))
+            for row, value in zip((3, 4, 2, 6), all_sums):
+                add_sum(layer, row, value)
+            gather2.begin(s)
+            return carry1
+
+        lax.fori_loop(0, 2, middle, 0)
+
+        def one_u(i, inner):
+            w[iu, rows_at(128 * i, 128), :] = tn(ffall[layer, :, cols128(i)], gpre[...]).astype(
+                BF16
             )
-            hb[rr, :] = ga
-            gbv = (mrow(layer, 2) * ga).astype(BF16)
-            gb[own_rows(r), :] = gbv
-            return (
-                sums[0] + fold(gf),
-                sums[1] + fold(gf * n),
-                sums[2] + fold(ga * own[layer, 2, rr, :]),
-                sums[3] + fold(gbv.astype(F32)),
-            )
-
-        s_shift2, s_scale2, s_gate1, s_bproj = lax.fori_loop(
-            0, 8, mid, (zero8, zero8, zero8, zero8)
-        )
-        put_sum(layer, 3, s_shift2)
-        put_sum(layer, 4, s_scale2)
-        put_sum(layer, 2, s_gate1)
-        put_sum(layer, 6, s_bproj)
-
-        def att_back(b):
-            rr = pool_rows(b)
+            return inner
+
+        lax.fori_loop(0, 9, one_u, 0)
+        g1(id_)
+        g0(iu, True)
+
+        def att_back(s, start):
+            rr = piece(start)
             doa[rr, :] = pltpu.roll(nn(gb[rr, :], w[ia, :, 384:640]), 224, 1).astype(BF16)
 
-        gather_plane(gb, 3, layer, att_back)
+        gather2.run(att_back)
         dkv[...] = jnp.zeros_like(dkv)
         ot[...] = jnp.zeros_like(ot)
 
         def head(j, inner):
-            h = j // 2
-            qh = j - 2 * h
+            h = lax.rem(j, 2)
+            qh = j // 2
             q_rows = rows_at(512 * qh, 512)
             q_cols = pl.ds(pl.multiple_of(512 * qh, 512), 512)
             qm = jnp.where(head_mask(72 * h), qa[layer, q_rows, :].astype(F32), 0.0)
@@ -1180,11 +1288,11 @@
 
             def first(kb, d8):
                 rr = rows_at(256 * kb, 256)
-                s = nt(qkv[layer, rr, 0:256], pb[0:512, 0:256]) * scale
-                pr = jnp.exp(s - log_row)
+                v = nt(qkv[layer, rr, 0:256], pb[0:512, 0:256]) * scale
+                pr = jnp.exp(v - log_row)
                 dp = nt(qkv[layer, rr, 128:384], pb[0:512, 256:512])
-                pool[rr, 0:512] = pr
-                pool[rr, 512:1024] = dp
+                pre[layer, rr, 0:512] = pr
+                pool[rr, 0:512] = dp
                 dkv[rr, 128:384] = dkv[rr, 128:384] + nn(pr.astype(BF16), pb[0:512, 256:512])
                 return d8 + fold(pr * dp)
 
@@ -1193,7 +1301,7 @@
 
             def second(kb, inner2):
                 rr = rows_at(256 * kb, 256)
-                ds = (pool[rr, 0:512] * (pool[rr, 512:1024] - delta)).astype(BF16)
+                ds = (pre[layer, rr, 0:512] * (pool[rr, 0:512] - delta)).astype(BF16)
                 pb[rows_at(512 + 256 * kb, 256), :] = ds
                 dkv[rr, 0:256] = dkv[rr, 0:256] + nn(ds, pb[0:512, 0:256]) * scale
                 return inner2
@@ -1219,49 +1327,58 @@
 
         add_sum(layer, 8 + c, lax.fori_loop(0, 8, put, jnp.zeros((8, 512), F32)))
 
-        @pl.when(layer == 0)
-        def _():
+        def pending():
             g2(5)
             g2(4)
 
-        def mix_back(block):
-            return nt(dqkv[pool_rows(block), :], w[ia, :, 0:512])
-
-        def beside2():
-            def one(i, inner):
-                rr = rows_at(128 * i, 128)
-                r1 = tn(mixed[layer, :, cols128(i)], dqkv[...])
-                r3 = tn(gb[:, cols128(i)], att[layer])
-                w[ia, rr, 0:384] = r1[:, 0:384].astype(BF16)
-                w[ia, rr, 384:512] = (r1[:, 384:512] + r3[:, 0:128]).astype(BF16)
-                w[ia, rr, 512:640] = r3[:, 128:256].astype(BF16)
-                return inner
-
-            lax.fori_loop(0, 9, one, 0)
-            g0(ia)
-
-        total2 = reduce_plane(3, layer, mix_back, beside2)
-
-        def last(r, sums):
-            rr = rows_at(16 * r, 16)
-            gm = total2(rr, r)
-            n = own[layer, 0, rr, :]
-            e = gm * (1.0 + mrow(layer, 1))
-            iv = inv[layer, 0, rr, 0:1]
-            hb[rr, :] = hb[rr, :] + iv * (
-                e
-                - jnp.mean(e, axis=-1, keepdims=True)
-                - n * jnp.mean(e * n, axis=-1, keepdims=True)
-            )
-            return (sums[0] + fold(gm), sums[1] + fold(gm * n))
-
-        s_shift1, s_scale1 = lax.fori_loop(0, 8, last, (zero8, zero8))
-        put_sum(layer, 0, s_shift1)
-        put_sum(layer, 1, s_scale1)
+        when(layer == 0, pending)
+        sum2 = Reduce(3, layer, lambda start: nt(dqkv[piece(start), :], w[ia, :, 0:512]))
+        sum2.run()
+
+        def one_a(i, inner):
+            rr = rows_at(128 * i, 128)
+            r1 = tn(mixed[layer, :, cols128(i)], dqkv[...])
+            r3 = tn(gb[:, cols128(i)], att[layer])
+            w[ia, rr, 0:384] = r1[:, 0:384].astype(BF16)
+            w[ia, rr, 384:512] = (r1[:, 384:512] + r3[:, 0:128]).astype(BF16)
+            w[ia, rr, 512:640] = r3[:, 128:256].astype(BF16)
+            return inner
+
+        lax.fori_loop(0, 9, one_a, 0)
+        g1(iu)
+        g0(ia, True)
+
+        def final(s, carry1):
+            sum2.finish(s)
+
+            def last(r, sums):
+                rr = rows_at(64 * s + 16 * r, 16)
+                gm = sum2.total(s, 16 * r)
+                n = own[layer, 0, rr, :]
+                e = gm * (1.0 + mrow(layer, 1))
+                iv = inv[layer, 0, rr, 0:1]
+                hb[rr, :] = hb[rr, :] + iv * (
+                    e
+                    - jnp.mean(e, axis=-1, keepdims=True)
+                    - n * jnp.mean(e * n, axis=-1, keepdims=True)
+                )
+                return (sums[0] + fold(gm), sums[1] + fold(gm * n))
+
+            all_sums = lax.fori_loop(0, 4, last, (zero8, zero8))
+            for row, value in zip((0, 1), all_sums):
+                add_sum(layer, row, value)
+            when(more, lambda: grad_in_ff(layer - 1, s, True))
+            return carry1
+
+        lax.fori_loop(0, 2, final, 0)
         return carry
 
     sm[...] = jnp.zeros_like(sm)
+    for s in range(2):
+        grad_in_ff(LAYERS - 1, s, False)
     lax.fori_loop(0, LAYERS, backward, 0)
+    g1(0)
+    when(jnp.logical_not(is_mid), lambda: pl.semaphore_wait(g_c, 1))
     small()
     g2(3)
     g2(2)
@@ -1343,13 +1460,13 @@
         pltpu.VMEM((2, 8, D), F32),
         pltpu.VMEM((128, D), F32),
         pltpu.VMEM((1024, D), F32),
-        pltpu.VMEM((4, 128, D), F32),
-        pltpu.VMEM((128, D), BF16),
-        pltpu.VMEM((128, D), BF16),
-        pltpu.VMEM((128, D), BF16),
-        pltpu.VMEM((128, D), BF16),
-        pltpu.VMEM((128, D), BF16),
-        pltpu.VMEM((128, D), BF16),
+        pltpu.VMEM((2, 4, 64, D), F32),
+        pltpu.VMEM((2, 64, D), BF16),
+        pltpu.VMEM((2, 64, D), BF16),
+        pltpu.VMEM((2, 64, D), BF16),
+        pltpu.VMEM((2, 64, D), BF16),
+        pltpu.VMEM((2, 64, D), BF16),
+        pltpu.VMEM((2, 64, D), BF16),
         pltpu.VMEM((1024, D), BF16),
         pltpu.VMEM((1024, 640), BF16),
         pltpu.VMEM((1024, D), BF16),
@@ -1360,6 +1477,7 @@
         pltpu.VMEM((256, 512), F32),
         pltpu.VMEM((256, 1024), F32),
         pltpu.VMEM((6, zs_n - 1, 288, 640), BF16),
+        pltpu.VMEM((288, 640), BF16),
         pltpu.VMEM((2, 16, D), F32),
         pltpu.VMEM((3, 2, 16, D), F32),
         dma((zs_n - 1,)),
@@ -1367,15 +1485,17 @@
         dma((6, 4)),
         dma((6, zs_n)),
         dma((6,)),
-        dma((4, 2, 13)),
-        dma((4, 2, 13)),
-        dma((4, 2, 8)),
-        dma((4, 2, 8)),
+        dma((4, 2, 2, 9)),
+        dma((4, 2, 2, 9)),
+        dma((4, 2, 2, 10)),
+        dma((4, 2, 2, 10)),
         dma((6, zs_n)),
         dma((6, zs_n)),
         dma((6,)),
         dma((6,)),
         dma((6,)),
+        pltpu.SemaphoreType.REGULAR,
+        pltpu.SemaphoreType.REGULAR,
         dma((3 + zs_n,)),
         dma((3 + zs_n,)),
     ]

time: 515 us -> 463 us (0.90)
  Pallas kernels: 459 us -> 406 us
    pallas_call x1, Pallas kernels: 451 us -> 399 us  [run_stage(): pl.pallas_call(functools.partial(stage_kernel, zs_n), name='two_blocks',...]
where the time goes in v3:
time: 463 us; the launch traced here: 462 us
  Pallas kernels  406 us (88%)
  local copies, waits for them, and re-layouts  22.5 us (5%)
  matrix products  19.2 us (4%)
  other arithmetic  13.3 us (3%)
    pallas_call x1, Pallas kernels, run_stage(): pl.pallas_call(functools.partial(stage_kernel, zs_n), name='two_blocks',...  399 us

profile of v3, /device:TPU:0, one launch (start us, length us, event | category | flops | bytes accessed | tf_op | source)
XLA Modules:
  0.0 462.0 jit_solution(5287011849007894403)
XLA Ops:
  0.7 0.8 constant_dynamic-slice_fusion.3
  1.5 0.1 pad_maximum_fusion.3
  1.5 0.8 constant_dynamic-slice_fusion.2
  2.4 0.7 reshape.133
  3.1 0.7 reshape.135
  3.7 0.7 pad_maximum_fusion.bias_ref
  4.4 0.7 copy.75
  5.1 6.0 %fusion.19 = f32[4,2,6,288]{3,0,2,1:T(4,128)S(1)} fusion(bf16[2,1152,6,288]{1,3,2,0:T(8,128)(2,1)} %param.15, f32[4,1152]{1,0:T(4,128)} %param.14), kind=kOutput, calls=%fused_computation.66 | convolution fusion | flops 31873536 | bytes 8036352 | tf_op jit(solution)/shard_map/sd,ldkc->lskc/dot_general | solution.py:1543
  11.1 0.7 bitcast_convert_fusion.modin_ref
  11.8 0.0 copy-done.12
  11.8 0.2 copy.113
  12.0 0.0 copy-start.4
  12.0 0.4 constant_dynamic-slice_fusion
  12.3 0.9 pad.28.su_ref
  13.3 0.0 copy-done.8
  13.3 0.3 dynamic-slice_bitcast_fusion
  13.6 0.9 pad.29.sd_ref
  14.6 0.4 dynamic-slice_bitcast_fusion.3
  14.9 1.3 fusion.11.sa_ref
  16.3 399.2 %two_blocks.1 = (bf16[128,1152]{1,0:T(8,128)(2,1)}, f32[128,1152]{1,0:T(8,128)}, bf16[6,2,288,640]{3,2,1,0:T(8,128)(2,1)}, f32[4,2,16,1152]{3,2,1,0:T(8,128)}) custom-call(bf16[128,1152]{1,0:T(8,128)(2,1)} %bitcast.113, bf16[128,1152]{1,0:T(8,128)(2,1)} %bitcast.114, f32[4,16,384]{2,1,0:T(8,128)} %bitcast_convert_fusion.modin_ref, ...), custom_call_target="tpu_custom_call" | custom-call | tf_op jit(solution)/shard_map/two_blocks/pallas_call | solution.py:1502
  415.5 2.5 copy.99
  417.9 1.1 slice_reduce_fusion
  419.1 1.0 slice.111
  420.0 0.1 convert_reduce_fusion
  420.2 0.6 copy.100
  420.8 0.1 fusion.26
  420.9 0.1 maximum_bitcast_fusion.1
  421.0 0.1 maximum_bitcast_fusion
  421.0 0.6 copy.101
  421.7 0.7 pad_maximum_fusion.1
  422.4 0.6 copy_bitcast_fusion
  423.0 5.0 %fusion.2.part_ref = f32[4,1152]{1,0:T(4,128)} fusion(bf16[2,1152,6,288]{1,3,2,0:T(8,128)(2,1)} %param.15, bf16[4,2,6,288]{3,2,1,0:T(8,128)(2,1)S(1)} %get-tuple-element.61), kind=kOutput, calls=%fused_computation.4 | convolution fusion | flops 31850496 | bytes 8008704 | tf_op jit(solution)/shard_map/slkc,ldkc->sd/dot_general | solution.py:1589
  428.0 6.9 %sum_shards.1 = f32[4,1152]{1,0:T(4,128)} custom-call(f32[4,1152]{1,0:T(4,128)} %fusion.2.part_ref), custom_call_target="tpu_custom_call" | custom-call | tf_op jit(solution)/shard_map/sum_shards/pallas_call | solution.py:1427
  435.0 0.0 copy-done.10
  435.0 1.4 fusion.16
  436.3 3.9 fusion.23
  440.2 2.0 slice_bitcast_fusion.1
  442.3 1.8 copy.123
  444.1 1.8 copy.124
  445.9 2.0 convert_bitcast_fusion.1
  447.9 3.2 convert_bitcast_fusion
  451.1 0.0 copy-done.1
  451.1 0.0 copy-done.2
  451.1 0.0 copy-done.3
  451.1 2.0 maximum_convert_fusion
  453.1 0.0 copy-done.11
  453.1 8.2 %convolution_bitcast_fusion = f32[2,1152,6,288]{1,3,2,0:T(8,128)} fusion(bf16[4,2,6,288]{3,2,1,0:T(8,128)(2,1)S(1)} %copy-done.6, f32[4,1152]{1,0:T(4,128)S(1)} %copy-done.11), kind=kOutput, calls=%fused_computation | convolution fusion | flops 31873536 | bytes 15971328 | tf_op jit(solution)/shard_map/sd,slkc->ldkc/dot_general | solution.py:1587
  461.3 0.7 copy.151
  (34 shorter events, 0.2 us)
Async XLA Ops:
  5.1 6.7 %copy-start.12 = (bf16[2,288,288]{2,1,0:T(8,128)(2,1)S(1)}, bf16[2,288,288]{2,1,0:T(8,128)(2,1)}, u32[]{:S(2)}) copy-start(bf16[2,288,288]{2,1,0:T(8,128)(2,1)} %param.19) | copy-start | bytes 995332
  5.1 6.9 %copy-start.7 = (bf16[2,288,1152]{2,1,0:T(8,128)(2,1)S(1)}, bf16[2,288,1152]{2,1,0:T(8,128)(2,1)}, u32[]{:S(2)}) copy-start(bf16[2,288,1152]{2,1,0:T(8,128)(2,1)} %param.21) | copy-start | bytes 3981316
  11.1 2.2 copy-start.8
  12.0 2.6 copy-start.4
  420.1 2.8 copy-start.5
  423.0 12.0 %copy-start.10 = (f32[4,1152]{1,0:T(4,128)S(1)}, f32[4,1152]{1,0:T(4,128)}, u32[]{:S(2)}) copy-start(f32[4,1152]{1,0:T(4,128)} %param.14) | copy-start | bytes 55300
  447.9 3.2 copy-start
  447.9 3.2 copy-start.1
  447.9 3.2 copy-start.2
  447.9 3.2 copy-start.3
  451.1 2.0 copy-start.6
  451.1 2.0 copy-start.11
  453.1 8.2 %copy-start.9 = (bf16[128,1152]{1,0:T(8,128)(2,1)S(1)}, bf16[128,1152]{1,0:T(8,128)(2,1)}, u32[]{:S(2)}) copy-start(bf16[128,1152]{1,0:T(8,128)(2,1)} %get-tuple-element.17) | copy-start | bytes 884740

commit v4 on v3

--- a/solution.py
+++ b/solution.py
@@ -444,7 +444,11 @@
     x_ref,
     cot_ref,
     modin_ref,
-    bias_ref,
+    bada_ref,
+    bqv_ref,
+    bproj_ref,
+    bup_ref,
+    bdown_ref,
     sa_ref,
     su_ref,
     sd_ref,
@@ -463,6 +467,8 @@
     own,
     inv,
     lse,
+    bias_ref,
+    mods,
     modr,
     modv,
     af,
@@ -532,10 +538,30 @@
     pl.semaphore_wait(barrier, 2 + zs_n)
 
     def mod_copy(d, to, frm):
-        return rc(modin_ref.at[to], modr.at[frm], m_s.at[d], m_r.at[frm], (to, c, t))
-
+        return rc(mods.at[to], modr.at[frm], m_s.at[d], m_r.at[frm], (to, c, t))
+
+    mods[...] = jnp.zeros_like(mods)
+    for layer in range(LAYERS):
+        for kind in range(6):
+            row = 8 * layer + kind
+            both = modin_ref[layer, kind] + bada_ref[layer, kind : kind + 1, :].astype(F32)
+            both = both.astype(BF16).astype(F32)
+            for zz in range(zs_n):
+                mods[zz, row : row + 1, 0:288] = both[zz : zz + 1, :]
     for d, zz in enumerate(zo):
         mod_copy(d, zz, z).start()
+
+    def own_half(value, size):
+        return jnp.where(c == 0, value[:, 0:size], value[:, size : 2 * size])
+
+    bias_ref[...] = jnp.zeros_like(bias_ref)
+    for layer in range(LAYERS):
+        b_heads = bqv_ref[layer].astype(F32)
+        bias_ref[layer, 0:1, 144:288] = own_half(b_heads[1:2], 144)
+        bias_ref[layer, 0:1, 288:432] = own_half(b_heads[0:1], 144)
+        bias_ref[layer, 1:2, :] = bproj_ref[layer : layer + 1, :].astype(F32)
+        bias_ref[layer, 2:3, 0:576] = own_half(bup_ref[layer : layer + 1, :].astype(F32), 576)
+        bias_ref[layer, 3:4, :] = bdown_ref[layer : layer + 1, :].astype(F32)
 
     shards = (sa_ref, su_ref, sd_ref)
     z_far = z + 2 - 4 * (z // 2)
@@ -606,7 +632,7 @@
     w0(0, 1)
 
 
-    modr[z] = modin_ref[z]
+    modr[z] = mods[z]
     for zz in zo:
         mod_copy(0, zz, zz).wait_recv()
     for d in range(zs_n - 1):
@@ -766,7 +792,7 @@
             mine = pool[rows_at(512 * s + 128 * q + 64 * k + row, 16), :]
             return mine + ra[s, q, rows_at(row, 16), :]
 
-        def step(self, s, q):
+        def step(self, s, q, both):
             chip = 2 * lax.rem(c + 1 - q // 2, 2) + lax.rem(y + 1 - lax.rem(q, 2), 2)
             pool[rows_at(512 * s + 128 * q, 128), :] = self.compute(512 * s + 128 * chip)
             self.to_p(s, q).start()
@@ -800,7 +826,13 @@
 
             when(q == 1, diagonal)
             when(q == 2, across_x)
-            when(q == 3, across_y)
+
+            def last():
+                across_y()
+                if both:
+                    self.hand_on(s)
+
+            when(q == 3, last)
 
         def hand_on(self, s):
             self.leg(s, 5).wait_recv()
@@ -824,13 +856,10 @@
 
         def run(self):
             def one(n, carry):
-                s, q = n // 4, lax.rem(n, 4)
-                self.step(s, q)
-                when(n == 5, lambda: self.hand_on(0))
+                self.step(lax.rem(n, 2), n // 2, True)
                 return carry
 
             lax.fori_loop(0, 8, one, 0)
-            self.hand_on(1)
 
         def finish(self, s):
             self.to_p(s, 3).wait_recv()
@@ -954,7 +983,7 @@
             lax.fori_loop(0, 4, put_att, 0)
 
             def reduce_step(q, inner):
-                sum1.step(qh, q)
+                sum1.step(qh, q, False)
                 return inner
 
             lax.fori_loop(0, 4, reduce_step, 0)
@@ -1061,88 +1090,110 @@
     when(z == 0, lambda: clear(0))
     when(z == 3, lambda: clear(2))
 
-    def g_copy(i, d, zz):
-        return rc(w.at[i, w_rows(zz)], rz.at[i, d], gz_s.at[i, d], gz_r.at[i, d], (zz, c, t))
-
-    def g_relay(i):
-        return rc(w.at[i, w_rows(3 - z)], rzr, gz_s.at[i, 3], gz_r.at[i, 3], (1 + z // 2, c, t))
-
-    def g_end_copies(i):
-        return (
-            (z == 0, lambda: g_copy(i, 0, 1)),
-            (z == 3, lambda: g_copy(i, 2, 2)),
-            (jnp.logical_not(is_mid), lambda: g_copy(i, 1, z_far)),
-        )
-
-    def g0(i, credit):
-        def from_mid():
-            g_copy(i, 0, z + 1).start()
-            g_copy(i, 2, z - 1).start()
-
-        def from_end():
-            when(jnp.logical_and(credit, True), lambda: pl.semaphore_wait(g_c, 1))
-            g_relay(i).start()
-
-        when(is_mid, from_mid)
-        when(jnp.logical_not(is_mid), from_end)
-        for condition, copy in g_end_copies(i):
-            when(condition, lambda copy=copy: copy().start())
+    def g_rows(zz, h):
+        return rows_at(288 * zz + 144 * h, 144)
+
+    def g_copy(i, d, zz, h):
+        got = rz.at[i, d, pl.ds(144 * h, 144)]
+        return rc(
+            w.at[i, g_rows(zz, h)], got, gz_s.at[i, d, h], gz_r.at[i, d, h], (zz, c, t)
+        )
+
+    def g_relay(i, h):
+        got = rzr.at[pl.ds(144 * h, 144)]
+        return rc(
+            w.at[i, g_rows(3 - z, h)], got, gz_s.at[i, 3, h], gz_r.at[i, 3, h], (1 + z // 2, c, t)
+        )
+
+    is_end = jnp.logical_not(is_mid)
+
+    def g_each(i, h, act_on):
+        when(z == 0, lambda: act_on(g_copy(i, 0, 1, h)))
+        when(z == 3, lambda: act_on(g_copy(i, 2, 2, h)))
+        when(is_end, lambda: act_on(g_copy(i, 1, z_far, h)))
+
+    def g_start(copy):
+        copy.start()
+
+    def g0(i):
+        for h in range(2):
+            g_each(i, h, g_start)
+
+            def from_mid(h=h):
+                g_copy(i, 0, z + 1, h).start()
+                g_copy(i, 2, z - 1, h).start()
+
+            when(is_mid, from_mid)
+
+    def g0_relay(i, credit):
+        when(is_end & jnp.logical_and(credit, True), lambda: pl.semaphore_wait(g_c, 1))
+        for h in range(2):
+            when(is_end, lambda h=h: g_relay(i, h).start())
 
     def g1(i):
         def at_mid():
-            g_relay(i).wait_recv()
-
-            def add(row):
-                rr = rows_at(288 * z_far + row, 16)
-                w[i, rr, :] = (
-                    w[i, rr, :].astype(F32) + rzr[rows_at(row, 16), :].astype(F32)
-                ).astype(BF16)
-
-            add_rows(288, add)
-            g_copy(i, 1, z_far).start()
+            for h in range(2):
+                g_relay(i, h).wait_recv()
+
+                def add(row, h=h):
+                    rr = rows_at(288 * z_far + 144 * h + row, 16)
+                    w[i, rr, :] = (
+                        w[i, rr, :].astype(F32) + rzr[rows_at(144 * h + row, 16), :].astype(F32)
+                    ).astype(BF16)
+
+                add_rows(144, add)
+                g_copy(i, 1, z_far, h).start()
             pl.semaphore_signal(g_c, inc=1, device_id=(z_end, c, t), device_id_type=MESH)
 
         when(is_mid, at_mid)
 
-    def g_send(i):
-        return rc(w.at[i, w_rows(z)], gw_ref.at[i, c], gf_s.at[i], gf_r.at[i], dev_x)
-
-    def g_keep(i):
-        return pltpu.make_async_copy(w.at[i, w_rows(z)], gw_ref.at[i, c], g_l.at[i])
+    def g_send(i, h):
+        there = gw_ref.at[i, c, pl.ds(144 * h, 144)]
+        return rc(w.at[i, g_rows(z, h)], there, gf_s.at[i, h], gf_r.at[i, h], dev_x)
+
+    def g_keep(i, h):
+        there = gw_ref.at[i, c, pl.ds(144 * h, 144)]
+        return pltpu.make_async_copy(w.at[i, g_rows(z, h)], there, g_l.at[i, h])
 
     def g2(i):
-        def got(d):
-            return rc(rz.at[i, d], rz.at[i, d], gz_s.at[i, d], gz_r.at[i, d], dev_x)
-
-        when(z != 0, lambda: got(0).wait_recv())
-        when(z != 3, lambda: got(2).wait_recv())
-        got(1).wait_recv()
-
-        def add(row):
-            rr = rows_at(288 * z + row, 16)
-            total = w[i, rr, :].astype(F32)
-            for d in range(3):
-                total = total + rz[i, d, rows_at(row, 16), :].astype(F32)
-            w[i, rr, :] = total.astype(BF16)
-
-        add_rows(288, add)
-        g_send(i).start()
-        g_keep(i).start()
+        for h in range(2):
+
+            def got(d, h=h):
+                part = rz.at[i, d, pl.ds(144 * h, 144)]
+                return rc(part, part, gz_s.at[i, d, h], gz_r.at[i, d, h], dev_x)
+
+            when(z != 0, lambda: got(0).wait_recv())
+            when(z != 3, lambda: got(2).wait_recv())
+            got(1).wait_recv()
+
+            def add(row, h=h):
+                rr = rows_at(288 * z + 144 * h + row, 16)
+                total = w[i, rr, :].astype(F32)
+                for d in range(3):
+                    total = total + rz[i, d, rows_at(144 * h + row, 16), :].astype(F32)
+                w[i, rr, :] = total.astype(BF16)
+
+            add_rows(144, add)
+            g_send(i, h).start()
+            g_keep(i, h).start()
 
     def g3(i):
-        other = gw_ref.at[i, 1 - c]
-        rc(other, other, gf_s.at[i], gf_r.at[i], dev_x).wait_recv()
-        g_send(i).wait_send()
-        g_keep(i).wait()
-
-        def from_mid():
-            for d, zz in ((0, z + 1), (1, z_far), (2, z - 1)):
-                g_copy(i, d, zz).wait_send()
-
-        when(is_mid, from_mid)
-        when(jnp.logical_not(is_mid), lambda: g_relay(i).wait_send())
-        for condition, copy in g_end_copies(i):
-            when(condition, lambda copy=copy: copy().wait_send())
+        def done(copy):
+            copy.wait_send()
+
+        for h in range(2):
+            other = gw_ref.at[i, 1 - c, pl.ds(144 * h, 144)]
+            rc(other, other, gf_s.at[i, h], gf_r.at[i, h], dev_x).wait_recv()
+            g_send(i, h).wait_send()
+            g_keep(i, h).wait()
+
+            def from_mid(h=h):
+                for d, zz in ((0, z + 1), (1, z_far), (2, z - 1)):
+                    g_copy(i, d, zz, h).wait_send()
+
+            when(is_mid, from_mid)
+            when(is_end, lambda h=h: g_relay(i, h).wait_send())
+            g_each(i, h, done)
 
     def small():
         for index, size, dev in ((0, 8, dev_p), (1, 8, dev_y), (2, 16, dev_x)):
@@ -1212,6 +1263,7 @@
             add_sum(layer, 10 + c, lax.fori_loop(0, 8, one, jnp.zeros((8, 640), F32)))
 
         Gather(gff, 2, layer).run(act_back, layer < LAYERS - 1)
+        when(layer == 0, lambda: g1(3))
         when(layer == LAYERS - 1, lambda: pl.semaphore_wait(r_c, 3))
         sum1 = Reduce(2, layer, lambda start: nt(gpre[piece(start), :], w[iu]))
         sum1.run()
@@ -1221,8 +1273,8 @@
             return inner
 
         lax.fori_loop(0, 9, one_d, 0)
-        when(layer == 0, lambda: g1(3))
-        g0(id_, layer < LAYERS - 1)
+        g0_relay(id_, layer < LAYERS - 1)
+        g0(id_)
         gather2 = Gather(gb, 3, layer)
 
         def middle(s, carry1):
@@ -1265,13 +1317,20 @@
 
         lax.fori_loop(0, 9, one_u, 0)
         g1(id_)
-        g0(iu, True)
+        g0(iu)
 
         def att_back(s, start):
             rr = piece(start)
             doa[rr, :] = pltpu.roll(nn(gb[rr, :], w[ia, :, 384:640]), 224, 1).astype(BF16)
 
         gather2.run(att_back)
+        g0_relay(iu, True)
+
+        def pending():
+            g2(5)
+            g2(4)
+
+        when(layer == 0, pending)
         dkv[...] = jnp.zeros_like(dkv)
         ot[...] = jnp.zeros_like(ot)
 
@@ -1327,11 +1386,7 @@
 
         add_sum(layer, 8 + c, lax.fori_loop(0, 8, put, jnp.zeros((8, 512), F32)))
 
-        def pending():
-            g2(5)
-            g2(4)
-
-        when(layer == 0, pending)
+        g1(iu)
         sum2 = Reduce(3, layer, lambda start: nt(dqkv[piece(start), :], w[ia, :, 0:512]))
         sum2.run()
 
@@ -1345,8 +1400,9 @@
             return inner
 
         lax.fori_loop(0, 9, one_a, 0)
-        g1(iu)
-        g0(ia, True)
+        g0_relay(ia, True)
+        g0(ia)
+        when(layer == 0, lambda: g2(3))
 
         def final(s, carry1):
             sum2.finish(s)
@@ -1380,7 +1436,6 @@
     g1(0)
     when(jnp.logical_not(is_mid), lambda: pl.semaphore_wait(g_c, 1))
     small()
-    g2(3)
     g2(2)
     g2(1)
     small_end()
@@ -1439,7 +1494,7 @@
     )(part)
 
 
-def run_stage(zs_n, x_in, cot, modin, bias, block_a, block_u, block_d):
+def run_stage(zs_n, *args):
     vm = pl.BlockSpec(memory_space=pltpu.VMEM)
     anyspace = pl.BlockSpec(memory_space=pl.ANY)
     dma = pltpu.SemaphoreType.DMA
@@ -1456,6 +1511,8 @@
         pltpu.VMEM((2, 4, 128, D), F32),
         pltpu.VMEM((2, 2, 128, 128), F32),
         pltpu.VMEM((2, 4, 8, 512), F32),
+        pltpu.VMEM((2, 4, D), F32),
+        pltpu.VMEM((zs_n, 16, 384), F32),
         pltpu.VMEM((zs_n, 16, 384), F32),
         pltpu.VMEM((2, 8, D), F32),
         pltpu.VMEM((128, D), F32),
@@ -1489,11 +1546,11 @@
         dma((4, 2, 2, 9)),
         dma((4, 2, 2, 10)),
         dma((4, 2, 2, 10)),
-        dma((6, zs_n)),
-        dma((6, zs_n)),
-        dma((6,)),
-        dma((6,)),
-        dma((6,)),
+        dma((6, zs_n, 2)),
+        dma((6, zs_n, 2)),
+        dma((6, 2)),
+        dma((6, 2)),
+        dma((6, 2)),
         pltpu.SemaphoreType.REGULAR,
         pltpu.SemaphoreType.REGULAR,
         dma((3 + zs_n,)),
@@ -1508,13 +1565,13 @@
             sds((6, 2, 288, 640), BF16),
             sds((zs_n, 2, 16, D), F32),
         ),
-        in_specs=[vm, vm, vm, vm, anyspace, anyspace, anyspace],
+        in_specs=[vm] * 8 + [anyspace] * 3,
         out_specs=(vm, vm, anyspace, vm),
         scratch_shapes=scratch,
         compiler_params=pltpu.CompilerParams(
             collective_id=0, has_side_effects=True, vmem_limit_bytes=67043328
         ),
-    )(x_in, cot, modin, bias, block_a, block_u, block_d)
+    )(*args)
 
 
 def fast_body(
@@ -1539,16 +1596,12 @@
     part = w_qkv.shape[3] // 2
     units = up_weight.shape[2] // 2
     cond_low = jax.nn.silu(cond).astype(BF16)
-    mod_terms = (
-        jnp.einsum("sd,ldkc->lskc", cond_low, w_ada, preferred_element_type=F32)
-        + b_ada.astype(F32)[:, None]
-    ).astype(BF16)
-    modin = jnp.pad(
-        mod_terms.astype(F32).transpose(1, 0, 2, 3), ((0, 0), (0, 0), (0, 2), (0, 384 - cols))
-    ).reshape(zs_n, 16, 384)
+    modin = jnp.einsum("sd,ldkc->lksc", cond_low, w_ada, preferred_element_type=F32)
 
     def mine(array, size, axis):
-        return lax.dynamic_slice_in_dim(array, c * size, size, axis)
+        low = lax.slice_in_dim(array, 0, size, axis=axis)
+        high = lax.slice_in_dim(array, size, 2 * size, axis=axis)
+        return jnp.where(c == 0, low, high)
 
     def wide(array, size):
         return jnp.pad(array, ((0, 0),) * (array.ndim - 1) + ((0, size - array.shape[-1]),))
@@ -1568,19 +1621,19 @@
     )
     block_u = wide(mine(up_weight, units, 2), 640)
     block_d = wide(mine(down_weight, units, 1).transpose(0, 2, 1), 640)
-    b_heads = mine(b_qv, part, 2).astype(F32)
-    b_qkv = jnp.concatenate((jnp.zeros((LAYERS, part), F32), b_heads[:, 1], b_heads[:, 0]), axis=1)
-    bias = jnp.stack(
-        (
-            wide(b_qkv, D),
-            b_proj.astype(F32),
-            wide(mine(up_bias_vector, units, 1).astype(F32), D),
-            down_bias_vector.astype(F32),
-        ),
-        axis=1,
-    )
     out, grad_in, gw, small = run_stage(
-        zs_n, x_in[:, 0], cotangent[:, 0], modin, bias, block_a, block_u, block_d
+        zs_n,
+        x_in[:, 0],
+        cotangent[:, 0],
+        modin,
+        b_ada,
+        b_qv,
+        b_proj,
+        up_bias_vector,
+        down_bias_vector,
+        block_a,
+        block_u,
+        block_d,
     )
     grad_mod = small[:, :, 0:6, :].astype(BF16)
     mod_cols = lax.dynamic_slice_in_dim(grad_mod, z * cols, cols, 3)

time: 463 us -> 450 us (0.972)
  Pallas kernels: 406 us -> 396 us
    pallas_call x1, Pallas kernels: 399 us -> 387 us  [run_stage(): pl.pallas_call(functools.partial(stage_kernel, zs_n), name='two_blocks',...]
    unnamed x34 -> x36, local copies, waits for them, and re-layouts: 8.89 us -> 11.2 us
where the time goes in v4:
time: 450 us
  Pallas kernels  396 us (88%)
  local copies, waits for them, and re-layouts  20.7 us (5%)
  matrix products  19.7 us (4%)
  other arithmetic  12.6 us (3%)
    pallas_call x1, Pallas kernels, run_stage(): pl.pallas_call(functools.partial(stage_kernel, zs_n), name='two_blocks',...  387 us
    unnamed x36, local copies, waits for them, and re-layouts  11.2 us
    pallas_call x1, Pallas kernels, sum_shards(): pl.pallas_call(functools.partial(sum_kernel, zs_n), name='sum_shards', ou...  9.21 us

profile of v4, /device:TPU:0, one launch (start us, length us, event | category | flops | bytes accessed | tf_op | source)
XLA Modules:
  0.0 449.8 jit_solution(14346906854225628804)
XLA Ops:
  0.7 1.3 copy.52.bada_ref
  2.0 6.5 %convolution_bitcast_fusion.1.modin_ref = f32[2,6,4,288]{3,2,1,0:T(4,128)} fusion(bf16[2,1152,6,288]{1,3,2,0:T(8,128)(2,1)} %param.15, f32[4,1152]{1,0:T(4,128)} %param.14), kind=kOutput, calls=%fused_computation.12 | convolution fusion | flops 31873536 | bytes 8036352 | tf_op jit(solution)/shard_map/sd,ldkc->lksc/dot_general | solution.py:1599
  8.5 0.0 copy-done.7
  8.5 0.2 copy.84
  8.7 0.0 copy-start.2
  8.7 0.2 copy.83
  9.0 0.9 copy-done.1
  9.8 0.3 slice_select_fusion
  10.1 0.0 copy-start
  10.1 0.9 pad.11.su_ref
  11.1 0.0 copy-done.2
  11.1 0.3 select_bitcast_fusion
  11.3 0.9 pad.12.sd_ref
  12.3 0.0 copy-done
  12.3 0.4 fusion.22
  12.7 0.1 copy_select_fusion
  12.8 0.1 slice_bitcast_fusion.12
  12.9 1.4 fusion.11.sa_ref
  14.2 386.7 %two_blocks.1 = (bf16[128,1152]{1,0:T(8,128)(2,1)}, f32[128,1152]{1,0:T(8,128)}, bf16[6,2,288,640]{3,2,1,0:T(8,128)(2,1)}, f32[4,2,16,1152]{3,2,1,0:T(8,128)}) custom-call(bf16[128,1152]{1,0:T(8,128)(2,1)} %bitcast.101, bf16[128,1152]{1,0:T(8,128)(2,1)} %bitcast.102, f32[2,6,4,288]{3,2,1,0:T(4,128)} %convolution_bitcast_fusion.1.modin_ref, ...), custom_call_target="tpu_custom_call" | custom-call | tf_op jit(solution)/shard_map/two_blocks/pallas_call | solution.py:1559
  400.9 2.5 copy.72
  403.4 1.1 slice_reduce_fusion
  404.5 1.0 slice.136
  405.5 0.1 convert_reduce_fusion
  405.6 0.0 copy-start.8
  405.6 0.6 copy.73
  406.2 0.1 fusion.26
  406.4 0.1 maximum_bitcast_fusion.1
  406.4 0.1 maximum_bitcast_fusion
  406.5 0.6 copy.74
  407.2 0.7 pad_maximum_fusion
  407.8 0.6 copy_bitcast_fusion
  408.4 0.0 copy-done.8
  408.5 5.0 %fusion.2.part_ref = f32[4,1152]{1,0:T(4,128)} fusion(bf16[2,1152,6,288]{1,3,2,0:T(8,128)(2,1)} %param.15, bf16[4,2,6,288]{3,2,1,0:T(8,128)(2,1)S(1)} %get-tuple-element.48), kind=kOutput, calls=%fused_computation.4 | convolution fusion | flops 31850496 | bytes 8008704 | tf_op jit(solution)/shard_map/slkc,ldkc->sd/dot_general | solution.py:1642
  413.5 9.2 %sum_shards.1 = f32[4,1152]{1,0:T(4,128)} custom-call(f32[4,1152]{1,0:T(4,128)} %fusion.2.part_ref), custom_call_target="tpu_custom_call" | custom-call | tf_op jit(solution)/shard_map/sum_shards/pallas_call | solution.py:1482
  422.7 0.0 copy-done.11
  422.7 1.4 fusion.15
  424.1 3.9 fusion.21
  428.0 2.0 slice_bitcast_fusion.1
  430.1 1.8 copy.94
  431.9 1.8 copy.95
  433.7 2.0 convert_bitcast_fusion.1
  435.7 3.2 convert_bitcast_fusion
  438.9 0.0 copy-done.3
  438.9 0.0 copy-done.5
  438.9 0.0 copy-done.6
  438.9 2.0 maximum_convert_fusion
  440.9 8.2 %convolution_bitcast_fusion = f32[2,1152,6,288]{1,3,2,0:T(8,128)} fusion(bf16[4,2,6,288]{3,2,1,0:T(8,128)(2,1)S(1)} %copy-done.9, f32[4,1152]{1,0:T(4,128)S(1)} %copy-done.12), kind=kOutput, calls=%fused_computation | convolution fusion | flops 31873536 | bytes 15971328 | tf_op jit(solution)/shard_map/sd,slkc->ldkc/dot_general | solution.py:1640
  449.1 0.7 copy.120
  (22 shorter events, 0.2 us)
Async XLA Ops:
  2.0 6.5 %copy-start.7 = (bf16[2,288,288]{2,1,0:T(8,128)(2,1)S(1)}, bf16[2,288,288]{2,1,0:T(8,128)(2,1)}, u32[]{:S(2)}) copy-start(bf16[2,288,288]{2,1,0:T(8,128)(2,1)} %param.19) | copy-start | bytes 995332
  8.5 1.3 copy-start.1
  8.7 2.3 copy-start.2
  10.1 2.2 copy-start
  405.6 2.8 copy-start.8
  408.5 14.3 %copy-start.11 = (f32[4,1152]{1,0:T(4,128)S(1)}, f32[4,1152]{1,0:T(4,128)}, u32[]{:S(2)}) copy-start(f32[4,1152]{1,0:T(4,128)} %param.14) | copy-start | bytes 55300
  435.7 3.2 copy-start.3
  435.7 3.2 copy-start.4
  435.7 3.2 copy-start.5
  435.7 3.2 copy-start.6
  438.9 2.0 copy-start.9
  438.9 2.0 copy-start.12
  440.9 8.2 %copy-start.10 = (bf16[128,1152]{1,0:T(8,128)(2,1)S(1)}, bf16[128,1152]{1,0:T(8,128)(2,1)}, u32[]{:S(2)}) copy-start(bf16[128,1152]{1,0:T(8,128)(2,1)} %get-tuple-element.17) | copy-start | bytes 884740

commit v5 on v4

--- a/solution.py
+++ b/solution.py
@@ -629,7 +629,6 @@
             w_take(3 * layer + m, z_far).wait_send()
 
     w0(0, 0)
-    w0(0, 1)
 
 
     modr[z] = mods[z]
@@ -926,7 +925,7 @@
         w2(ia)
         Gather(mixed.at[layer], 0, layer).run(lambda s, start: project(start), layer > 0)
         relay(iu)
-        when(more, lambda: w0(layer + 1, 0))
+        when(jnp.logical_not(more), lambda: w0(LAYERS - 1, 2))
         ot[...] = jnp.zeros_like(ot)
         sum1 = Reduce(
             0, layer, lambda start: nt(att[layer, piece(start), :], w[ia, :, 384:640])
@@ -1016,7 +1015,7 @@
 
         lax.fori_loop(0, 2, norm_mid, 0)
         relay(id_)
-        when(more, lambda: w0(layer + 1, 1))
+        when(more, lambda: w0(layer + 1, 0))
         w2(iu)
 
         def up(s, start):
@@ -1037,7 +1036,7 @@
 
         def hand():
             relay(id_ + 1)
-            w0(layer + 1, 2)
+            w0(layer + 1, 1)
 
         when(more, hand)
 
@@ -1070,6 +1069,7 @@
         last_gather.begin(s)
     first_gather.alone()
     relay(0)
+    w0(0, 1)
     w0(0, 2)
     last_gather.alone()
     first_gather.drain()

time: 450 us -> 445 us (0.989)
  Pallas kernels: 396 us -> 391 us
    pallas_call x1, Pallas kernels: 387 us -> 381 us  [run_stage(): pl.pallas_call(functools.partial(stage_kernel, zs_n), name='two_blocks',...]
where the time goes in v5:
time: 445 us
  Pallas kernels  391 us (88%)
  local copies, waits for them, and re-layouts  20.7 us (5%)
  matrix products  19.7 us (4%)
  other arithmetic  12.6 us (3%)
    pallas_call x1, Pallas kernels, run_stage(): pl.pallas_call(functools.partial(stage_kernel, zs_n), name='two_blocks',...  381 us
    unnamed x36, local copies, waits for them, and re-layouts  11.2 us
    pallas_call x1, Pallas kernels, sum_shards(): pl.pallas_call(functools.partial(sum_kernel, zs_n), name='sum_shards', ou...  9.45 us

profile of v5, /device:TPU:0, one launch (start us, length us, event | category | flops | bytes accessed | tf_op | source)
XLA Modules:
  0.0 444.8 jit_solution(7365030532362875958)
XLA Ops:
  0.7 1.3 copy.52.bada_ref
  2.0 6.5 %convolution_bitcast_fusion.1.modin_ref = f32[2,6,4,288]{3,2,1,0:T(4,128)} fusion(bf16[2,1152,6,288]{1,3,2,0:T(8,128)(2,1)} %param.15, f32[4,1152]{1,0:T(4,128)} %param.14), kind=kOutput, calls=%fused_computation.12 | convolution fusion | flops 31873536 | bytes 8036352 | tf_op jit(solution)/shard_map/sd,ldkc->lksc/dot_general | solution.py:1599
  8.5 0.0 copy-done.7
  8.5 0.2 copy.84
  8.7 0.0 copy-start.2
  8.7 0.2 copy.83
  9.0 0.9 copy-done.1
  9.8 0.3 slice_select_fusion
  10.1 0.0 copy-start
  10.1 0.9 pad.11.su_ref
  11.1 0.0 copy-done.2
  11.1 0.3 select_bitcast_fusion
  11.3 0.9 pad.12.sd_ref
  12.3 0.0 copy-done
  12.3 0.4 fusion.22
  12.7 0.1 copy_select_fusion
  12.8 0.1 slice_bitcast_fusion.12
  12.9 1.4 fusion.11.sa_ref
  14.2 381.4 %two_blocks.1 = (bf16[128,1152]{1,0:T(8,128)(2,1)}, f32[128,1152]{1,0:T(8,128)}, bf16[6,2,288,640]{3,2,1,0:T(8,128)(2,1)}, f32[4,2,16,1152]{3,2,1,0:T(8,128)}) custom-call(bf16[128,1152]{1,0:T(8,128)(2,1)} %bitcast.101, bf16[128,1152]{1,0:T(8,128)(2,1)} %bitcast.102, f32[2,6,4,288]{3,2,1,0:T(4,128)} %convolution_bitcast_fusion.1.modin_ref, ...), custom_call_target="tpu_custom_call" | custom-call | tf_op jit(solution)/shard_map/two_blocks/pallas_call | solution.py:1559
  395.7 2.5 copy.72
  398.2 1.1 slice_reduce_fusion
  399.3 1.0 slice.136
  400.3 0.1 convert_reduce_fusion
  400.4 0.0 copy-start.8
  400.4 0.6 copy.73
  401.0 0.1 fusion.26
  401.1 0.1 maximum_bitcast_fusion.1
  401.2 0.1 maximum_bitcast_fusion
  401.3 0.6 copy.74
  401.9 0.7 pad_maximum_fusion
  402.6 0.6 copy_bitcast_fusion
  403.2 0.0 copy-done.8
  403.2 5.0 %fusion.2.part_ref = f32[4,1152]{1,0:T(4,128)} fusion(bf16[2,1152,6,288]{1,3,2,0:T(8,128)(2,1)} %param.15, bf16[4,2,6,288]{3,2,1,0:T(8,128)(2,1)S(1)} %get-tuple-element.48), kind=kOutput, calls=%fused_computation.4 | convolution fusion | flops 31850496 | bytes 8008704 | tf_op jit(solution)/shard_map/slkc,ldkc->sd/dot_general | solution.py:1642
  408.3 9.5 %sum_shards.1 = f32[4,1152]{1,0:T(4,128)} custom-call(f32[4,1152]{1,0:T(4,128)} %fusion.2.part_ref), custom_call_target="tpu_custom_call" | custom-call | tf_op jit(solution)/shard_map/sum_shards/pallas_call | solution.py:1482
  417.7 0.0 copy-done.11
  417.7 1.4 fusion.15
  419.1 3.9 fusion.21
  423.0 2.0 slice_bitcast_fusion.1
  425.1 1.8 copy.94
  426.9 1.8 copy.95
  428.7 2.0 convert_bitcast_fusion.1
  430.7 3.2 convert_bitcast_fusion
  433.9 0.0 copy-done.3
  433.9 0.0 copy-done.5
  433.9 0.0 copy-done.6
  433.9 2.0 maximum_convert_fusion
  435.9 8.2 %convolution_bitcast_fusion = f32[2,1152,6,288]{1,3,2,0:T(8,128)} fusion(bf16[4,2,6,288]{3,2,1,0:T(8,128)(2,1)S(1)} %copy-done.9, f32[4,1152]{1,0:T(4,128)S(1)} %copy-done.12), kind=kOutput, calls=%fused_computation | convolution fusion | flops 31873536 | bytes 15971328 | tf_op jit(solution)/shard_map/sd,slkc->ldkc/dot_general | solution.py:1640
  444.1 0.7 copy.120
  (22 shorter events, 0.2 us)
Async XLA Ops:
  2.0 6.5 %copy-start.7 = (bf16[2,288,288]{2,1,0:T(8,128)(2,1)S(1)}, bf16[2,288,288]{2,1,0:T(8,128)(2,1)}, u32[]{:S(2)}) copy-start(bf16[2,288,288]{2,1,0:T(8,128)(2,1)} %param.19) | copy-start | bytes 995332
  8.5 1.3 copy-start.1
  8.7 2.3 copy-start.2
  10.1 2.2 copy-start
  400.4 2.8 copy-start.8
  403.2 14.5 %copy-start.11 = (f32[4,1152]{1,0:T(4,128)S(1)}, f32[4,1152]{1,0:T(4,128)}, u32[]{:S(2)}) copy-start(f32[4,1152]{1,0:T(4,128)} %param.14) | copy-start | bytes 55300
  430.7 3.2 copy-start.3
  430.7 3.2 copy-start.4
  430.7 3.2 copy-start.5
  430.7 3.2 copy-start.6
  433.9 2.0 copy-start.9
  433.9 2.0 copy-start.12
  435.9 8.2 %copy-start.10 = (bf16[128,1152]{1,0:T(8,128)(2,1)S(1)}, bf16[128,1152]{1,0:T(8,128)(2,1)}, u32[]{:S(2)}) copy-start(bf16[128,1152]{1,0:T(8,128)(2,1)} %get-tuple-element.17) | copy-start | bytes 884740
